TPU v7x, 256 devices: a whole 4x4x8 slice. The times are simulated.
256 devices in a mesh: gx: 8 (over z), gy: 4 (over y), gz: 8 (over x, core).
Axes of the slice: x: 4, y: 4, z: 8, core: 2. Of those that a mesh axis runs over, the one named last changes fastest.
Arguments:
- point_data: float32 [1, 6, 131072], P(None, None, ('gx', 'gy', 'gz')), may hold values from -1 to 1
- neighbours: int32 [1, 64, 64, 64, 32], P(None, 'gx', 'gy', 'gz'), may hold values from 0 to 131071, as said below
- counts: int32 [1, 64, 64, 64], P(None, 'gx', 'gy', 'gz'), may hold values from 1 to 32, as said below
- kernel_in: bfloat16 [6, 80], replicated, may hold values from -2.5 to 2.5
- kernel_mid: bfloat16 [80, 80], replicated, may hold values from -0.625 to 0.625
- kernel_out: bfloat16 [80, 64], replicated, may hold values from -0.625 to 0.625
- spectral: bfloat16 [2, 16, 16, 16, 64, 64], P(None, 'gz', 'gx', 'gy'), may hold values from -48 to 48
- skip_weight: bfloat16 [64, 64], replicated, may hold values from -0.75 to 0.75
Outputs:
- latent_out: float32 [1, 64, 64, 64, 64], P(None, 'gx', 'gy', 'gz')
Inputs may be any that keep to these rules, and one draw needn't show every extreme that they name: `neighbours`: points are owned by location: point j of a geometry belongs to the device at position j // 512 in the order gx, gy, gz. Every neighbour of a node is owned by the node's own device or by a device whose gx, gy and gz indices each differ from it by at most one. Slots s >= counts of the node are padding that names some point all the same. `counts`: on every device some node of every geometry has all 32 slots valid.
All inputs are finite; a program needn't handle non-finite values.
Results may differ from a plain program's by a relative error of at most 0.02.
Values may be sent and summed in bfloat16 or wider, within the bound.
A program may use at most 64 MiB of HBM per device.

v0:
```python
import math

import jax
import jax.numpy as jnp
from jax import lax
from jax.sharding import Mesh
from jax.sharding import PartitionSpec as P

GRID = 64
MODES = 16
NB = 32
GZ = ("gz_0", "gz_1")
GX_GY_GZ = ("gx", "gy", "gz_0", "gz_1")


HIGHEST = lax.Precision.HIGHEST
NORM_FLOOR = 1.0


def extended(cells, sides, width):
    for axis, dim in sides:
        count = lax.axis_size(axis)
        ends = count - 1
        head = lax.slice_in_dim(cells, 0, width, axis=dim)
        tail = lax.slice_in_dim(cells, cells.shape[dim] - width, cells.shape[dim], axis=dim)
        cells = jnp.concatenate(
            [
                lax.ppermute(tail, axis, [(i, (i + 1) % count) for i in range(ends)]),
                cells,
                lax.ppermute(head, axis, [((i + 1) % count, i) for i in range(ends)]),
            ],
            axis=dim,
        )
    return cells


def in_one_piece(arrays, axis, split_dim, concat_dim, along):
    both = jnp.concatenate(arrays, axis=along)
    result, at, done = (
        lax.all_to_all(both, axis, split_axis=split_dim, concat_axis=concat_dim, tiled=True),
        0,
        [],
    )
    for a in arrays:
        done.append(lax.slice_in_dim(result, at, at + a.shape[along], axis=along))
        at += a.shape[along]
    return tuple(done)


def all_in_one(x, axis):
    leaves = jax.tree.leaves(x)
    turns = sorted(range(len(leaves)), key=lambda k: -leaves[k].size)
    width = (1, *leaves[turns[0]].shape)[-1]
    lines = [
        jnp.pad(leaves[k].reshape(-1), (0, -leaves[k].size % width)).reshape(-1, width)
        for k in turns
    ]
    both, at, found = (lax.all_gather(jnp.concatenate(lines), axis), 0, {})
    for k, line in zip(turns, lines):
        share = both[:, at : at + len(line)].reshape(len(both), -1)
        found[k] = share[:, : leaves[k].size].reshape(-1, *leaves[k].shape)
        at += len(line)
    numbers = iter(range(len(leaves)))
    return jax.tree.map(lambda _: found[next(numbers)], x)


def merged_by_axis(x, axes, combine):
    for axis in axes:
        pieces = all_in_one(x, axis)
        x = jax.tree.map(lambda part: part[0], pieces)
        for k in range(1, lax.axis_size(axis)):
            x = combine(x, jax.tree.map(lambda part: part[k], pieces))
    return x


def tables(length, keep_count, centred):
    position = jnp.arange(length, dtype=jnp.int32)
    frequency = jnp.arange(keep_count, dtype=jnp.int32)
    if centred:
        frequency = jnp.where(
            frequency < keep_count // 2, frequency, frequency + length - keep_count
        )
    phases = frequency[:, None] * position[None, :] % length
    angles = phases.astype(jnp.float32) * (2.0 * math.pi / length)
    return (jnp.cos(angles), jnp.sin(angles))


def third_weights(cos_table, sin_table, length):
    factor = (
        jnp.where(jnp.arange(cos_table.shape[0]) == 0, 1.0, 2.0).astype(jnp.float32)[:, None]
        / length**3
    )
    return (cos_table * factor, sin_table * factor)


def contract(pattern, operand, table):
    return jnp.einsum(pattern, operand, table, precision=HIGHEST)


def forward_real(values, cos_table, sin_table, pattern):
    return (contract(pattern, values, cos_table), -contract(pattern, values, sin_table))


def forward_complex(real_part, imag_part, cos_table, sin_table, pattern):
    new_real = contract(pattern, real_part, cos_table) + contract(pattern, imag_part, sin_table)
    new_imag = contract(pattern, imag_part, cos_table) - contract(pattern, real_part, sin_table)
    return (new_real, new_imag)


def inverse_complex(real_part, imag_part, cos_table, sin_table, pattern):
    new_real = contract(pattern, real_part, cos_table) - contract(pattern, imag_part, sin_table)
    new_imag = contract(pattern, real_part, sin_table) + contract(pattern, imag_part, cos_table)
    return (new_real, new_imag)


def inverse_real(real_part, imag_part, cos_table, sin_table, pattern):
    return contract(pattern, real_part, cos_table) - contract(pattern, imag_part, sin_table)


def kernel_mean(pair, valid, kernel_in, kernel_mid, kernel_out):
    hidden_one = jax.nn.gelu(
        jnp.dot(kernel_in.T, pair, preferred_element_type=jnp.float32), approximate=True
    ).astype(jnp.bfloat16)
    hidden_two = jax.nn.gelu(
        jnp.dot(kernel_mid.T, hidden_one, preferred_element_type=jnp.float32), approximate=True
    ).astype(jnp.bfloat16)
    values = jnp.dot(kernel_out.T, hidden_two, preferred_element_type=jnp.float32)
    values = values.reshape(values.shape[0], -1, NB)
    slots = jnp.arange(NB, dtype=jnp.int32)
    used = (slots[None, :] < valid[:, None]).astype(jnp.float32)
    total = jnp.sum(values * used[None], axis=2)
    return (total / valid.astype(jnp.float32)[None]).T.astype(jnp.bfloat16)


def split_exact(values):
    upper = values.astype(jnp.bfloat16)
    rest = values - upper.astype(jnp.float32)
    middle = rest.astype(jnp.bfloat16)
    lower = (rest - middle.astype(jnp.float32)).astype(jnp.bfloat16)
    return jnp.stack([upper, middle, lower], axis=1)


def merge_moments(first, second):
    count_a, mean_a, square_a = first
    count_b, mean_b, square_b = second
    total = count_a + count_b
    delta = mean_b - mean_a
    return (
        total,
        mean_a + delta * (count_b / total),
        square_a + square_b + delta * delta * (count_a * count_b / total),
    )


def body(point_data, neighbours, counts, kernel_in, kernel_mid, kernel_out, spectral, skip_weight):
    count_y = lax.axis_size("gy")
    count_z = lax.axis_size(GZ)
    place_x = lax.axis_index("gx")
    place_y = lax.axis_index("gy")
    place_z = lax.axis_index(GZ)
    geometry_count, cells_x, cells_y, cells_z = neighbours.shape[0:4]
    per_device = point_data.shape[2]
    channels = skip_weight.shape[0]
    beside_all = extended(point_data[None, None, None], (("gx", 0), ("gy", 1), (GZ, 2)), 1)
    table = jnp.transpose(beside_all, (3, 4, 0, 1, 2, 5)).reshape(
        geometry_count, point_data.shape[1], 27, per_device
    )
    pieces = split_exact(table).reshape(geometry_count, 3 * point_data.shape[1] * 27, per_device)
    owner = neighbours // per_device
    offset_z = owner % count_z - place_z + 1
    offset_y = owner // count_z % count_y - place_y + 1
    offset_x = owner // (count_z * count_y) - place_x + 1
    block_index = (offset_x * 3 + offset_y) * 3 + offset_z
    slot_index = neighbours % per_device
    centre_y = (
        (place_y * cells_y + jnp.arange(cells_y, dtype=jnp.int32)).astype(jnp.float32) + 0.5
    ) / GRID
    centre_z = (
        (place_z * cells_z + jnp.arange(cells_z, dtype=jnp.int32)).astype(jnp.float32) + 0.5
    ) / GRID
    row_y = jnp.broadcast_to(centre_y[:, None, None], (cells_y, cells_z, NB)).reshape(1, -1)
    row_z = jnp.broadcast_to(centre_z[None, :, None], (cells_y, cells_z, NB)).reshape(1, -1)
    slot_ids = jnp.arange(per_device, dtype=jnp.int32)[:, None]
    block_ids = jnp.arange(27, dtype=jnp.int32)[:, None]

    def one_slab(step):
        geometry = step // cells_x
        slab = step % cells_x
        rows = lax.dynamic_index_in_dim(pieces, geometry, 0, keepdims=False)
        blocks = lax.dynamic_index_in_dim(
            lax.dynamic_index_in_dim(block_index, geometry, 0, keepdims=False),
            slab,
            0,
            keepdims=False,
        ).reshape(1, -1)
        slots = lax.dynamic_index_in_dim(
            lax.dynamic_index_in_dim(slot_index, geometry, 0, keepdims=False),
            slab,
            0,
            keepdims=False,
        ).reshape(1, -1)
        valid = lax.dynamic_index_in_dim(
            lax.dynamic_index_in_dim(counts, geometry, 0, keepdims=False), slab, 0, keepdims=False
        ).reshape(-1)
        slot_hot = (slots == slot_ids).astype(jnp.bfloat16)
        found = jnp.dot(rows, slot_hot, preferred_element_type=jnp.float32).reshape(3, 6, 27, -1)
        found = found[0] + found[1] + found[2]
        block_hot = (blocks == block_ids).astype(jnp.float32)
        picked = jnp.sum(found * block_hot[None], axis=1)
        row_x = ((place_x * cells_x + slab).astype(jnp.float32) + 0.5) / GRID
        pair = jnp.concatenate(
            [picked[0:1] - row_x, picked[1:2] - row_y, picked[2:3] - row_z, picked[3:6]], axis=0
        ).astype(jnp.bfloat16)
        return kernel_mean(pair, valid, kernel_in, kernel_mid, kernel_out)

    latent = lax.map(one_slab, jnp.arange(geometry_count * cells_x, dtype=jnp.int32))
    latent = latent.reshape(geometry_count, cells_x, cells_y, cells_z, channels)
    cos_centred, sin_centred = tables(GRID, MODES, True)
    cos_third, sin_third = tables(GRID, MODES, False)
    back_cos, back_sin = third_weights(cos_third, sin_third, GRID)
    depth_full = lax.all_to_all(latent, GZ, split_axis=4, concat_axis=3, tiled=True)
    real_part, imag_part = forward_real(
        depth_full.astype(jnp.float32), cos_third, sin_third, "gxyzc,kz->gxykc"
    )
    real_part, imag_part = in_one_piece((real_part, imag_part), "gy", 3, 2, 0)
    real_part, imag_part = forward_complex(
        real_part, imag_part, cos_centred, sin_centred, "gxykc,jy->gxjkc"
    )
    real_part, imag_part = in_one_piece((real_part, imag_part), "gx", 2, 1, 0)
    real_part, imag_part = forward_complex(
        real_part, imag_part, cos_centred, sin_centred, "gxjkc,ix->gijkc"
    )
    spec_real, spec_imag = in_one_piece((real_part, imag_part), GZ, 1, 4, 0)
    spec_real = spec_real.astype(jnp.bfloat16)
    spec_imag = spec_imag.astype(jnp.bfloat16)
    mixed_real = jnp.einsum(
        "gijkc,ijkco->gijko", spec_real, spectral[0], preferred_element_type=jnp.float32
    ) - jnp.einsum("gijkc,ijkco->gijko", spec_imag, spectral[1], preferred_element_type=jnp.float32)
    mixed_imag = jnp.einsum(
        "gijkc,ijkco->gijko", spec_real, spectral[1], preferred_element_type=jnp.float32
    ) + jnp.einsum("gijkc,ijkco->gijko", spec_imag, spectral[0], preferred_element_type=jnp.float32)
    mixed_real = mixed_real.astype(jnp.bfloat16)
    mixed_imag = mixed_imag.astype(jnp.bfloat16)
    real_part, imag_part = in_one_piece((mixed_real, mixed_imag), GZ, 4, 1, 0)
    real_part, imag_part = inverse_complex(
        real_part.astype(jnp.float32),
        imag_part.astype(jnp.float32),
        cos_centred,
        sin_centred,
        "gijkc,ix->gxjkc",
    )
    real_part, imag_part = in_one_piece((real_part, imag_part), "gx", 1, 2, 0)
    real_part, imag_part = inverse_complex(
        real_part, imag_part, cos_centred, sin_centred, "gxjkc,jy->gxykc"
    )
    real_part, imag_part = in_one_piece((real_part, imag_part), "gy", 2, 3, 0)
    depth_part = inverse_real(real_part, imag_part, back_cos, back_sin, "gxykc,kz->gxyzc")
    branch = lax.all_to_all(depth_part, GZ, split_axis=3, concat_axis=4, tiled=True)
    skip = jnp.einsum("gxyzc,co->gxyzo", latent, skip_weight, preferred_element_type=jnp.float32)
    cells_total = float(GRID**3)
    local_cells = float(branch.shape[1] * branch.shape[2] * branch.shape[3])
    local_mean = jnp.sum(branch, axis=(1, 2, 3)) / local_cells
    local_centred = branch - local_mean[:, None, None, None, :]
    local_square = jnp.sum(local_centred * local_centred, axis=(1, 2, 3))
    local_count = jnp.full(local_mean.shape, local_cells, jnp.float32)
    merged = merged_by_axis((local_count, local_mean, local_square), GX_GY_GZ, merge_moments)
    mean = merged[1]
    variance = merged[2] / cells_total
    centred_branch = branch - mean[:, None, None, None, :]
    normed = centred_branch / jnp.sqrt(variance + NORM_FLOOR)[:, None, None, None, :]
    return jax.nn.gelu(normed + skip, approximate=True)


def solution(mesh):
    split = Mesh(
        mesh.devices.reshape(mesh.shape["gx"], mesh.shape["gy"], 4, 2), ("gx", "gy", "gz_0", "gz_1")
    )
    return jax.shard_map(
        body,
        mesh=split,
        in_specs=(
            P(None, None, GX_GY_GZ),
            P(None, "gx", "gy", GZ, None),
            P(None, "gx", "gy", GZ),
            P(),
            P(),
            P(),
            P(None, GZ, "gx", "gy", None, None),
            P(),
        ),
        out_specs=P(None, "gx", "gy", GZ, None),
        check_vma=False,
    )
```

profile of v0, /device:TPU:1, one launch (start us, length us, event | category | flops | bytes accessed | tf_op | source)
XLA Modules:
  0.0 357.7 jit_solution(7783864194018625842)
XLA Ops:
  0.0 4.5 %collective-permute-start = (f32[1,1,1,1,6,512]{5,0,4,3,2,1:T(1,128)}, f32[1,1,1,1,6,512]{5,0,4,3,2,1:T(1,128)S(1)}, u32[]{:S(2)}, u32[]{:S(2)}) collective-permute-start(f32[1,1,1,1,6,512]{5,0,4,3,2,1:T(1,128)} %bitcast.912), channel_id=1, source_target_pairs={{0,32},{32,64},{64,96},{96,128},{128,160},{160,192},{192,224},{1,3... | collective-permute-start | bytes 36872 | tf_op jit(solution)/shard_map/ppermute | solution.py:28
  4.5 1.3 collective-permute-start.1
  5.8 3.4 fusion.65
  10.1 3.2 collective-permute-start.2
  13.3 1.3 collective-permute-start.3
  14.6 3.5 collective-permute-done.3
  18.9 6.4 %collective-permute-start.4 = (f32[3,3,1,1,6,512]{5,0,4,3,2,1:T(4,128)S(1)}, f32[3,3,1,1,6,512]{5,0,4,3,2,1:T(4,128)S(1)}, u32[]{:S(2)}, u32[]{:S(2)}) collective-permute-start(f32[3,3,1,1,6,512]{5,0,4,3,2,1:T(4,128)S(1)} %pad_maximum_fusion.3), channel_id=1, source_target_pairs={{0,1},{1,2},{2,3},{3,4},{4,5},{5,6},{6,7},{8,9},{9,10},{10,11},{11... | collective-permute-start | bytes 331784 | tf_op jit(solution)/shard_map/ppermute | solution.py:28
  25.3 1.9 collective-permute-start.5
  27.3 4.4 %collective-permute-done.5 = f32[3,3,1,1,6,512]{5,0,4,3,2,1:T(4,128)S(1)} collective-permute-done((f32[3,3,1,1,6,512]{5,0,4,3,2,1:T(4,128)S(1)}, f32[3,3,1,1,6,512]{5,0,4,3,2,1:T(4,128)S(1)}, u32[]{:S(2)}, u32[]{:S(2)}) %collective-permute-start.5) | collective-permute-done | bytes 110624 | tf_op jit(solution)/shard_map/ppermute | solution.py:30
  33.6 3.7 %maximum_reduce_fusion = bf16[3,6,27,512]{3,2,1,0:T(8,128)(2,1)S(1)} fusion(bf16[1,1,6,27,512]{4,0,3,2,1:T(2,128)(2,1)S(1)} %get-tuple-element.357, bf16[1,1,6,27,512]{4,0,3,2,1:T(2,128)(2,1)S(1)} %get-tuple-element.356, bf16[1,1,6,27,512]{4,0,3,2,1:T(2,128)(2,1)S(1)} %convert_element_type.231), kind=kLoop, calls=%fused_computation.77 | loop fusion | flops 497664 | bytes 995328 | tf_op jit(solution)/shard_map/stack | solution.py:140
  38.3 135.5 %while.13 = (s32[]{:T(128)}, bf16[8,128,64]{2,1,0:T(8,128)(2,1)}, s32[8]{0:T(128)S(1)}, s32[1,8,16,8,32]{4,3,2,1,0:T(8,128)}, bf16[1,486,512]{2,1,0:T(8,128)(2,1...) while((s32[]{:T(128)}, bf16[8,128,64]{2,1,0:T(8,128)(2,1)}, ...), condition=%wide.region_3.4_spmd.clone, body=%wide.region_0.3_spmd.clone.sunk | while | flops 2148343808 | bytes 34155936 | solution.py:216
  41.7 3.5 fusion.355
  45.3 2.3 slice_add_fusion.7
  47.5 2.1 add.1595
  58.6 3.5 fusion.355
  62.2 2.3 slice_add_fusion.7
  64.5 2.1 add.1595
  75.6 3.5 fusion.355
  79.1 2.3 slice_add_fusion.7
  81.4 2.1 add.1595
  92.5 3.5 fusion.355
  96.1 2.3 slice_add_fusion.7
  98.4 2.1 add.1595
  109.5 3.5 fusion.355
  113.0 2.3 slice_add_fusion.7
  115.3 2.1 add.1595
  126.4 3.5 fusion.355
  130.0 2.3 slice_add_fusion.7
  132.2 2.1 add.1595
  143.3 3.5 fusion.355
  146.9 2.3 slice_add_fusion.7
  149.2 2.1 add.1595
  160.3 3.5 fusion.355
  163.8 2.3 slice_add_fusion.7
  166.1 2.1 add.1595
  173.8 2.8 copy.175
  177.6 9.4 %all_to_all.123 = bf16[8,2,4096]{2,1,0:T(2,128)(2,1)S(1)} all-to-all(bf16[8,2,4096]{2,1,0:T(2,128)(2,1)S(1)} %reshape.2088), channel_id=1, replica_groups=mesh['gx'=8,'gy'=4,'gz_0'=4,'gz_1'=2] {'gz_0','gz_1'}, dimensions={0} | all-to-all | bytes 262144 | tf_op jit(solution)/shard_map/all_to_all | solution.py:221
  189.3 2.0 convolution_bitcast_fusion.3
  191.2 2.0 fusion.57
  194.7 3.9 %all-to-all-start.1 = ((f32[4,1,8192]{2,1,0:T(1,128)}), f32[4,1,8192]{2,1,0:T(1,128)S(1)}, u32[]{:S(2)}, u32[]{:S(2)}) async-start(f32[4,1,8192]{2,1,0:T(1,128)} %reshape.2090), calls=%async_computation.1 | async-start | bytes 262144 | tf_op jit(solution)/shard_map/all_to_all | solution.py:40
  198.6 4.8 %all-to-all-done.1 = f32[4,1,8192]{2,1,0:T(1,128)S(1)} async-done(((f32[4,1,8192]{2,1,0:T(1,128)}), f32[4,1,8192]{2,1,0:T(1,128)S(1)}, u32[]{:S(2)}, u32[]{:S(2)}) %all-to-all-start.1) | async-done | bytes 131104 | tf_op jit(solution)/shard_map/all_to_all | solution.py:40
  209.3 15.8 %all_to_all.124 = f32[8,1,1024]{2,1,0:T(1,128)S(1)} all-to-all(f32[8,1,1024]{2,1,0:T(1,128)S(1)} %reshape.2092), channel_id=1, replica_groups=mesh['gx'=8,'gy'=4,'gz_0'=4,'gz_1'=2] {'gx'}, dimensions={0} | all-to-all | bytes 65536 | tf_op jit(solution)/shard_map/all_to_all | solution.py:40
  228.6 10.7 %all_to_all.125 = bf16[8,2,128]{2,1,0:T(2,128)(2,1)S(1)} all-to-all(bf16[8,2,128]{2,1,0:T(2,128)(2,1)S(1)} %reshape.2094), channel_id=1, replica_groups=mesh['gx'=8,'gy'=4,'gz_0'=4,'gz_1'=2] {'gz_0','gz_1'}, dimensions={0} | all-to-all | bytes 8192 | tf_op jit(solution)/shard_map/all_to_all | solution.py:40
  240.8 8.1 %all_to_all.126 = bf16[8,2,128]{2,1,0:T(2,128)(2,1)S(1)} all-to-all(bf16[8,2,128]{2,1,0:T(2,128)(2,1)S(1)} %reshape.2096), channel_id=1, replica_groups=mesh['gx'=8,'gy'=4,'gz_0'=4,'gz_1'=2] {'gz_0','gz_1'}, dimensions={0} | all-to-all | bytes 8192 | tf_op jit(solution)/shard_map/all_to_all | solution.py:40
  251.9 9.3 %all_to_all.127 = f32[8,1,1024]{2,1,0:T(1,128)S(1)} all-to-all(f32[8,1,1024]{2,1,0:T(1,128)S(1)} %reshape.2098), channel_id=1, replica_groups=mesh['gx'=8,'gy'=4,'gz_0'=4,'gz_1'=2] {'gx'}, dimensions={0} | all-to-all | bytes 65536 | tf_op jit(solution)/shard_map/all_to_all | solution.py:40
  264.8 2.3 copy.204
  267.1 3.1 reshape.2100
  270.2 3.5 all-to-all-start.6
  273.7 4.8 %all-to-all-done.6 = f32[4,1,8192]{2,1,0:T(1,128)S(1)} async-done(((f32[4,1,8192]{2,1,0:T(1,128)}), f32[4,1,8192]{2,1,0:T(1,128)S(1)}, u32[]{:S(2)}, u32[]{:S(2)}) %all-to-all-start.6) | async-done | bytes 131104 | tf_op jit(solution)/shard_map/all_to_all | solution.py:40
  279.4 2.5 reshape.2101
  281.9 1.5 copy.228
  285.7 1.8 copy.210
  287.5 1.5 reshape.2102
  289.0 6.3 %all-to-all-start.7 = ((f32[8,1,8192]{2,1,0:T(1,128)}), f32[8,1,8192]{2,1,0:T(1,128)S(1)}, u32[]{:S(2)}, u32[]{:S(2)}) async-start(f32[8,1,8192]{2,1,0:T(1,128)} %reshape.2102), calls=%async_computation.7 | async-start | bytes 524288 | tf_op jit(solution)/shard_map/all_to_all | solution.py:258
  295.3 6.5 %all-to-all-done.7 = f32[8,1,8192]{2,1,0:T(1,128)S(1)} async-done(((f32[8,1,8192]{2,1,0:T(1,128)}), f32[8,1,8192]{2,1,0:T(1,128)S(1)}, u32[]{:S(2)}, u32[]{:S(2)}) %all-to-all-start.7) | async-done | bytes 262176 | tf_op jit(solution)/shard_map/all_to_all | solution.py:258
  301.8 1.2 reduce.10
  303.0 2.0 reshape.2103
  305.1 1.7 copy.211
  307.6 1.6 copy.244
  309.4 15.6 %all-gather.4 = f32[8,3,64]{2,1,0:T(4,128)S(1)} all-gather(f32[1,3,64]{2,1,0:T(4,128)S(1)} %maximum_bitcast_fusion.1), channel_id=2, replica_groups=mesh['gx'=8,'gy'=4,'gz_0'=4,'gz_1'=2] {'gx'}, dimensions={0}, use_global_device_ids=true | all-gather | bytes 6912 | tf_op jit(solution)/shard_map/all_gather | solution.py:58
  325.0 8.1 %all-gather.5 = f32[4,3,64]{2,1,0:T(4,128)S(1)} all-gather(f32[1,3,64]{2,1,0:T(4,128)S(1)} %maximum_bitcast_fusion.2), channel_id=3, replica_groups=mesh['gx'=8,'gy'=4,'gz_0'=4,'gz_1'=2] {'gy'}, dimensions={0}, use_global_device_ids=true | all-gather | bytes 3840 | tf_op jit(solution)/shard_map/all_gather | solution.py:58
  333.2 8.1 %all-gather.6 = f32[4,3,64]{2,1,0:T(4,128)S(1)} all-gather(f32[1,3,64]{2,1,0:T(4,128)S(1)} %maximum_bitcast_fusion.3), channel_id=4, replica_groups=mesh['gx'=8,'gy'=4,'gz_0'=4,'gz_1'=2] {'gz_0'}, dimensions={0}, use_global_device_ids=true | all-gather | bytes 3840 | tf_op jit(solution)/shard_map/all_gather | solution.py:58
  341.4 12.6 %all-gather.7 = f32[2,3,64]{2,1,0:T(4,128)S(1)} all-gather(f32[1,3,64]{2,1,0:T(4,128)S(1)} %maximum_bitcast_fusion.4), channel_id=5, replica_groups=mesh['gx'=8,'gy'=4,'gz_0'=4,'gz_1'=2] {'gz_1'}, dimensions={0}, use_global_device_ids=true | all-gather | bytes 2304 | tf_op jit(solution)/shard_map/all_gather | solution.py:58
  354.0 2.2 copy.213
  (315 shorter events, 88.3 us)
Async XLA Ops:
  0.0 356.2 %copy-start = (bf16[64,64]{1,0:T(8,128)(2,1)S(1)}, bf16[64,64]{1,0:T(8,128)(2,1)}, u32[]{:S(2)}) copy-start(bf16[64,64]{1,0:T(8,128)(2,1)} %param.17) | copy-start | bytes 24580
  0.0 9.2 %collective-permute-start = (f32[1,1,1,1,6,512]{5,0,4,3,2,1:T(1,128)}, f32[1,1,1,1,6,512]{5,0,4,3,2,1:T(1,128)S(1)}, u32[]{:S(2)}, u32[]{:S(2)}) collective-permute-start(f32[1,1,1,1,6,512]{5,0,4,3,2,1:T(1,128)} %bitcast.912), channel_id=1, source_target_pairs={{0,32},{32,64},{64,96},{96,128},{128,160},{160,192},{192,224},{1,3... | collective-permute-start | bytes 36872 | tf_op jit(solution)/shard_map/ppermute | solution.py:28
  4.5 4.8 %collective-permute-start.1 = (f32[1,1,1,1,6,512]{5,0,4,3,2,1:T(1,128)}, f32[1,1,1,1,6,512]{5,0,4,3,2,1:T(1,128)S(1)}, u32[]{:S(2)}, u32[]{:S(2)}) collective-permute-start(f32[1,1,1,1,6,512]{5,0,4,3,2,1:T(1,128)} %bitcast.913), channel_id=1, source_target_pairs={{32,0},{64,32},{96,64},{128,96},{160,128},{192,160},{224,192},{33,... | collective-permute-start | bytes 36872 | tf_op jit(solution)/shard_map/ppermute | solution.py:30
  10.1 4.5 %collective-permute-start.2 = (f32[3,1,1,1,6,512]{5,0,4,3,2,1:T(4,128)S(1)}, f32[3,1,1,1,6,512]{5,0,4,3,2,1:T(4,128)S(1)}, u32[]{:S(2)}, u32[]{:S(2)}) collective-permute-start(f32[3,1,1,1,6,512]{5,0,4,3,2,1:T(4,128)S(1)} %pad_maximum_fusion.6), channel_id=1, source_target_pairs={{0,8},{8,16},{16,24},{1,9},{9,17},{17,25},{2,10},{10,18},{18,26},{... | collective-permute-start | bytes 110600 | tf_op jit(solution)/shard_map/ppermute | solution.py:28
  13.3 4.8 %collective-permute-start.3 = (f32[3,1,1,1,6,512]{5,0,4,3,2,1:T(4,128)S(1)}, f32[3,1,1,1,6,512]{5,0,4,3,2,1:T(4,128)S(1)}, u32[]{:S(2)}, u32[]{:S(2)}) collective-permute-start(f32[3,1,1,1,6,512]{5,0,4,3,2,1:T(4,128)S(1)} %pad_maximum_fusion.6), channel_id=1, source_target_pairs={{8,0},{16,8},{24,16},{9,1},{17,9},{25,17},{10,2},{18,10},{26,18},{... | collective-permute-start | bytes 110600 | tf_op jit(solution)/shard_map/ppermute | solution.py:30
  18.9 8.4 %collective-permute-start.4 = (f32[3,3,1,1,6,512]{5,0,4,3,2,1:T(4,128)S(1)}, f32[3,3,1,1,6,512]{5,0,4,3,2,1:T(4,128)S(1)}, u32[]{:S(2)}, u32[]{:S(2)}) collective-permute-start(f32[3,3,1,1,6,512]{5,0,4,3,2,1:T(4,128)S(1)} %pad_maximum_fusion.3), channel_id=1, source_target_pairs={{0,1},{1,2},{2,3},{3,4},{4,5},{5,6},{6,7},{8,9},{9,10},{10,11},{11... | collective-permute-start | bytes 331784 | tf_op jit(solution)/shard_map/ppermute | solution.py:28
  25.3 6.5 %collective-permute-start.5 = (f32[3,3,1,1,6,512]{5,0,4,3,2,1:T(4,128)S(1)}, f32[3,3,1,1,6,512]{5,0,4,3,2,1:T(4,128)S(1)}, u32[]{:S(2)}, u32[]{:S(2)}) collective-permute-start(f32[3,3,1,1,6,512]{5,0,4,3,2,1:T(4,128)S(1)} %pad_maximum_fusion.3), channel_id=1, source_target_pairs={{1,0},{2,1},{3,2},{4,3},{5,4},{6,5},{7,6},{9,8},{10,9},{11,10},{12... | collective-permute-start | bytes 331784 | tf_op jit(solution)/shard_map/ppermute | solution.py:30
  32.9 5.3 %copy-start.1 = (bf16[80,64]{0,1:T(8,128)(2,1)S(1)}, bf16[80,64]{0,1:T(8,128)(2,1)}, u32[]{:S(2)}) copy-start(bf16[80,64]{0,1:T(8,128)(2,1)} %param.15) | copy-start | bytes 30724
  32.9 5.3 %copy-start.4 = (bf16[80,80]{1,0:T(8,128)(2,1)S(1)}, bf16[80,80]{1,0:T(8,128)(2,1)}, u32[]{:S(2)}) copy-start(bf16[80,80]{1,0:T(8,128)(2,1)} %param.14) | copy-start | bytes 38404
  32.9 5.3 %copy-start.5 = (bf16[6,80]{1,0:T(8,128)(2,1)S(1)}, bf16[6,80]{1,0:T(8,128)(2,1)}, u32[]{:S(2)}) copy-start(bf16[6,80]{1,0:T(8,128)(2,1)} %param.13) | copy-start | bytes 2884
  194.7 8.7 %all-to-all-start.1 = ((f32[4,1,8192]{2,1,0:T(1,128)}), f32[4,1,8192]{2,1,0:T(1,128)S(1)}, u32[]{:S(2)}, u32[]{:S(2)}) async-start(f32[4,1,8192]{2,1,0:T(1,128)} %reshape.2090), calls=%async_computation.1 | async-start | bytes 262144 | tf_op jit(solution)/shard_map/all_to_all | solution.py:40
  226.5 13.1 %copy-start.3 = (bf16[2,2,2,4,64,64]{5,4,3,2,1,0:T(8,128)(2,1)S(1)}, bf16[2,2,2,4,64,64]{5,4,3,2,1,0:T(8,128)(2,1)}, u32[]{:S(2)}) copy-start(bf16[2,2,2,4,64,64]{5,4,3,2,1,0:T(8,128)(2,1)} %param.16) | copy-start | bytes 786436
  270.2 8.3 %all-to-all-start.6 = ((f32[4,1,8192]{2,1,0:T(1,128)}), f32[4,1,8192]{2,1,0:T(1,128)S(1)}, u32[]{:S(2)}, u32[]{:S(2)}) async-start(f32[4,1,8192]{2,1,0:T(1,128)} %reshape.2100), calls=%async_computation.6 | async-start | bytes 262144 | tf_op jit(solution)/shard_map/all_to_all | solution.py:40
  289.0 12.8 %all-to-all-start.7 = ((f32[8,1,8192]{2,1,0:T(1,128)}), f32[8,1,8192]{2,1,0:T(1,128)S(1)}, u32[]{:S(2)}, u32[]{:S(2)}) async-start(f32[8,1,8192]{2,1,0:T(1,128)} %reshape.2102), calls=%async_computation.7 | async-start | bytes 524288 | tf_op jit(solution)/shard_map/all_to_all | solution.py:258
  309.2 47.0 %copy-start.2 = (bf16[8,128,64]{2,1,0:T(8,128)(2,1)S(1)}, bf16[8,128,64]{2,1,0:T(8,128)(2,1)}, u32[]{:S(2)}) copy-start(bf16[8,128,64]{2,1,0:T(8,128)(2,1)} %get-tuple-element.193) | copy-start | bytes 393220
where the time goes:
time: 363 us; the launch traced here: 358 us
  blocking collectives  97.5 us (27%)
  local copies, waits for them, and re-layouts  83.7 us (23%)
  matrix products  51.6 us (14%)
  other arithmetic  51.4 us (14%)
  starting transfers between devices  32.3 us (9%)
  waiting for transfers between devices  24.2 us (7%)
  loops' own time  16 us (4%)
    all_gather x4, blocking collectives, all_in_one(): both, at, found = (lax.all_gather(jnp.concatenate(lines), axis), 0, {})  44.4 us
    all_to_all x4, blocking collectives, in_one_piece(): lax.all_to_all(both, axis, split_axis=split_dim, concat_axis=concat_dim,...  43.7 us
    dot_general x8, matrix products, one_slab(): jnp.dot(rows, slot_hot, preferred_element_type=jnp.float32)  28.3 us
    add x8, other arithmetic, one_slab(): found = found[0] + found[1] + found[2]  18.1 us
    add x8, local copies, waits for them, and re-layouts, one_slab(): found = found[0] + found[1] + found[2]  17 us
    another operation x1, loops' own time, body(): lax.map(one_slab, jnp.arange(geometry_count * cells_x, dtype=jnp.int32))  16 us
    unnamed x30, local copies, waits for them, and re-layouts  15.6 us
    ppermute x3, starting transfers between devices, extended(): lax.ppermute(tail, axis, [(i, (i + 1) % count) for i in range(ends)])  14 us
  transfers between devices with their start and end apart: 9, of which 7 were waited for; matrix products, arithmetic and copies ran while one was open for 1% of the time, Pallas kernels for 0%

commit v1 on v0

v1 whole, which is shorter than its diff:
```python
import functools
import math

import jax
import jax.numpy as jnp
import numpy as np
from jax import lax
from jax.experimental import pallas as pl
from jax.experimental.pallas import tpu as pltpu
from jax.sharding import PartitionSpec as P

GRID = 64
MODES = 16
NB = 32
KH = 80
CH = 64
PTS = 512
NX, NY, NZ = 8, 4, 8
F32 = jnp.float32
BF16 = jnp.bfloat16
MESH_ID = pl.DeviceIdType.MESH


def dot(a, b):
    return jnp.dot(a, b, preferred_element_type=F32)


def gelu(v):
    inner = v * (0.7978845608028654 + 0.035677408136300125 * (v * v))
    half = 0.5 * v
    return half + half * jnp.tanh(inner)


def split_two(values):
    upper = values.astype(BF16)
    return upper, (values - upper.astype(F32)).astype(BF16)


def halo_kernel(pts_ref, out_ref, own, around, rows, send_sem, recv_sem):
    at = (lax.axis_index("gx"), lax.axis_index("gy"), lax.axis_index("gz"))
    sizes = (NX, NY, NZ)
    steps = [
        (dx, dy, dz)
        for dx in (-1, 0, 1)
        for dy in (-1, 0, 1)
        for dz in (-1, 0, 1)
        if (dx, dy, dz) != (0, 0, 0)
    ]

    def peer(step):
        return tuple(lax.rem(a + d + n, n) for a, d, n in zip(at, step, sizes))

    barrier = pltpu.get_barrier_semaphore()
    for step in steps:
        pl.semaphore_signal(barrier, inc=1, device_id=peer(step), device_id_type=MESH_ID)
    pl.semaphore_wait(barrier, len(steps))
    for step in steps:
        slot = ((1 - step[0]) * 3 + (1 - step[1])) * 3 + (1 - step[2])
        pltpu.make_async_remote_copy(
            src_ref=pts_ref,
            dst_ref=around.at[slot],
            send_sem=send_sem,
            recv_sem=recv_sem,
            device_id=peer(step),
            device_id_type=MESH_ID,
        ).start()
    around[13] = pts_ref[...]
    rows[pl.ds(240, 16), :] = jnp.zeros((16, PTS), F32)
    many = around.at[pl.ds(0, 26)]
    pltpu.make_async_copy(many, many, recv_sem).wait()
    for b in range(27):
        block = around[b]
        place = block[0:3]
        upper = place.astype(BF16).astype(F32)
        rows[pl.ds(9 * b, 9), :] = jnp.concatenate([upper, place - upper, block[3:6]], axis=0)
    out_ref[...] = rows[...].astype(BF16)
    pltpu.make_async_copy(many, many, send_sem).wait()


def halo_table(points):
    return pl.pallas_call(
        halo_kernel,
        out_shape=jax.ShapeDtypeStruct((256, PTS), BF16),
        in_specs=[pl.BlockSpec(memory_space=pltpu.VMEM)],
        out_specs=pl.BlockSpec(memory_space=pltpu.VMEM),
        scratch_shapes=[
            pltpu.VMEM((8, 128), F32),
            pltpu.VMEM((27, 6, PTS), F32),
            pltpu.VMEM((256, PTS), F32),
            pltpu.SemaphoreType.DMA,
            pltpu.SemaphoreType.DMA,
        ],
        compiler_params=pltpu.CompilerParams(collective_id=0, has_side_effects=True),
        name="halo",
    )(points)


def encode_kernel(
    tab_ref, blk_ref, slot_ref, cnt_ref, pre_ref, ids_ref, rowblk_ref, win_ref, wmid_ref, wout_ref,
    wskip_ref, lat_ref, skip_ref, acc, held,
):
    one = jnp.ones((PTS, 128), BF16)
    none = jnp.zeros((PTS, 128), BF16)
    lanes = 2

    def slab(x, carry):
        acc[...] = jnp.zeros((KH, 128), F32)
        base = pre_ref[x]
        valid = cnt_ref[x]

        def chunk(c, inner):
            first = pl.multiple_of(c * 8, 8)
            slots = slot_ref[x, pl.ds(first, 8), :]
            blocks = blk_ref[x, pl.ds(first, 8), :]
            total = jnp.zeros((KH, 128), F32)
            for part in range(8 // lanes):
                hot = []
                for s in range(part * lanes, (part + 1) * lanes):
                    row = jnp.broadcast_to(slots[s : s + 1], (PTS, 128)).astype(BF16)
                    hot.append(jnp.where(ids_ref[...] == row, one, none))
                found = dot(tab_ref[...], jnp.concatenate(hot, axis=1)).astype(BF16)
                kept = []
                for n, s in enumerate(range(part * lanes, (part + 1) * lanes)):
                    row = jnp.broadcast_to(blocks[s : s + 1], (256, 128)).astype(BF16)
                    kept.append(
                        jnp.where(
                            rowblk_ref[...] == row, found[:, n * 128 : (n + 1) * 128], none[0:256]
                        )
                    )
                pre = dot(win_ref[...], jnp.concatenate(kept, axis=1))
                pre = pre + jnp.concatenate([base] * lanes, axis=1)
                hidden = gelu(pre).astype(BF16)
                hidden = gelu(dot(wmid_ref[...], hidden)).astype(BF16).astype(F32)
                for n, s in enumerate(range(part * lanes, (part + 1) * lanes)):
                    used = valid > (c * 8 + s).astype(F32)
                    total = total + jnp.where(used, hidden[:, n * 128 : (n + 1) * 128], 0.0)
            acc[...] += total
            return inner

        lax.fori_loop(0, NB // 8, chunk, 0)
        upper, lower = split_two(acc[...])
        values = dot(wout_ref[...], upper) + dot(wout_ref[...], lower)
        latent = (values / valid).astype(BF16)
        skip_ref[x] = dot(wskip_ref[...], latent)
        held[x] = latent.astype(F32)
        return carry

    lax.fori_loop(0, 8, slab, 0)
    for x in range(8):
        lat_ref[:, x, :] = held[x]


def encode(tab, blk, slot, cnt, pre, ids, rowblk, win, wmid, wout, wskip):
    vmem = pl.BlockSpec(memory_space=pltpu.VMEM)
    return pl.pallas_call(
        encode_kernel,
        out_shape=(
            jax.ShapeDtypeStruct((CH, 8, 128), F32),
            jax.ShapeDtypeStruct((8, CH, 128), F32),
        ),
        in_specs=[vmem] * 11,
        out_specs=(vmem, vmem),
        scratch_shapes=[pltpu.VMEM((KH, 128), F32), pltpu.VMEM((8, CH, 128), F32)],
        name="encode",
    )(tab, blk, slot, cnt, pre, ids, rowblk, win, wmid, wout, wskip)


@functools.cache
def transform_tables():
    m = np.arange(GRID)
    centred = np.where(np.arange(MODES) < MODES // 2, np.arange(MODES), np.arange(MODES) - MODES)
    third = np.arange(MODES)

    def angles(f):
        return 2.0 * np.pi * ((f[:, None] * m[None, :]) % GRID) / GRID

    cos_c, sin_c = np.cos(angles(centred)), np.sin(angles(centred))
    cos_t, sin_t = np.cos(angles(third)), np.sin(angles(third))
    eye_y, eye_k = np.eye(16), np.eye(4)
    both = np.stack([cos_t, -sin_t], axis=-1)
    fz = np.einsum(
        "kqzr,yw->qyzkwr", both.reshape(MODES, NZ, 8, 2), eye_y
    ).reshape(NZ, 16, 8, 4, 4, 16, 2)
    fz = fz.transpose(0, 1, 2, 3, 5, 4, 6).reshape(1024, 512)
    turn = np.stack([np.stack([cos_c, -sin_c], -1), np.stack([sin_c, cos_c], -1)], -2)
    fy = np.einsum("jpyro,kl->pykrojl", turn.reshape(MODES, NY, 16, 2, 2), eye_k).reshape(512, 128)
    fx = np.concatenate([cos_c, sin_c], axis=0)
    ix = np.concatenate([cos_c.T, sin_c.T], axis=0)
    back = np.stack([np.stack([cos_c, sin_c], -1), np.stack([-sin_c, cos_c], -1)], -2)
    iy = np.einsum("jqyro,kl->rjkqylo", back.reshape(MODES, NY, 16, 2, 2), eye_k).reshape(128, 512)
    weight = np.where(third == 0, 1.0, 2.0)[:, None, None] / GRID**3
    iz = np.einsum(
        "kqzr,yw->kyrqwz", (both * weight).reshape(MODES, NZ, 8, 2), eye_y
    ).reshape(4, 4, 16, 2, NZ, 16, 8)
    iz = iz.transpose(0, 2, 1, 3, 4, 5, 6).reshape(512, 1024)
    mirror = np.zeros((MODES, MODES))
    for i in range(MODES):
        if i != MODES // 2:
            mirror[i, (MODES - i) % MODES] = 1.0
    flip = np.einsum(
        "rs,ij,kl->riksjl", np.diag([1.0, -1.0]), mirror.T, np.diag([1.0, 0, 0, 0])
    ).reshape(128, 128)
    return fz, fy, fx, ix, iy, iz, mirror, flip


def two_tables(table):
    import ml_dtypes

    upper = table.astype(np.float32).astype(ml_dtypes.bfloat16)
    lower = (table - upper.astype(np.float64)).astype(np.float32).astype(ml_dtypes.bfloat16)
    return jnp.asarray(upper), jnp.asarray(lower)


def layer_kernel(
    lat_ref, skip_ref, w0_ref, w1_ref, fzh_ref, fzl_ref, fyh_ref, fyl_ref, fxh_ref, fxl_ref,
    ixh_ref, ixl_ref, iyh_ref, iyl_ref, izh_ref, mir_ref, flip_ref, out_ref,
    s1, r1, s2, r2, s3, r3, s4, r4, s5, r5, s6, r6, s7, r7, sv, rv, s8, r8, spec, grid, wide,
    send_sem, recv_sem,
):
    gx, gy, gz = lax.axis_index("gx"), lax.axis_index("gy"), lax.axis_index("gz")
    barrier = pltpu.get_barrier_semaphore()

    def along_x(d):
        return (lax.rem(gx + d, NX), gy, gz)

    def along_y(d):
        return (gx, lax.rem(gy + d, NY), gz)

    def along_z(d):
        return (gx, gy, lax.rem(gz + d, NZ))

    plane = [
        (lax.rem(gx + dx, NX), gy, lax.rem(gz + dz, NZ))
        for dx in range(NX)
        for dz in range(NZ)
        if (dx, dz) != (0, 0)
    ]
    peers = plane + [along_y(d) for d in range(1, NY)]
    for peer in peers:
        pl.semaphore_signal(barrier, inc=1, device_id=peer, device_id_type=MESH_ID)
    s1[...] = lat_ref[...].reshape(NZ, 64, 128).astype(BF16)
    pl.semaphore_wait(barrier, len(peers))

    def send(n, source, target, peer):
        pltpu.make_async_remote_copy(
            src_ref=source,
            dst_ref=target,
            send_sem=send_sem.at[n],
            recv_sem=recv_sem.at[n],
            device_id=peer,
            device_id_type=MESH_ID,
        ).start()

    def arrived(n, buffer, count):
        part = buffer.at[pl.ds(0, count)]
        pltpu.make_async_copy(part, part, recv_sem.at[n]).wait()

    def left(n, buffer, count):
        part = buffer.at[pl.ds(0, count)]
        pltpu.make_async_copy(part, part, send_sem.at[n]).wait()

    for d in range(1, NZ):
        peer = along_z(d)
        send(0, s1.at[peer[2]], r1.at[gz], peer)
    r1[gz] = s1[gz]
    arrived(0, r1, NZ - 1)
    row = jnp.concatenate([r1[q] for q in range(NZ)], axis=1)
    deep = dot(row, fzh_ref[...]) + dot(row, fzl_ref[...])
    for q in range(NY):
        s2[q] = deep[:, q * 128 : (q + 1) * 128]
    for d in range(1, NY):
        peer = along_y(d)
        send(1, s2.at[peer[1]], r2.at[gy], peer)
    r2[gy] = s2[gy]
    arrived(1, r2, NY - 1)
    upper, lower = split_two(jnp.concatenate([r2[q] for q in range(NY)], axis=1))
    flat = dot(upper, fyh_ref[...]) + dot(upper, fyl_ref[...]) + dot(lower, fyh_ref[...])
    s3[...] = flat.reshape(NX, 8, 128)
    for d in range(1, NX):
        peer = along_x(d)
        send(2, s3.at[peer[0]], r3.at[gx], peer)
    r3[gx] = s3[gx]
    arrived(2, r3, NX - 1)
    upper, lower = split_two(r3[...].reshape(GRID, 128))
    both = dot(fxh_ref[...], upper) + dot(fxl_ref[...], upper) + dot(fxh_ref[...], lower)
    lane = lax.broadcasted_iota(jnp.int32, (MODES, 128), 1)
    turned = pltpu.roll(both[MODES:], 64, axis=1)
    modes = both[:MODES] + jnp.where(lane < 64, turned, -turned)
    for q in range(NZ):
        s4[q] = modes[2 * q : 2 * q + 2]
    for peer in plane:
        send(3, s4.at[peer[2]], r4.at[gz * NX + gx], peer)
    r4[gz * NX + gx] = s4[gz]
    arrived(3, r4, 63)
    for c in range(CH):
        for i in range(2):
            spec[i, pl.ds(c, 1), :] = r4[c, pl.ds(i, 1), :]
    srow = lax.broadcasted_iota(jnp.int32, (MODES, 128), 0)
    pick = jnp.where(lane == (srow // 8) * 64 + gx * 8 + srow % 8, 1.0, 0.0).astype(BF16)
    found = []
    for i in range(2):
        values = spec[i].astype(BF16)
        found.append(
            lax.dot_general(
                pick,
                jnp.concatenate([values, values], axis=0),
                (((1,), (1,)), ((), ())),
                preferred_element_type=F32,
            )
        )
    rows = jnp.concatenate(
        [found[0][0:8], found[1][0:8], found[0][8:16], found[1][8:16]], axis=0
    )
    spread = jnp.concatenate([rows] * 8, axis=1)
    big_row = lax.broadcasted_iota(jnp.int32, (32, 1024), 0)
    big_lane = lax.broadcasted_iota(jnp.int32, (32, 1024), 1)
    spread = jnp.where(big_lane // CH == big_row % MODES, spread, 0.0).astype(BF16)
    by_real, by_imag = dot(spread, w0_ref[...]), dot(spread, w1_ref[...])
    mixed_real = by_real[0:16] - by_imag[16:32]
    mixed_imag = by_imag[0:16] + by_real[16:32]
    for i in range(2):
        mine = jnp.concatenate(
            [mixed_real[8 * i : 8 * i + 8], mixed_imag[8 * i : 8 * i + 8]], axis=0
        ).astype(BF16)
        placed = lax.dot_general(
            mine, pick, (((0,), (0,)), ((), ())), preferred_element_type=F32
        )
        spec[i] = placed
    for c in range(CH):
        for i in range(2):
            s5[c, pl.ds(i, 1), :] = spec[i, pl.ds(c, 1), :]
    for peer in plane:
        send(4, s5.at[peer[2] * NX + peer[0]], r5.at[gz * NX + gx], peer)
    r5[gz * NX + gx] = s5[gz * NX + gx]
    arrived(4, r5, 63)
    for q in range(NZ):
        pair = r5[q * NX]
        for n in range(1, NX):
            pair = pair + r5[q * NX + n]
        grid[pl.ds(2 * q, 2), :] = pair
    is_mean = (srow == 0) & ((lane == 0) | (lane == 64)) & (gy == 0)
    values = jnp.where(is_mean, 0.0, grid[...])
    exact = values.astype(BF16)
    weight = jnp.where((lane % 4 == 0) & (gy == 0), 0.5, 2.0)
    pairs = dot(dot(mir_ref[...], exact).astype(BF16), flip_ref[...])
    pairs = jnp.where(gy == 0, 0.5 * pairs, 0.0)
    power = values * (weight * values + pairs)
    power = jnp.sum(jnp.sum(power, axis=1, keepdims=True), axis=0, keepdims=True)
    both = dot(ixh_ref[...], exact) + dot(ixl_ref[...], exact)
    lane = lax.broadcasted_iota(jnp.int32, (GRID, 128), 1)
    turned = pltpu.roll(both[GRID:], 64, axis=1)
    cells = both[:GRID] + jnp.where(lane < 64, -turned, turned)
    s6[:, 0:8, :] = cells.reshape(NX, 8, 128)
    s6[:, 8:16, :] = jnp.broadcast_to(power[None], (NX, 8, 128))
    for d in range(1, NX):
        peer = along_x(d)
        send(5, s6.at[peer[0]], r6.at[gx], peer)
    r6[gx] = s6[gx]
    arrived(5, r6, NX - 1)
    plain = r6[:, 0:8, :].reshape(64, 128).astype(BF16)
    flat = dot(plain, iyh_ref[...]) + dot(plain, iyl_ref[...])
    own_power = r6[:, 8:16, :].reshape(64, 128)
    for q in range(NY):
        s7[q] = flat[:, q * 128 : (q + 1) * 128].astype(BF16)
    sv[...] = own_power
    rv[gy] = own_power
    r7[gy] = s7[gy]
    for d in range(1, NY):
        peer = along_y(d)
        send(6, s7.at[peer[1]], r7.at[gy], peer)
        send(7, sv, rv.at[gy], peer)
    arrived(6, r7, NY - 1)
    row = jnp.concatenate([r7[q] for q in range(NY)], axis=1)
    depth = dot(row, izh_ref[...])
    arrived(7, rv, NY - 1)
    power = (rv[0] + rv[1]) + (rv[2] + rv[3])
    scale = 1.0 / jnp.sqrt(power * (1.0 / float(GRID) ** 6) + 1.0)
    for q in range(NZ):
        s8[q] = (depth[:, q * 128 : (q + 1) * 128] * scale).astype(BF16)
    for d in range(1, NZ):
        peer = along_z(d)
        send(8, s8.at[peer[2]], r8.at[gz], peer)
    r8[gz] = s8[gz]
    arrived(8, r8, NZ - 1)
    wide[...] = r8[...].astype(F32).reshape(CH, 8, 128)
    for x in range(8):
        out_ref[x] = gelu(wide[:, x, :] + skip_ref[x]).T
    left(0, r1, NZ - 1)
    left(1, r2, NY - 1)
    left(2, r3, NX - 1)
    left(3, r4, 63)
    left(4, r5, 63)
    left(5, r6, NX - 1)
    left(6, r7, NY - 1)
    left(7, rv, NY - 1)
    left(8, r8, NZ - 1)


def layer(lat, skip, w0, w1):
    fz, fy, fx, ix, iy, iz, mirror, flip = transform_tables()
    tables = [*two_tables(fz), *two_tables(fy), *two_tables(fx), *two_tables(ix), *two_tables(iy)]
    tables += [two_tables(iz)[0], two_tables(mirror)[0], two_tables(flip)[0]]
    vmem = pl.BlockSpec(memory_space=pltpu.VMEM)
    v = pltpu.VMEM
    return pl.pallas_call(
        layer_kernel,
        out_shape=jax.ShapeDtypeStruct((8, 128, CH), F32),
        in_specs=[vmem] * (4 + len(tables)),
        out_specs=vmem,
        scratch_shapes=[
            v((NZ, 64, 128), BF16), v((NZ, 64, 128), BF16),
            v((NY, 64, 128), F32), v((NY, 64, 128), F32),
            v((NX, 8, 128), F32), v((NX, 8, 128), F32),
            v((NZ, 2, 128), F32), v((CH, 2, 128), F32),
            v((CH, 2, 128), F32), v((CH, 2, 128), F32),
            v((NX, 16, 128), F32), v((NX, 16, 128), F32),
            v((NY, 64, 128), BF16), v((NY, 64, 128), BF16),
            v((64, 128), F32), v((NY, 64, 128), F32),
            v((NZ, 64, 128), BF16), v((NZ, 64, 128), BF16),
            v((2, CH, 128), F32), v((MODES, 128), F32), v((CH, 8, 128), F32),
            pltpu.SemaphoreType.DMA((9,)), pltpu.SemaphoreType.DMA((9,)),
        ],
        compiler_params=pltpu.CompilerParams(collective_id=1, has_side_effects=True),
        name="layer",
    )(lat, skip, w0, w1, *tables)


def body(point_data, neighbours, counts, kernel_in, kernel_mid, kernel_out, spectral, skip_weight):
    place = [lax.axis_index(a) for a in ("gx", "gy", "gz")]
    tab = halo_table(point_data[0])
    near = jnp.swapaxes(neighbours.reshape(8, 128, NB), 1, 2)
    owner = near // PTS
    offset_z = owner % NZ - place[2] + 1
    offset_y = owner // NZ % NY - place[1] + 1
    offset_x = owner // (NZ * NY) - place[0] + 1
    blk = ((offset_x * 3 + offset_y) * 3 + offset_z).astype(F32)
    slot = (near % PTS - 256).astype(F32)
    cnt = counts.reshape(8, 1, 128).astype(F32)
    wide_in = kernel_in.astype(F32)

    def centre(start, count):
        cells = start * count + jnp.arange(count, dtype=jnp.int32)
        return (cells.astype(F32) + 0.5) / GRID

    cx, cy, cz = centre(place[0], 8), centre(place[1], 16), centre(place[2], 8)
    inner = (
        wide_in[1][:, None, None] * cy[None, :, None] + wide_in[2][:, None, None] * cz[None, None, :]
    ).reshape(KH, 128)
    pre = -(inner[None] + (wide_in[0][None, :] * cx[:, None])[:, :, None])
    nine = jnp.concatenate([kernel_in[0:3], kernel_in[0:3], kernel_in[3:6]], axis=0)
    win = jnp.pad(jnp.concatenate([nine] * 27, axis=0), ((0, 13), (0, 0))).T
    ids = jnp.broadcast_to((jnp.arange(PTS) - 256).astype(BF16)[:, None], (PTS, 128))
    rowblk = jnp.broadcast_to((jnp.arange(256) // 9).astype(BF16)[:, None], (256, 128))
    lat, skip = encode(
        tab, blk, slot, cnt, pre, ids, rowblk, win, kernel_mid.T, kernel_out.T, skip_weight.T
    )
    out = layer(lat, skip, spectral[0].reshape(1024, CH), spectral[1].reshape(1024, CH))
    return out.reshape(1, 8, 16, 8, CH)


def solution(mesh):
    cells = P(None, "gx", "gy", "gz", None)
    return jax.shard_map(
        body,
        mesh=mesh,
        in_specs=(
            P(None, None, ("gx", "gy", "gz")),
            cells,
            P(None, "gx", "gy", "gz"),
            P(),
            P(),
            P(),
            P(None, "gz", "gx", "gy", None, None),
            P(),
        ),
        out_specs=cells,
        check_vma=False,
    )
```

time: 363 us -> 146 us (0.40); the launches traced: 358 us -> 146 us
  Pallas kernels: 0 us -> 133 us
  blocking collectives: 97.5 us -> 0 us
  local copies, waits for them, and re-layouts: 83.7 us -> 10.2 us
  matrix products: 51.6 us -> 0 us
  other arithmetic: 51.4 us -> 2.22 us
  starting transfers between devices: 32.3 us -> 0 us
  waiting for transfers between devices: 24.2 us -> 0 us
  loops' own time: 16 us -> 0 us
    pallas_call x0 -> x3, Pallas kernels: none -> 133 us  [the longest x1 65.9 us: encode(): pl.pallas_call(encode_kernel, out_shape=(jax.ShapeDtypeStruct((CH, 8, 128...]
    all_to_all x5 -> x0, blocking collectives: 53.1 us -> none  [the longest x4 43.7 us: in_one_piece(): lax.all_to_all(both, axis, split_axis=split_dim, concat_axis=concat_dim,...]
    dot_general x33 -> x0, matrix products: 46.5 us -> none  [the longest x8 28.3 us: one_slab(): jnp.dot(rows, slot_hot, preferred_element_type=jnp.float32)]
    all_gather x4 -> x0, blocking collectives: 44.4 us -> none  [all_in_one(): both, at, found = (lax.all_gather(jnp.concatenate(lines), axis), 0, {})]
    add x19 -> x1, other arithmetic: 21.8 us -> 0.01 us  [body(): wide_in[1][:, None, None] * cy[None, :, None]]
    ppermute x6 -> x0, starting transfers between devices: 18.5 us -> none  [the longest x3 14 us: extended(): lax.ppermute(tail, axis, [(i, (i + 1) % count) for i in range(ends)])]
    dynamic_slice x32 -> x0, local copies, waits for them, and re-layouts: 18 us -> none  [the longest x8 7.09 us: one_slab(): lax.dynamic_index_in_dim(lax.dynamic_index_in_dim(block_index, geometry,...]
    add x8 -> x1, local copies, waits for them, and re-layouts: 17 us -> 0.08 us  [body(): wide_in[1][:, None, None] * cy[None, :, None]]
  transfers between devices with their start and end apart: 9 -> 0, of which waited for: 7 -> 0; matrix products, arithmetic and copies ran while one was open for 1% -> 0% of each run, Pallas kernels for 0% -> 0%
where the time goes in v1:
time: 146 us
  Pallas kernels  133 us (91%)
  local copies, waits for them, and re-layouts  10.2 us (7%)
  other arithmetic  2.22 us (2%)
    pallas_call x1, Pallas kernels, encode(): pl.pallas_call(encode_kernel, out_shape=(jax.ShapeDtypeStruct((CH, 8, 128...  65.9 us
    pallas_call x1, Pallas kernels, layer(): pl.pallas_call(layer_kernel, out_shape=jax.ShapeDtypeStruct((8, 128, CH),...  50.2 us
    pallas_call x1, Pallas kernels, halo_table(): pl.pallas_call(halo_kernel, out_shape=jax.ShapeDtypeStruct((256, PTS), BF...  17.3 us
    unnamed x19, local copies, waits for them, and re-layouts  5.26 us

profile of v1, /device:TPU:1, one launch (start us, length us, event | category | flops | bytes accessed | tf_op | source)
XLA Modules:
  0.0 145.9 jit_solution(10528915008042643134)
XLA Ops:
  0.0 0.0 copy-start.5
  0.1 0.7 copy-done.5
  0.7 0.0 copy-start.6
  0.7 0.1 broadcast_multiply_fusion.1
  0.8 0.1 broadcast_multiply_fusion.2
  0.9 0.1 broadcast_multiply_fusion
  1.0 0.5 copy-done.6
  1.4 0.0 copy-start.4
  1.4 0.6 copy.142
  2.1 0.1 copy-done.4
  2.2 0.0 copy-start.3
  2.2 0.7 copy.138
  2.9 0.1 copy.83
  3.0 0.0 copy-done.3
  3.0 0.7 copy.137
  3.7 0.1 copy.84
  3.8 0.0 copy-start.2
  3.8 0.8 concatenate.6
  4.6 0.0 copy-start
  4.6 0.6 pad_bitcast_fusion.win_ref
  5.3 0.0 copy-done.2
  5.3 0.1 copy.81
  5.3 0.7 convert_element_type.54
  6.0 0.1 copy.82
  6.1 0.7 broadcast_in_dim.5.rowblk_ref
  6.9 0.8 broadcast_in_dim.4.ids_ref
  7.7 0.0 copy-done
  7.7 0.2 copy.80
  7.8 1.1 fusion.14
  8.9 17.3 %halo.1.tab_ref = bf16[256,512]{1,0:T(8,128)(2,1)} custom-call(f32[6,512]{1,0:T(8,128)} %bitcast.57), custom_call_target="tpu_custom_call" | custom-call | tf_op jit(solution)/shard_map/halo/pallas_call | solution.py:81
  26.2 0.9 add_negate_fusion.pre_ref
  27.1 0.0 copy-start.1
  27.1 65.9 %encode.1 = (f32[64,8,128]{2,1,0:T(8,128)}, f32[8,64,128]{2,1,0:T(8,128)}) custom-call(bf16[256,512]{1,0:T(8,128)(2,1)} %halo.1.tab_ref, f32[8,32,128]{2,1,0:T(8,128)} %get-tuple-element.12.blk_ref, f32[8,32,128]{2,1,0:T(8,128)} %get-tuple-element.11.slot_ref, f32[8,1,128]{2,1,0:T(1,128)} %bitcast.59, f32[8,80,128]{2,1,0:T(8,128)} %add_negate_fusion.pre_ref, ...), custom_call_target="tpu_custom_call" | custom-call | tf_op jit(solution)/shard_map/encode/pallas_call | solution.py:155
  93.0 0.0 copy-done.1
  93.0 0.8 fusion.21
  93.8 50.2 %layer.1 = f32[8,128,64]{2,1,0:T(8,128)} custom-call(f32[64,8,128]{2,1,0:T(8,128)} %get-tuple-element.7.lat_ref, f32[8,64,128]{2,1,0:T(8,128)} %get-tuple-element.8.skip_ref, bf16[1024,64]{1,0:T(8,128)(2,1)} %bitcast.53, bf16[1024,64]{1,0:T(8,128)(2,1)} %bitcast.52, bf16[1024,512]{1,0:T(8,128)(2,1)} %constant.135.clone.fzh_ref, ...), custom_call_target="tpu_custom_call" | custom-call | tf_op jit(solution)/shard_map/layer/pallas_call | solution.py:405
  144.0 1.9 %copy.144 = f32[1,8,16,8,64]{4,3,2,1,0:T(8,128)} copy(f32[1,8,16,8,64]{4,3,2,1,0:T(8,128)} %bitcast.51) | data formatting | bytes 524288
  (10 shorter events, 0.1 us)
Async XLA Ops:
  0.0 0.7 copy-start.5
  0.7 0.7 copy-start.6
  1.4 0.7 copy-start.4
  2.2 0.8 copy-start.3
  3.8 1.5 %copy-start.2 = (s32[1,8,16,8]{2,3,1,0:T(8,128)S(1)}, s32[1,8,16,8]{2,3,1,0:T(8,128)}, u32[]{:S(2)}) copy-start(s32[1,8,16,8]{2,3,1,0:T(8,128)} %param.23) | copy-start | bytes 12292
  4.6 3.0 %copy-start = (s32[1,8,16,8,32]{4,3,2,1,0:T(8,128)S(1)}, s32[1,8,16,8,32]{4,3,2,1,0:T(8,128)}, u32[]{:S(2)}) copy-start(s32[1,8,16,8,32]{4,3,2,1,0:T(8,128)} %param.22) | copy-start | bytes 393220
  27.1 65.9 %copy-start.1 = (bf16[2,2,2,4,64,64]{5,4,3,2,1,0:T(8,128)(2,1)S(1)}, bf16[2,2,2,4,64,64]{5,4,3,2,1,0:T(8,128)(2,1)}, u32[]{:S(2)}) copy-start(bf16[2,2,2,4,64,64]{5,4,3,2,1,0:T(8,128)(2,1)} %param.27) | copy-start | bytes 786436

commit v2 on v1

--- a/solution.py
+++ b/solution.py
@@ -95,74 +95,110 @@
     )(points)
 
 
+def dot_first(a, b):
+    return lax.dot_general(a, b, (((0,), (0,)), ((), ())), preferred_element_type=F32)
+
+
+def twice_gelu(v):
+    inner = v * (0.7978845608028654 + 0.035677408136300125 * (v * v))
+    return v + v * jnp.tanh(inner)
+
+
+CHUNKS = 32
+PART = 256
+
+
 def encode_kernel(
-    tab_ref, blk_ref, slot_ref, cnt_ref, pre_ref, ids_ref, rowblk_ref, win_ref, wmid_ref, wout_ref,
-    wskip_ref, lat_ref, skip_ref, acc, held,
+    tab_ref, blk_ref, slot_ref, cnt_ref, kin_ref, kmid_ref, kout_ref, wskip_ref,
+    lat_ref, skip_ref, acc, pre, ids, rowblk, win, wmid, masked_a, masked_b, hid_a, hid_b,
 ):
+    def iota(shape, dim):
+        return lax.broadcasted_iota(jnp.int32, shape, dim)
+
+    ids[...] = (iota((PTS, 128), 0) - 256).astype(F32).astype(BF16)
+    rowblk[...] = (iota((256, 128), 0) // 9).astype(F32).astype(BF16)
+    col = iota((6, 256), 1)
+    nine = col % 9
+    source = jnp.where(nine < 3, nine, nine - 3)
+    chosen = jnp.where((source == iota((6, 256), 0)) & (col < 243), 1.0, 0.0).astype(BF16)
+    win[...] = dot_first(kin_ref[...], chosen).astype(BF16)
+    eye = jnp.where(iota((KH, KH), 0) == iota((KH, KH), 1), 0.5, 0.0).astype(BF16)
+    wmid[...] = dot_first(kmid_ref[...], eye).astype(BF16)
+    row, lane = iota((6, 128), 0), iota((6, 128), 1)
+    index_y = lax.axis_index("gy") * 16 + lane // 8
+    index_z = lax.axis_index("gz") * 8 + lane % 8
+    for x in range(8):
+        index = jnp.where(row == 0, lax.axis_index("gx") * 8 + x, jnp.where(row == 1, index_y, index_z))
+        centre = jnp.where(row < 3, -(index.astype(F32) + 0.5) / GRID, 0.0).astype(BF16)
+        pre[x] = dot_first(kin_ref[...], centre)
+    acc[...] = jnp.zeros((8, KH, 128), F32)
     one = jnp.ones((PTS, 128), BF16)
     none = jnp.zeros((PTS, 128), BF16)
-    lanes = 2
-
-    def slab(x, carry):
-        acc[...] = jnp.zeros((KH, 128), F32)
-        base = pre_ref[x]
-        valid = cnt_ref[x]
-
-        def chunk(c, inner):
-            first = pl.multiple_of(c * 8, 8)
-            slots = slot_ref[x, pl.ds(first, 8), :]
-            blocks = blk_ref[x, pl.ds(first, 8), :]
-            total = jnp.zeros((KH, 128), F32)
-            for part in range(8 // lanes):
-                hot = []
-                for s in range(part * lanes, (part + 1) * lanes):
-                    row = jnp.broadcast_to(slots[s : s + 1], (PTS, 128)).astype(BF16)
-                    hot.append(jnp.where(ids_ref[...] == row, one, none))
-                found = dot(tab_ref[...], jnp.concatenate(hot, axis=1)).astype(BF16)
-                kept = []
-                for n, s in enumerate(range(part * lanes, (part + 1) * lanes)):
-                    row = jnp.broadcast_to(blocks[s : s + 1], (256, 128)).astype(BF16)
-                    kept.append(
-                        jnp.where(
-                            rowblk_ref[...] == row, found[:, n * 128 : (n + 1) * 128], none[0:256]
-                        )
-                    )
-                pre = dot(win_ref[...], jnp.concatenate(kept, axis=1))
-                pre = pre + jnp.concatenate([base] * lanes, axis=1)
-                hidden = gelu(pre).astype(BF16)
-                hidden = gelu(dot(wmid_ref[...], hidden)).astype(BF16).astype(F32)
-                for n, s in enumerate(range(part * lanes, (part + 1) * lanes)):
-                    used = valid > (c * 8 + s).astype(F32)
-                    total = total + jnp.where(used, hidden[:, n * 128 : (n + 1) * 128], 0.0)
-            acc[...] += total
-            return inner
-
-        lax.fori_loop(0, NB // 8, chunk, 0)
-        upper, lower = split_two(acc[...])
-        values = dot(wout_ref[...], upper) + dot(wout_ref[...], lower)
-        latent = (values / valid).astype(BF16)
-        skip_ref[x] = dot(wskip_ref[...], latent)
-        held[x] = latent.astype(F32)
+
+    def step(t, masked_out, masked_in, hid_out, hid_in):
+        early = jnp.minimum(t, CHUNKS - 1)
+        middle = jnp.clip(t - 1, 0, CHUNKS - 1)
+        late = jnp.maximum(t - 2, 0)
+        slots, blocks = slot_ref[early], blk_ref[early]
+        base = jnp.concatenate([pre[middle // 4]] * 2, axis=1)
+        valid = jnp.where(t >= 2, cnt_ref[late // 4], 0.0)
+        first = (late % 4 * 8).astype(F32)
+        total = jnp.zeros((KH, 128), F32)
+        for part in range(4):
+            span = pl.ds(part * PART, PART)
+            hot = []
+            for s in (2 * part, 2 * part + 1):
+                chosen = jnp.broadcast_to(slots[s : s + 1], (PTS, 128)).astype(BF16)
+                hot.append(jnp.where(ids[...] == chosen, one, none))
+            found = dot(tab_ref[...], jnp.concatenate(hot, axis=1))
+            ahead = dot(win[...], masked_in[:, span])
+            last = dot(wmid[...], hid_in[:, span])
+            hid_out[:, span] = twice_gelu(ahead + base).astype(BF16)
+            last = twice_gelu(last).astype(BF16).astype(F32)
+            for n in range(2):
+                used = valid > first + (2 * part + n)
+                total = total + jnp.where(used, last[:, n * 128 : (n + 1) * 128], 0.0)
+            found = found.astype(BF16)
+            for n in range(2):
+                s = 2 * part + n
+                chosen = jnp.broadcast_to(blocks[s : s + 1], (256, 128)).astype(BF16)
+                masked_out[:, pl.ds(s * 128, 128)] = jnp.where(
+                    rowblk[...] == chosen, found[:, n * 128 : (n + 1) * 128], none[0:256]
+                )
+        acc[late // 4] += total
+
+    def two_steps(tt, carry):
+        step(2 * tt, masked_a, masked_b, hid_a, hid_b)
+        step(2 * tt + 1, masked_b, masked_a, hid_b, hid_a)
         return carry
 
-    lax.fori_loop(0, 8, slab, 0)
+    lax.fori_loop(0, CHUNKS // 2 + 1, two_steps, 0)
     for x in range(8):
-        lat_ref[:, x, :] = held[x]
-
-
-def encode(tab, blk, slot, cnt, pre, ids, rowblk, win, wmid, wout, wskip):
+        upper, lower = split_two(0.5 * acc[x])
+        values = dot_first(kout_ref[...], upper) + dot_first(kout_ref[...], lower)
+        latent = (values / cnt_ref[x]).astype(BF16)
+        skip_ref[x] = dot_first(wskip_ref[...], latent)
+        lat_ref[x] = latent.astype(F32)
+
+
+def encode(tab, blk, slot, cnt, kin, kmid, kout, wskip):
     vmem = pl.BlockSpec(memory_space=pltpu.VMEM)
+    v = pltpu.VMEM
     return pl.pallas_call(
         encode_kernel,
         out_shape=(
-            jax.ShapeDtypeStruct((CH, 8, 128), F32),
+            jax.ShapeDtypeStruct((8, CH, 128), F32),
             jax.ShapeDtypeStruct((8, CH, 128), F32),
         ),
-        in_specs=[vmem] * 11,
+        in_specs=[vmem] * 8,
         out_specs=(vmem, vmem),
-        scratch_shapes=[pltpu.VMEM((KH, 128), F32), pltpu.VMEM((8, CH, 128), F32)],
+        scratch_shapes=[
+            v((8, KH, 128), F32), v((8, KH, 128), F32),
+            v((PTS, 128), BF16), v((256, 128), BF16), v((KH, 256), BF16), v((KH, KH), BF16),
+            v((256, 1024), BF16), v((256, 1024), BF16), v((KH, 1024), BF16), v((KH, 1024), BF16),
+        ],
         name="encode",
-    )(tab, blk, slot, cnt, pre, ids, rowblk, win, wmid, wout, wskip)
+    )(tab, blk, slot, cnt, kin, kmid, kout, wskip)
 
 
 @functools.cache
@@ -212,7 +248,7 @@
 
 
 def layer_kernel(
-    lat_ref, skip_ref, w0_ref, w1_ref, fzh_ref, fzl_ref, fyh_ref, fyl_ref, fxh_ref, fxl_ref,
+    lat_ref, skip_ref, w_ref, fzh_ref, fzl_ref, fyh_ref, fyl_ref, fxh_ref, fxl_ref,
     ixh_ref, ixl_ref, iyh_ref, iyl_ref, izh_ref, mir_ref, flip_ref, out_ref,
     s1, r1, s2, r2, s3, r3, s4, r4, s5, r5, s6, r6, s7, r7, sv, rv, s8, r8, spec, grid, wide,
     send_sem, recv_sem,
@@ -238,7 +274,8 @@
     peers = plane + [along_y(d) for d in range(1, NY)]
     for peer in peers:
         pl.semaphore_signal(barrier, inc=1, device_id=peer, device_id_type=MESH_ID)
-    s1[...] = lat_ref[...].reshape(NZ, 64, 128).astype(BF16)
+    for q in range(NZ):
+        s1[q] = lat_ref[:, pl.ds(8 * q, 8), :].reshape(64, 128).astype(BF16)
     pl.semaphore_wait(barrier, len(peers))
 
     def send(n, source, target, peer):
@@ -275,7 +312,8 @@
     arrived(1, r2, NY - 1)
     upper, lower = split_two(jnp.concatenate([r2[q] for q in range(NY)], axis=1))
     flat = dot(upper, fyh_ref[...]) + dot(upper, fyl_ref[...]) + dot(lower, fyh_ref[...])
-    s3[...] = flat.reshape(NX, 8, 128)
+    for x in range(8):
+        s3[:, x, :] = flat[8 * x : 8 * x + 8]
     for d in range(1, NX):
         peer = along_x(d)
         send(2, s3.at[peer[0]], r3.at[gx], peer)
@@ -315,7 +353,7 @@
     big_row = lax.broadcasted_iota(jnp.int32, (32, 1024), 0)
     big_lane = lax.broadcasted_iota(jnp.int32, (32, 1024), 1)
     spread = jnp.where(big_lane // CH == big_row % MODES, spread, 0.0).astype(BF16)
-    by_real, by_imag = dot(spread, w0_ref[...]), dot(spread, w1_ref[...])
+    by_real, by_imag = dot(spread, w_ref[0:1024]), dot(spread, w_ref[1024:2048])
     mixed_real = by_real[0:16] - by_imag[16:32]
     mixed_imag = by_imag[0:16] + by_real[16:32]
     for i in range(2):
@@ -357,9 +395,9 @@
         send(5, s6.at[peer[0]], r6.at[gx], peer)
     r6[gx] = s6[gx]
     arrived(5, r6, NX - 1)
-    plain = r6[:, 0:8, :].reshape(64, 128).astype(BF16)
+    plain = jnp.concatenate([r6[:, x, :] for x in range(8)], axis=0).astype(BF16)
     flat = dot(plain, iyh_ref[...]) + dot(plain, iyl_ref[...])
-    own_power = r6[:, 8:16, :].reshape(64, 128)
+    own_power = jnp.concatenate([r6[:, 8, :]] * 8, axis=0)
     for q in range(NY):
         s7[q] = flat[:, q * 128 : (q + 1) * 128].astype(BF16)
     sv[...] = own_power
@@ -382,9 +420,9 @@
         send(8, s8.at[peer[2]], r8.at[gz], peer)
     r8[gz] = s8[gz]
     arrived(8, r8, NZ - 1)
-    wide[...] = r8[...].astype(F32).reshape(CH, 8, 128)
+    wide[...] = r8[...].astype(F32)
     for x in range(8):
-        out_ref[x] = gelu(wide[:, x, :] + skip_ref[x]).T
+        out_ref[x] = gelu(wide[:, pl.ds(8 * x, 8), :].reshape(CH, 128) + skip_ref[x]).T
     left(0, r1, NZ - 1)
     left(1, r2, NY - 1)
     left(2, r3, NX - 1)
@@ -396,7 +434,7 @@
     left(8, r8, NZ - 1)
 
 
-def layer(lat, skip, w0, w1):
+def layer(lat, skip, weights):
     fz, fy, fx, ix, iy, iz, mirror, flip = transform_tables()
     tables = [*two_tables(fz), *two_tables(fy), *two_tables(fx), *two_tables(ix), *two_tables(iy)]
     tables += [two_tables(iz)[0], two_tables(mirror)[0], two_tables(flip)[0]]
@@ -405,7 +443,7 @@
     return pl.pallas_call(
         layer_kernel,
         out_shape=jax.ShapeDtypeStruct((8, 128, CH), F32),
-        in_specs=[vmem] * (4 + len(tables)),
+        in_specs=[vmem] * (3 + len(tables)),
         out_specs=vmem,
         scratch_shapes=[
             v((NZ, 64, 128), BF16), v((NZ, 64, 128), BF16),
@@ -417,12 +455,12 @@
             v((NY, 64, 128), BF16), v((NY, 64, 128), BF16),
             v((64, 128), F32), v((NY, 64, 128), F32),
             v((NZ, 64, 128), BF16), v((NZ, 64, 128), BF16),
-            v((2, CH, 128), F32), v((MODES, 128), F32), v((CH, 8, 128), F32),
+            v((2, CH, 128), F32), v((MODES, 128), F32), v((NZ, 64, 128), F32),
             pltpu.SemaphoreType.DMA((9,)), pltpu.SemaphoreType.DMA((9,)),
         ],
         compiler_params=pltpu.CompilerParams(collective_id=1, has_side_effects=True),
         name="layer",
-    )(lat, skip, w0, w1, *tables)
+    )(lat, skip, weights, *tables)
 
 
 def body(point_data, neighbours, counts, kernel_in, kernel_mid, kernel_out, spectral, skip_weight):
@@ -433,28 +471,13 @@
     offset_z = owner % NZ - place[2] + 1
     offset_y = owner // NZ % NY - place[1] + 1
     offset_x = owner // (NZ * NY) - place[0] + 1
-    blk = ((offset_x * 3 + offset_y) * 3 + offset_z).astype(F32)
-    slot = (near % PTS - 256).astype(F32)
+    blk = ((offset_x * 3 + offset_y) * 3 + offset_z).astype(F32).reshape(CHUNKS, 8, 128)
+    slot = (near % PTS - 256).astype(F32).reshape(CHUNKS, 8, 128)
     cnt = counts.reshape(8, 1, 128).astype(F32)
-    wide_in = kernel_in.astype(F32)
-
-    def centre(start, count):
-        cells = start * count + jnp.arange(count, dtype=jnp.int32)
-        return (cells.astype(F32) + 0.5) / GRID
-
-    cx, cy, cz = centre(place[0], 8), centre(place[1], 16), centre(place[2], 8)
-    inner = (
-        wide_in[1][:, None, None] * cy[None, :, None] + wide_in[2][:, None, None] * cz[None, None, :]
-    ).reshape(KH, 128)
-    pre = -(inner[None] + (wide_in[0][None, :] * cx[:, None])[:, :, None])
-    nine = jnp.concatenate([kernel_in[0:3], kernel_in[0:3], kernel_in[3:6]], axis=0)
-    win = jnp.pad(jnp.concatenate([nine] * 27, axis=0), ((0, 13), (0, 0))).T
-    ids = jnp.broadcast_to((jnp.arange(PTS) - 256).astype(BF16)[:, None], (PTS, 128))
-    rowblk = jnp.broadcast_to((jnp.arange(256) // 9).astype(BF16)[:, None], (256, 128))
     lat, skip = encode(
-        tab, blk, slot, cnt, pre, ids, rowblk, win, kernel_mid.T, kernel_out.T, skip_weight.T
+        tab, blk, slot, cnt, kernel_in, kernel_mid, kernel_out, skip_weight
     )
-    out = layer(lat, skip, spectral[0].reshape(1024, CH), spectral[1].reshape(1024, CH))
+    out = layer(lat, skip, spectral.reshape(2048, CH))
     return out.reshape(1, 8, 16, 8, CH)
 
 

time: 146 us -> 98.4 us (0.67)
  Pallas kernels: 133 us -> 91.1 us
  local copies, waits for them, and re-layouts: 10.2 us -> 5.87 us
    pallas_call x1, Pallas kernels: 65.9 us -> 23.8 us  [encode(): pl.pallas_call(encode_kernel, out_shape=(jax.ShapeDtypeStruct((8, CH, 128...]
    broadcast_in_dim x2 -> x0, local copies, waits for them, and re-layouts: 1.53 us -> none  [the longest x1 0.79 us: body(): jnp.broadcast_to((jnp.arange(PTS) - 256).astype(BF16)[:, None], (PTS, 128))]
    unnamed x19 -> x9, local copies, waits for them, and re-layouts: 5.26 us -> 3.9 us
where the time goes in v2:
time: 98.4 us; the launch traced here: 98.1 us
  Pallas kernels  91.1 us (93%)
  local copies, waits for them, and re-layouts  5.87 us (6%)
  other arithmetic  1.08 us (1%)
    pallas_call x1, Pallas kernels, layer(): pl.pallas_call(layer_kernel, out_shape=jax.ShapeDtypeStruct((8, 128, CH),...  50 us
    pallas_call x1, Pallas kernels, encode(): pl.pallas_call(encode_kernel, out_shape=(jax.ShapeDtypeStruct((8, CH, 128...  23.8 us
    pallas_call x1, Pallas kernels, halo_table(): pl.pallas_call(halo_kernel, out_shape=jax.ShapeDtypeStruct((256, PTS), BF...  17.3 us
    unnamed x9, local copies, waits for them, and re-layouts  3.9 us

profile of v2, /device:TPU:1, one launch (start us, length us, event | category | flops | bytes accessed | tf_op | source)
XLA Modules:
  0.0 98.1 jit_solution(8052404529477580355)
XLA Ops:
  0.0 0.0 copy-start.2
  0.0 0.0 copy-start.1
  0.0 0.7 copy-done.2
  0.7 0.0 copy-start
  0.7 0.6 copy.31
  1.3 0.0 copy-done.1
  1.3 0.7 copy.28.kout_ref
  2.0 0.0 copy-done
  2.0 0.1 copy.26
  2.1 0.7 convert_element_type.14
  2.8 1.2 %copy.25 = s32[8,128,32]{1,2,0:T(8,128)S(1)} copy(s32[8,128,32]{2,1,0:T(8,128)} %bitcast.41) | data formatting | bytes 262144 | tf_op jit(solution)/shard_map/reshape | solution.py:469
  4.0 1.1 %fusion.14 = (f32[8,32,128]{2,1,0:T(8,128)}, f32[8,32,128]{2,1,0:T(8,128)}) fusion(s32[8,128,32]{1,2,0:T(8,128)S(1)} %copy.25, s32[]{:T(128)S(6)} %axis_index.38, s32[]{:T(128)S(6)} %axis_index.36, s32[]{:T(128)S(6)} %axis_index.33), kind=kLoop, calls=%fused_computation.30 | loop fusion | flops 2359296 | bytes 393228 | tf_op jit(solution)/shard_map/convert_element_type | solution.py:475
  5.1 17.3 %halo.1.tab_ref = bf16[256,512]{1,0:T(8,128)(2,1)} custom-call(f32[6,512]{1,0:T(8,128)} %bitcast.44), custom_call_target="tpu_custom_call" | custom-call | tf_op jit(solution)/shard_map/halo/pallas_call | solution.py:81
  22.4 23.8 %encode.1 = (f32[8,64,128]{2,1,0:T(8,128)}, f32[8,64,128]{2,1,0:T(8,128)}) custom-call(bf16[256,512]{1,0:T(8,128)(2,1)} %halo.1.tab_ref, f32[32,8,128]{2,1,0:T(8,128)} %bitcast.43, f32[32,8,128]{2,1,0:T(8,128)} %bitcast.42, f32[8,1,128]{2,1,0:T(1,128)} %bitcast.45, bf16[6,80]{1,0:T(8,128)(2,1)} %kin_ref.1, bf16[80,80]{1,0:T(8,128)(2,1)} %kmid_ref.1, ...), custom_call_target="tpu_custom_call" | custom-call | tf_op jit(solution)/shard_map/encode/pallas_call | solution.py:187
  46.2 50.0 %layer.1 = f32[8,128,64]{2,1,0:T(8,128)} custom-call(f32[8,64,128]{2,1,0:T(8,128)} %get-tuple-element.7.lat_ref, f32[8,64,128]{2,1,0:T(8,128)} %get-tuple-element.8.skip_ref, bf16[2048,64]{1,0:T(8,128)(2,1)} %bitcast.40, bf16[1024,512]{1,0:T(8,128)(2,1)} %constant.112.clone.fzh_ref, bf16[1024,512]{1,0:T(8,128)(2,1)} %constant.113.clone.fzl_ref, ...), custom_call_target="tpu_custom_call" | custom-call | tf_op jit(solution)/shard_map/layer/pallas_call | solution.py:443
  96.2 1.9 %copy.33 = f32[1,8,16,8,64]{4,3,2,1,0:T(8,128)} copy(f32[1,8,16,8,64]{4,3,2,1,0:T(8,128)} %bitcast.39) | data formatting | bytes 524288
  (1 shorter events, 0.0 us)
Async XLA Ops:
  0.0 0.7 copy-start.2
  0.0 1.3 %copy-start.1 = (bf16[80,64]{0,1:T(8,128)(2,1)S(1)}, bf16[80,64]{0,1:T(8,128)(2,1)}, u32[]{:S(2)}) copy-start(bf16[80,64]{0,1:T(8,128)(2,1)} %param.26) | copy-start | bytes 30724
  0.7 1.3 %copy-start = (s32[1,8,16,8]{2,3,1,0:T(8,128)S(1)}, s32[1,8,16,8]{2,3,1,0:T(8,128)}, u32[]{:S(2)}) copy-start(s32[1,8,16,8]{2,3,1,0:T(8,128)} %param.23) | copy-start | bytes 12292

commit v3 on v2

--- a/solution.py
+++ b/solution.py
@@ -212,31 +212,27 @@
 
     cos_c, sin_c = np.cos(angles(centred)), np.sin(angles(centred))
     cos_t, sin_t = np.cos(angles(third)), np.sin(angles(third))
-    eye_y, eye_k = np.eye(16), np.eye(4)
+    eye_k = np.eye(4)
     both = np.stack([cos_t, -sin_t], axis=-1)
-    fz = np.einsum(
-        "kqzr,yw->qyzkwr", both.reshape(MODES, NZ, 8, 2), eye_y
-    ).reshape(NZ, 16, 8, 4, 4, 16, 2)
-    fz = fz.transpose(0, 1, 2, 3, 5, 4, 6).reshape(1024, 512)
+    fz = np.broadcast_to(
+        both.reshape(4, 4, GRID, 2).transpose(2, 0, 1, 3)[:, :, None], (GRID, 4, 16, 4, 2)
+    ).reshape(GRID, 512)
     turn = np.stack([np.stack([cos_c, -sin_c], -1), np.stack([sin_c, cos_c], -1)], -2)
-    fy = np.einsum("jpyro,kl->pykrojl", turn.reshape(MODES, NY, 16, 2, 2), eye_k).reshape(512, 128)
-    fx = np.concatenate([cos_c, sin_c], axis=0)
-    ix = np.concatenate([cos_c.T, sin_c.T], axis=0)
+    fy = np.einsum("jcpyro,kl->pykrjocl", turn.reshape(8, 2, NY, 16, 2, 2), eye_k).reshape(512, 128)
+    first = np.stack([cos_c, sin_c]).reshape(2, 8, 2, NX, 8)
+    fx = np.broadcast_to(
+        first.transpose(3, 2, 1, 0, 4)[..., None], (NX, 2, 8, 2, 8, 8)
+    ).reshape(NX, 16, 128)
+    ix = np.broadcast_to(
+        first.transpose(3, 4, 0, 2, 1)[..., None], (NX, 8, 2, 2, 8, 8)
+    ).reshape(NX, 8, 256)
     back = np.stack([np.stack([cos_c, sin_c], -1), np.stack([-sin_c, cos_c], -1)], -2)
-    iy = np.einsum("jqyro,kl->rjkqylo", back.reshape(MODES, NY, 16, 2, 2), eye_k).reshape(128, 512)
+    iy = np.einsum("jcqyro,kl->jrckqylo", back.reshape(8, 2, NY, 16, 2, 2), eye_k).reshape(128, 512)
     weight = np.where(third == 0, 1.0, 2.0)[:, None, None] / GRID**3
-    iz = np.einsum(
-        "kqzr,yw->kyrqwz", (both * weight).reshape(MODES, NZ, 8, 2), eye_y
-    ).reshape(4, 4, 16, 2, NZ, 16, 8)
-    iz = iz.transpose(0, 2, 1, 3, 4, 5, 6).reshape(512, 1024)
-    mirror = np.zeros((MODES, MODES))
-    for i in range(MODES):
-        if i != MODES // 2:
-            mirror[i, (MODES - i) % MODES] = 1.0
-    flip = np.einsum(
-        "rs,ij,kl->riksjl", np.diag([1.0, -1.0]), mirror.T, np.diag([1.0, 0, 0, 0])
-    ).reshape(128, 128)
-    return fz, fy, fx, ix, iy, iz, mirror, flip
+    iz = np.broadcast_to(
+        (both * weight).transpose(0, 2, 1).reshape(32, NZ, 1, 8), (32, NZ, 16, 8)
+    ).reshape(32, 1024)
+    return fz, fy, fx, ix, iy, iz
 
 
 def two_tables(table):
@@ -247,17 +243,33 @@
     return jnp.asarray(upper), jnp.asarray(lower)
 
 
+def wide_table(table):
+    return jnp.asarray(np.ascontiguousarray(table, dtype=np.float32))
+
+
+def iota(shape, dim):
+    return lax.broadcasted_iota(jnp.int32, shape, dim)
+
+
+def block_swap(x):
+    row, lane = iota(x.shape, 0), iota(x.shape, 1) // 16
+    for bit in (1, 2, 4):
+        high, right = (row & bit) != 0, (lane & bit) != 0
+        down = pltpu.roll(pltpu.roll(x, bit, axis=0), 128 - 16 * bit, axis=1)
+        up = pltpu.roll(pltpu.roll(x, x.shape[0] - bit, axis=0), 16 * bit, axis=1)
+        x = jnp.where(high == right, x, jnp.where(high, down, up))
+    return x
+
+
 def layer_kernel(
-    lat_ref, skip_ref, w_ref, fzh_ref, fzl_ref, fyh_ref, fyl_ref, fxh_ref, fxl_ref,
-    ixh_ref, ixl_ref, iyh_ref, iyl_ref, izh_ref, mir_ref, flip_ref, out_ref,
-    s1, r1, s2, r2, s3, r3, s4, r4, s5, r5, s6, r6, s7, r7, sv, rv, s8, r8, spec, grid, wide,
+    lat_ref, skip_ref, w_ref, fzc_ref, fyh_ref, fyl_ref, fxc_ref, ixc_ref, iyh_ref, iyl_ref,
+    izc_ref, out_ref,
+    s1, r1, s2, r2, s4, r4, s5, r5, s7, r7, sv, rv, s8, r8, fzh, fzl, iz, grid, wide,
     send_sem, recv_sem,
 ):
     gx, gy, gz = lax.axis_index("gx"), lax.axis_index("gy"), lax.axis_index("gz")
+    me = gz * NX + gx
     barrier = pltpu.get_barrier_semaphore()
-
-    def along_x(d):
-        return (lax.rem(gx + d, NX), gy, gz)
 
     def along_y(d):
         return (gx, lax.rem(gy + d, NY), gz)
@@ -276,6 +288,36 @@
         pl.semaphore_signal(barrier, inc=1, device_id=peer, device_id_type=MESH_ID)
     for q in range(NZ):
         s1[q] = lat_ref[:, pl.ds(8 * q, 8), :].reshape(64, 128).astype(BF16)
+    own_y = iota((128, 512), 0) // 8 == iota((128, 512), 1) % 128 // 8
+    for q in range(NZ):
+        part = jnp.concatenate([fzc_ref[pl.ds(8 * q, 8), :]] * 16, axis=0)
+        upper, lower = split_two(jnp.where(own_y, part, 0.0))
+        fzh[pl.ds(128 * q, 128), :] = upper
+        fzl[pl.ds(128 * q, 128), :] = lower
+    own_y = iota((128, 1024), 0) // 8 == iota((128, 1024), 1) % 128 // 8
+    for q in range(NY):
+        part = jnp.concatenate([izc_ref[pl.ds(8 * q, 8), :]] * 16, axis=0)
+        iz[pl.ds(128 * q, 128), :] = jnp.where(own_y, part, 0.0).astype(BF16)
+    part = jnp.concatenate(
+        [jnp.broadcast_to(fxc_ref[gx, pl.ds(n, 1), :], (8, 128)) for n in range(16)], axis=0
+    )
+    row, lane = iota((128, 128), 0), iota((128, 128), 1)
+    fxh, fxl = split_two(jnp.where(row % 8 == lane % 8, part, 0.0))
+    part = jnp.concatenate(
+        [jnp.broadcast_to(ixc_ref[gx, pl.ds(n, 1), :], (8, 256)) for n in range(8)], axis=0
+    )
+    ixh, ixl = split_two(jnp.where(iota((64, 256), 0) % 8 == iota((64, 256), 1) % 8, part, 0.0))
+    row_i, lane_i = row // 8 % 8 * 2 + row // 64, lane // 8 % 8 * 2 + lane // 64
+    mirror = (row % 8 == lane % 8) & (row_i != 8) & (lane_i == (16 - row_i) % 16)
+    mirror = jnp.where(mirror, 1.0, 0.0).astype(BF16)
+    row_j, lane_j = row // 16 * 2 + row // 4 % 2, lane // 16 * 2 + lane // 4 % 2
+    flip = (row % 4 == 0) & (lane % 4 == 0) & (row // 8 % 2 == lane // 8 % 2)
+    flip = flip & (lane_j != 8) & (row_j == (16 - lane_j) % 16)
+    flip = jnp.where(flip, jnp.where(lane // 8 % 2 == 0, 1.0, -1.0), 0.0).astype(BF16)
+    pick = jnp.where(iota((16, 128), 1) % 16 == iota((16, 128), 0), 1.0, 0.0).astype(BF16)
+    gather = jnp.where(iota((8, 64), 1) // 8 == iota((8, 64), 0), 1.0, 0.0).astype(BF16)
+    own_channel = iota((64, 128), 0) % 8 == iota((64, 128), 1) // 16
+    own_mode = iota((32, 1024), 1) // CH == iota((32, 1024), 0) % MODES
     pl.semaphore_wait(barrier, len(peers))
 
     def send(n, source, target, peer):
@@ -301,8 +343,8 @@
         send(0, s1.at[peer[2]], r1.at[gz], peer)
     r1[gz] = s1[gz]
     arrived(0, r1, NZ - 1)
-    row = jnp.concatenate([r1[q] for q in range(NZ)], axis=1)
-    deep = dot(row, fzh_ref[...]) + dot(row, fzl_ref[...])
+    line = jnp.concatenate([r1[q] for q in range(NZ)], axis=1)
+    deep = dot(line, fzh[...]) + dot(line, fzl[...])
     for q in range(NY):
         s2[q] = deep[:, q * 128 : (q + 1) * 128]
     for d in range(1, NY):
@@ -312,32 +354,27 @@
     arrived(1, r2, NY - 1)
     upper, lower = split_two(jnp.concatenate([r2[q] for q in range(NY)], axis=1))
     flat = dot(upper, fyh_ref[...]) + dot(upper, fyl_ref[...]) + dot(lower, fyh_ref[...])
-    for x in range(8):
-        s3[:, x, :] = flat[8 * x : 8 * x + 8]
-    for d in range(1, NX):
-        peer = along_x(d)
-        send(2, s3.at[peer[0]], r3.at[gx], peer)
-    r3[gx] = s3[gx]
-    arrived(2, r3, NX - 1)
-    upper, lower = split_two(r3[...].reshape(GRID, 128))
-    both = dot(fxh_ref[...], upper) + dot(fxl_ref[...], upper) + dot(fxh_ref[...], lower)
-    lane = lax.broadcasted_iota(jnp.int32, (MODES, 128), 1)
-    turned = pltpu.roll(both[MODES:], 64, axis=1)
-    modes = both[:MODES] + jnp.where(lane < 64, turned, -turned)
+    real = iota((64, 128), 1) // 8 % 2 == 0
+    turned = jnp.where(real, pltpu.roll(flat, 120, axis=1), -pltpu.roll(flat, 8, axis=1))
+    upper, lower = split_two(jnp.concatenate([flat, turned], axis=0))
+    share = block_swap(dot(fxh, upper) + dot(fxl, upper) + dot(fxh, lower))
+    for i in range(2):
+        s4[:, i, :] = share[64 * i : 64 * i + 64]
+    for peer in plane:
+        send(2, s4.at[peer[2] * NX + peer[0]], r4.at[me], peer)
+    r4[me] = s4[me]
+    arrived(2, r4, 63)
     for q in range(NZ):
-        s4[q] = modes[2 * q : 2 * q + 2]
-    for peer in plane:
-        send(3, s4.at[peer[2]], r4.at[gz * NX + gx], peer)
-    r4[gz * NX + gx] = s4[gz]
-    arrived(3, r4, 63)
-    for c in range(CH):
-        for i in range(2):
-            spec[i, pl.ds(c, 1), :] = r4[c, pl.ds(i, 1), :]
-    srow = lax.broadcasted_iota(jnp.int32, (MODES, 128), 0)
-    pick = jnp.where(lane == (srow // 8) * 64 + gx * 8 + srow % 8, 1.0, 0.0).astype(BF16)
+        pair = r4[q * NX]
+        for n in range(1, NX):
+            pair = pair + r4[q * NX + n]
+        grid[pl.ds(2 * q, 2), :] = pair
     found = []
     for i in range(2):
-        values = spec[i].astype(BF16)
+        values = jnp.concatenate(
+            [jnp.broadcast_to(grid[pl.ds(2 * q + i, 1), :], (8, 128)) for q in range(NZ)], axis=0
+        )
+        values = jnp.where(own_channel, values, 0.0).astype(BF16)
         found.append(
             lax.dot_general(
                 pick,
@@ -349,10 +386,7 @@
     rows = jnp.concatenate(
         [found[0][0:8], found[1][0:8], found[0][8:16], found[1][8:16]], axis=0
     )
-    spread = jnp.concatenate([rows] * 8, axis=1)
-    big_row = lax.broadcasted_iota(jnp.int32, (32, 1024), 0)
-    big_lane = lax.broadcasted_iota(jnp.int32, (32, 1024), 1)
-    spread = jnp.where(big_lane // CH == big_row % MODES, spread, 0.0).astype(BF16)
+    spread = jnp.where(own_mode, jnp.concatenate([rows] * 8, axis=1), 0.0).astype(BF16)
     by_real, by_imag = dot(spread, w_ref[0:1024]), dot(spread, w_ref[1024:2048])
     mixed_real = by_real[0:16] - by_imag[16:32]
     mixed_imag = by_imag[0:16] + by_real[16:32]
@@ -360,84 +394,66 @@
         mine = jnp.concatenate(
             [mixed_real[8 * i : 8 * i + 8], mixed_imag[8 * i : 8 * i + 8]], axis=0
         ).astype(BF16)
-        placed = lax.dot_general(
-            mine, pick, (((0,), (0,)), ((), ())), preferred_element_type=F32
-        )
-        spec[i] = placed
-    for c in range(CH):
-        for i in range(2):
-            s5[c, pl.ds(i, 1), :] = spec[i, pl.ds(c, 1), :]
+        placed = jnp.where(own_channel, dot_first(mine, pick), 0.0).astype(BF16)
+        s5[:, i, :] = dot(gather, placed)
     for peer in plane:
-        send(4, s5.at[peer[2] * NX + peer[0]], r5.at[gz * NX + gx], peer)
-    r5[gz * NX + gx] = s5[gz * NX + gx]
-    arrived(4, r5, 63)
-    for q in range(NZ):
-        pair = r5[q * NX]
-        for n in range(1, NX):
-            pair = pair + r5[q * NX + n]
-        grid[pl.ds(2 * q, 2), :] = pair
-    is_mean = (srow == 0) & ((lane == 0) | (lane == 64)) & (gy == 0)
-    values = jnp.where(is_mean, 0.0, grid[...])
+        send(3, s5.at[peer[2]], r5.at[me], peer)
+    r5[me] = s5[gz]
+    arrived(3, r5, 63)
+    values = block_swap(jnp.concatenate([r5[:, i, :] for i in range(2)], axis=0))
+    is_mean = (row < 8) & ((lane == 0) | (lane == 8)) & (gy == 0)
+    values = jnp.where(is_mean, 0.0, values)
     exact = values.astype(BF16)
-    weight = jnp.where((lane % 4 == 0) & (gy == 0), 0.5, 2.0)
-    pairs = dot(dot(mir_ref[...], exact).astype(BF16), flip_ref[...])
-    pairs = jnp.where(gy == 0, 0.5 * pairs, 0.0)
-    power = values * (weight * values + pairs)
-    power = jnp.sum(jnp.sum(power, axis=1, keepdims=True), axis=0, keepdims=True)
-    both = dot(ixh_ref[...], exact) + dot(ixl_ref[...], exact)
-    lane = lax.broadcasted_iota(jnp.int32, (GRID, 128), 1)
-    turned = pltpu.roll(both[GRID:], 64, axis=1)
-    cells = both[:GRID] + jnp.where(lane < 64, -turned, turned)
-    s6[:, 0:8, :] = cells.reshape(NX, 8, 128)
-    s6[:, 8:16, :] = jnp.broadcast_to(power[None], (NX, 8, 128))
-    for d in range(1, NX):
-        peer = along_x(d)
-        send(5, s6.at[peer[0]], r6.at[gx], peer)
-    r6[gx] = s6[gx]
-    arrived(5, r6, NX - 1)
-    plain = jnp.concatenate([r6[:, x, :] for x in range(8)], axis=0).astype(BF16)
+    real = lane // 8 % 2 == 0
+    turned = jnp.where(real, -pltpu.roll(values, 120, axis=1), pltpu.roll(values, 8, axis=1))
+    stacked = jnp.concatenate([exact, turned.astype(BF16)], axis=0)
+    plain = (dot(ixh, stacked) + dot(ixl, stacked)).astype(BF16)
     flat = dot(plain, iyh_ref[...]) + dot(plain, iyl_ref[...])
-    own_power = jnp.concatenate([r6[:, 8, :]] * 8, axis=0)
     for q in range(NY):
         s7[q] = flat[:, q * 128 : (q + 1) * 128].astype(BF16)
-    sv[...] = own_power
-    rv[gy] = own_power
-    r7[gy] = s7[gy]
     for d in range(1, NY):
         peer = along_y(d)
-        send(6, s7.at[peer[1]], r7.at[gy], peer)
-        send(7, sv, rv.at[gy], peer)
-    arrived(6, r7, NY - 1)
-    row = jnp.concatenate([r7[q] for q in range(NY)], axis=1)
-    depth = dot(row, izh_ref[...])
-    arrived(7, rv, NY - 1)
+        send(4, s7.at[peer[1]], r7.at[gy], peer)
+    r7[gy] = s7[gy]
+    weight = jnp.where((lane % 4 == 0) & (gy == 0), 0.5, 2.0)
+    pairs = dot(dot(mirror, exact).astype(BF16), flip)
+    pairs = jnp.where(gy == 0, 0.5 * pairs, 0.0)
+    power = jnp.sum(values * (weight * values + pairs), axis=1, keepdims=True)
+    power = jnp.sum(power.reshape(16, 8, 1), axis=0)
+    sv[...] = jnp.broadcast_to(power, (8, 128))
+    for d in range(1, NY):
+        send(5, sv, rv.at[gy], along_y(d))
+    rv[gy] = sv[...]
+    arrived(4, r7, NY - 1)
+    line = jnp.concatenate([r7[q] for q in range(NY)], axis=1)
+    depth = dot(line, iz[...])
+    arrived(5, rv, NY - 1)
     power = (rv[0] + rv[1]) + (rv[2] + rv[3])
     scale = 1.0 / jnp.sqrt(power * (1.0 / float(GRID) ** 6) + 1.0)
+    scale = jnp.concatenate([scale] * 8, axis=0)
     for q in range(NZ):
         s8[q] = (depth[:, q * 128 : (q + 1) * 128] * scale).astype(BF16)
     for d in range(1, NZ):
         peer = along_z(d)
-        send(8, s8.at[peer[2]], r8.at[gz], peer)
+        send(6, s8.at[peer[2]], r8.at[gz], peer)
     r8[gz] = s8[gz]
-    arrived(8, r8, NZ - 1)
+    arrived(6, r8, NZ - 1)
     wide[...] = r8[...].astype(F32)
     for x in range(8):
         out_ref[x] = gelu(wide[:, pl.ds(8 * x, 8), :].reshape(CH, 128) + skip_ref[x]).T
     left(0, r1, NZ - 1)
     left(1, r2, NY - 1)
-    left(2, r3, NX - 1)
-    left(3, r4, 63)
-    left(4, r5, 63)
-    left(5, r6, NX - 1)
-    left(6, r7, NY - 1)
-    left(7, rv, NY - 1)
-    left(8, r8, NZ - 1)
+    left(2, r4, 63)
+    left(3, r5, 63)
+    left(4, r7, NY - 1)
+    left(5, rv, NY - 1)
+    left(6, r8, NZ - 1)
 
 
 def layer(lat, skip, weights):
-    fz, fy, fx, ix, iy, iz, mirror, flip = transform_tables()
-    tables = [*two_tables(fz), *two_tables(fy), *two_tables(fx), *two_tables(ix), *two_tables(iy)]
-    tables += [two_tables(iz)[0], two_tables(mirror)[0], two_tables(flip)[0]]
+    fz, fy, fx, ix, iy, iz = transform_tables()
+    tables = [wide_table(fz), *two_tables(fy), wide_table(fx), wide_table(ix)]
+    tables += [*two_tables(iy), wide_table(iz)]
     vmem = pl.BlockSpec(memory_space=pltpu.VMEM)
     v = pltpu.VMEM
     return pl.pallas_call(
@@ -448,15 +464,14 @@
         scratch_shapes=[
             v((NZ, 64, 128), BF16), v((NZ, 64, 128), BF16),
             v((NY, 64, 128), F32), v((NY, 64, 128), F32),
-            v((NX, 8, 128), F32), v((NX, 8, 128), F32),
+            v((CH, 2, 128), F32), v((CH, 2, 128), F32),
             v((NZ, 2, 128), F32), v((CH, 2, 128), F32),
-            v((CH, 2, 128), F32), v((CH, 2, 128), F32),
-            v((NX, 16, 128), F32), v((NX, 16, 128), F32),
             v((NY, 64, 128), BF16), v((NY, 64, 128), BF16),
-            v((64, 128), F32), v((NY, 64, 128), F32),
+            v((8, 128), F32), v((NY, 8, 128), F32),
             v((NZ, 64, 128), BF16), v((NZ, 64, 128), BF16),
-            v((2, CH, 128), F32), v((MODES, 128), F32), v((NZ, 64, 128), F32),
-            pltpu.SemaphoreType.DMA((9,)), pltpu.SemaphoreType.DMA((9,)),
+            v((1024, 512), BF16), v((1024, 512), BF16), v((512, 1024), BF16),
+            v((MODES, 128), F32), v((NZ, 64, 128), F32),
+            pltpu.SemaphoreType.DMA((7,)), pltpu.SemaphoreType.DMA((7,)),
         ],
         compiler_params=pltpu.CompilerParams(collective_id=1, has_side_effects=True),
         name="layer",

time: 98.4 us -> 87.7 us (0.89)
  Pallas kernels: 91.1 us -> 80.4 us
    pallas_call x1, Pallas kernels: 50 us -> 39.3 us  [layer(): pl.pallas_call(layer_kernel, out_shape=jax.ShapeDtypeStruct((8, 128, CH),...]
where the time goes in v3:
time: 87.7 us; the launch traced here: 87.4 us
  Pallas kernels  80.4 us (92%)
  local copies, waits for them, and re-layouts  5.87 us (7%)
  other arithmetic  1.08 us (1%)
    pallas_call x1, Pallas kernels, layer(): pl.pallas_call(layer_kernel, out_shape=jax.ShapeDtypeStruct((8, 128, CH),...  39.3 us
    pallas_call x1, Pallas kernels, encode(): pl.pallas_call(encode_kernel, out_shape=(jax.ShapeDtypeStruct((8, CH, 128...  23.8 us
    pallas_call x1, Pallas kernels, halo_table(): pl.pallas_call(halo_kernel, out_shape=jax.ShapeDtypeStruct((256, PTS), BF...  17.3 us
    unnamed x9, local copies, waits for them, and re-layouts  3.9 us

profile of v3, /device:TPU:1, one launch (start us, length us, event | category | flops | bytes accessed | tf_op | source)
XLA Modules:
  0.0 87.4 jit_solution(17743472498180246308)
XLA Ops:
  0.0 0.0 copy-start.2
  0.0 0.0 copy-start.1
  0.0 0.7 copy-done.2
  0.7 0.0 copy-start
  0.7 0.6 copy.26
  1.3 0.0 copy-done.1
  1.3 0.7 copy.23.kout_ref
  2.0 0.0 copy-done
  2.0 0.1 copy.21
  2.1 0.7 convert_element_type.14
  2.8 1.2 %copy.20 = s32[8,128,32]{1,2,0:T(8,128)S(1)} copy(s32[8,128,32]{2,1,0:T(8,128)} %bitcast.41) | data formatting | bytes 262144 | tf_op jit(solution)/shard_map/reshape | solution.py:484
  4.0 1.1 %fusion.14 = (f32[8,32,128]{2,1,0:T(8,128)}, f32[8,32,128]{2,1,0:T(8,128)}) fusion(s32[8,128,32]{1,2,0:T(8,128)S(1)} %copy.20, s32[]{:T(128)S(6)} %axis_index.38, s32[]{:T(128)S(6)} %axis_index.36, s32[]{:T(128)S(6)} %axis_index.33), kind=kLoop, calls=%fused_computation.30 | loop fusion | flops 2359296 | bytes 393228 | tf_op jit(solution)/shard_map/convert_element_type | solution.py:490
  5.1 17.3 %halo.1.tab_ref = bf16[256,512]{1,0:T(8,128)(2,1)} custom-call(f32[6,512]{1,0:T(8,128)} %bitcast.44), custom_call_target="tpu_custom_call" | custom-call | tf_op jit(solution)/shard_map/halo/pallas_call | solution.py:81
  22.4 23.8 %encode.1 = (f32[8,64,128]{2,1,0:T(8,128)}, f32[8,64,128]{2,1,0:T(8,128)}) custom-call(bf16[256,512]{1,0:T(8,128)(2,1)} %halo.1.tab_ref, f32[32,8,128]{2,1,0:T(8,128)} %bitcast.43, f32[32,8,128]{2,1,0:T(8,128)} %bitcast.42, f32[8,1,128]{2,1,0:T(1,128)} %bitcast.45, bf16[6,80]{1,0:T(8,128)(2,1)} %kin_ref.1, bf16[80,80]{1,0:T(8,128)(2,1)} %kmid_ref.1, ...), custom_call_target="tpu_custom_call" | custom-call | tf_op jit(solution)/shard_map/encode/pallas_call | solution.py:187
  46.2 39.3 %layer.1 = f32[8,128,64]{2,1,0:T(8,128)} custom-call(f32[8,64,128]{2,1,0:T(8,128)} %get-tuple-element.7.lat_ref, f32[8,64,128]{2,1,0:T(8,128)} %get-tuple-element.8.skip_ref, bf16[2048,64]{1,0:T(8,128)(2,1)} %bitcast.40, f32[64,512]{1,0:T(8,128)} %constant.102.clone.fzc_ref, bf16[512,128]{1,0:T(8,128)(2,1)} %constant.103.clone.fyh_ref, ...), custom_call_target="tpu_custom_call" | custom-call | tf_op jit(solution)/shard_map/layer/pallas_call | solution.py:459
  85.5 1.9 %copy.28 = f32[1,8,16,8,64]{4,3,2,1,0:T(8,128)} copy(f32[1,8,16,8,64]{4,3,2,1,0:T(8,128)} %bitcast.39) | data formatting | bytes 524288
  (1 shorter events, 0.0 us)
Async XLA Ops:
  0.0 0.7 copy-start.2
  0.0 1.3 %copy-start.1 = (bf16[80,64]{0,1:T(8,128)(2,1)S(1)}, bf16[80,64]{0,1:T(8,128)(2,1)}, u32[]{:S(2)}) copy-start(bf16[80,64]{0,1:T(8,128)(2,1)} %param.21) | copy-start | bytes 30724
  0.7 1.3 %copy-start = (s32[1,8,16,8]{2,3,1,0:T(8,128)S(1)}, s32[1,8,16,8]{2,3,1,0:T(8,128)}, u32[]{:S(2)}) copy-start(s32[1,8,16,8]{2,3,1,0:T(8,128)} %param.18) | copy-start | bytes 12292

commit v4 on v3

v4 whole, which is shorter than its diff:
```python
import functools
import math

import jax
import jax.numpy as jnp
import numpy as np
from jax import lax
from jax.experimental import pallas as pl
from jax.experimental.pallas import tpu as pltpu
from jax.sharding import PartitionSpec as P

GRID = 64
MODES = 16
NB = 32
KH = 80
CH = 64
PTS = 512
NX, NY, NZ = 8, 4, 8
F32 = jnp.float32
BF16 = jnp.bfloat16
MESH_ID = pl.DeviceIdType.MESH


def dot(a, b):
    return jnp.dot(a, b, preferred_element_type=F32)


def gelu(v):
    inner = v * (0.7978845608028654 + 0.035677408136300125 * (v * v))
    half = 0.5 * v
    return half + half * jnp.tanh(inner)


def split_two(values):
    upper = values.astype(BF16)
    return upper, (values - upper.astype(F32)).astype(BF16)


def dot_first(a, b):
    return lax.dot_general(a, b, (((0,), (0,)), ((), ())), preferred_element_type=F32)


def twice_gelu(v):
    inner = v * (0.7978845608028654 + 0.035677408136300125 * (v * v))
    return v + v * jnp.tanh(inner)


CHUNKS = 32
PART = 256


@functools.cache
def transform_tables():
    m = np.arange(GRID)
    centred = np.where(np.arange(MODES) < MODES // 2, np.arange(MODES), np.arange(MODES) - MODES)
    third = np.arange(MODES)

    def angles(f):
        return 2.0 * np.pi * ((f[:, None] * m[None, :]) % GRID) / GRID

    cos_c, sin_c = np.cos(angles(centred)), np.sin(angles(centred))
    cos_t, sin_t = np.cos(angles(third)), np.sin(angles(third))
    eye_k = np.eye(4)
    both = np.stack([cos_t, -sin_t], axis=-1)
    fz = np.broadcast_to(
        both.reshape(4, 4, GRID, 2).transpose(2, 0, 1, 3)[:, :, None], (GRID, 4, 16, 4, 2)
    ).reshape(GRID, 512)
    turn = np.stack([np.stack([cos_c, -sin_c], -1), np.stack([sin_c, cos_c], -1)], -2)
    fy = np.einsum("jcpyro,kl->pykrjocl", turn.reshape(8, 2, NY, 16, 2, 2), eye_k).reshape(512, 128)
    first = np.stack([cos_c, sin_c]).reshape(2, 8, 2, NX, 8)
    fx = np.broadcast_to(
        first.transpose(3, 2, 1, 0, 4)[..., None], (NX, 2, 8, 2, 8, 8)
    ).reshape(NX, 16, 128)
    ix = np.broadcast_to(
        first.transpose(3, 4, 0, 2, 1)[..., None], (NX, 8, 2, 2, 8, 8)
    ).reshape(NX, 8, 256)
    back = np.stack([np.stack([cos_c, sin_c], -1), np.stack([-sin_c, cos_c], -1)], -2)
    iy = np.einsum("jcqyro,kl->jrckqylo", back.reshape(8, 2, NY, 16, 2, 2), eye_k).reshape(128, 512)
    weight = np.where(third == 0, 1.0, 2.0)[:, None, None] / GRID**3
    iz = np.broadcast_to(
        (both * weight).transpose(0, 2, 1).reshape(32, NZ, 1, 8), (32, NZ, 16, 8)
    ).reshape(32, 1024)
    return fz, fy, fx, ix, iy, iz


def two_tables(table):
    import ml_dtypes

    upper = table.astype(np.float32).astype(ml_dtypes.bfloat16)
    lower = (table - upper.astype(np.float64)).astype(np.float32).astype(ml_dtypes.bfloat16)
    return jnp.asarray(upper), jnp.asarray(lower)


def wide_table(table):
    return jnp.asarray(np.ascontiguousarray(table, dtype=np.float32))


def iota(shape, dim):
    return lax.broadcasted_iota(jnp.int32, shape, dim)


def block_swap(x):
    row, lane = iota(x.shape, 0), iota(x.shape, 1) // 16
    for bit in (1, 2, 4):
        high, right = (row & bit) != 0, (lane & bit) != 0
        down = pltpu.roll(pltpu.roll(x, bit, axis=0), 128 - 16 * bit, axis=1)
        up = pltpu.roll(pltpu.roll(x, x.shape[0] - bit, axis=0), 16 * bit, axis=1)
        x = jnp.where(high == right, x, jnp.where(high, down, up))
    return x


def whole_kernel(
    pts_ref, cnt_ref, kin_ref, kmid_ref, kout_ref, wskip_ref,
    near_hbm, w_hbm, fzc_hbm, fyh_hbm, fyl_hbm, fxc_hbm, ixc_hbm, iyh_hbm, iyl_hbm, izc_hbm,
    out_ref,
    near, w_ref, fzc_ref, fyh_ref, fyl_ref, fxc_ref, ixc_ref, iyh_ref, iyl_ref, izc_ref,
    around, table_rows, tab, slot_ids, block_ids, valid_slots, pre, ids, rowblk, win, wmid,
    masked_a, masked_b, hid_a, hid_b, acc, lat_ref, skip_ref, fxh, fxl, ixh, ixl,
    s1, r1, s2, r2, s4, r4, s5, r5, s7, r7, sv, rv, s8, r8, fzh, fzl, iz, grid, wide,
    send_sem, recv_sem, in_sem,
):
    gx, gy, gz = lax.axis_index("gx"), lax.axis_index("gy"), lax.axis_index("gz")
    me = gz * NX + gx
    barrier = pltpu.get_barrier_semaphore()
    fetched = [
        (near_hbm, near), (fzc_hbm, fzc_ref), (fxc_hbm.at[gx], fxc_ref), (ixc_hbm.at[gx], ixc_ref),
        (izc_hbm, izc_ref), (fyh_hbm, fyh_ref), (fyl_hbm, fyl_ref), (iyh_hbm, iyh_ref),
        (iyl_hbm, iyl_ref), (w_hbm, w_ref),
    ]

    def fetch(n):
        return pltpu.make_async_copy(fetched[n][0], fetched[n][1], in_sem.at[n])

    for n in range(len(fetched)):
        fetch(n).start()

    def along_y(d):
        return (gx, lax.rem(gy + d, NY), gz)

    def along_z(d):
        return (gx, gy, lax.rem(gz + d, NZ))

    def beside(step):
        return tuple(lax.rem(p + d + n, n) for p, d, n in zip((gx, gy, gz), step, (NX, NY, NZ)))

    plane = [
        (lax.rem(gx + dx, NX), gy, lax.rem(gz + dz, NZ))
        for dx in range(NX)
        for dz in range(NZ)
        if (dx, dz) != (0, 0)
    ]
    steps = [
        (dx, dy, dz)
        for dx in (-1, 0, 1)
        for dy in (-1, 0, 1)
        for dz in (-1, 0, 1)
        if (dx, dy, dz) != (0, 0, 0)
    ]
    apart = [beside(s) for s in steps if s[1] != 0 and (s[0], s[2]) != (0, 0)]
    peers = plane + [along_y(d) for d in range(1, NY)] + apart
    for peer in peers:
        pl.semaphore_signal(barrier, inc=1, device_id=peer, device_id_type=MESH_ID)

    ids[...] = (iota((PTS, 128), 0) - 256).astype(F32).astype(BF16)
    rowblk[...] = (iota((256, 128), 0) // 9).astype(F32).astype(BF16)
    col = iota((6, 256), 1)
    nine = col % 9
    source = jnp.where(nine < 3, nine, nine - 3)
    chosen = jnp.where((source == iota((6, 256), 0)) & (col < 243), 1.0, 0.0).astype(BF16)
    win[...] = dot_first(kin_ref[...], chosen).astype(BF16)
    eye = jnp.where(iota((KH, KH), 0) == iota((KH, KH), 1), 0.5, 0.0).astype(BF16)
    wmid[...] = dot_first(kmid_ref[...], eye).astype(BF16)
    row, lane = iota((6, 128), 0), iota((6, 128), 1)
    index_y, index_z = gy * 16 + lane // 8, gz * 8 + lane % 8
    for x in range(8):
        index = jnp.where(row == 0, gx * 8 + x, jnp.where(row == 1, index_y, index_z))
        centre = jnp.where(row < 3, -(index.astype(F32) + 0.5) / GRID, 0.0).astype(BF16)
        pre[x] = dot_first(kin_ref[...], centre)
    by_row = jnp.where(iota((16, 128), 1) // 8 == iota((16, 128), 0), 1.0, 0.0).astype(BF16)
    spread = dot(cnt_ref[...].astype(F32).astype(BF16), by_row)
    spread = jnp.where(iota((64, 128), 0) % 8 == iota((64, 128), 1) % 8, spread, 0.0)
    gather = jnp.where(iota((8, 64), 1) // 8 == iota((8, 64), 0), 1.0, 0.0).astype(BF16)
    spread = dot(gather, spread.astype(BF16))
    for x in range(8):
        valid_slots[x] = jnp.broadcast_to(spread[x : x + 1], (8, 128))
    acc[...] = jnp.zeros((8, KH, 128), F32)
    table_rows[pl.ds(240, 16), :] = jnp.zeros((16, PTS), F32)
    fetch(0).wait()
    for x in range(8):
        point = near[x].T
        owner = point >> 9
        offset_z = (owner & 7) - gz + 1
        offset_y = ((owner >> 3) & 3) - gy + 1
        offset_x = (owner >> 5) - gx + 1
        block = ((offset_x * 3 + offset_y) * 3 + offset_z).astype(F32)
        block_ids[pl.ds(4 * x, 4)] = block.reshape(4, 8, 128)
        slot_ids[pl.ds(4 * x, 4)] = ((point & 511) - 256).astype(F32).reshape(4, 8, 128)
    pl.semaphore_wait(barrier, len(peers))

    def send(n, source, target, peer):
        pltpu.make_async_remote_copy(
            src_ref=source,
            dst_ref=target,
            send_sem=send_sem.at[n],
            recv_sem=recv_sem.at[n],
            device_id=peer,
            device_id_type=MESH_ID,
        ).start()

    def arrived(n, buffer, count):
        part = buffer.at[pl.ds(0, count)]
        pltpu.make_async_copy(part, part, recv_sem.at[n]).wait()

    def left(n, buffer, count):
        part = buffer.at[pl.ds(0, count)]
        pltpu.make_async_copy(part, part, send_sem.at[n]).wait()

    for step in steps:
        block = ((1 - step[0]) * 3 + (1 - step[1])) * 3 + (1 - step[2])
        send(7, pts_ref, around.at[block], beside(step))
    around[13] = pts_ref[...]
    for n in range(1, 5):
        fetch(n).wait()
    own_y = iota((128, 512), 0) // 8 == iota((128, 512), 1) % 128 // 8
    for q in range(NZ):
        part = jnp.concatenate([fzc_ref[pl.ds(8 * q, 8), :]] * 16, axis=0)
        upper, lower = split_two(jnp.where(own_y, part, 0.0))
        fzh[pl.ds(128 * q, 128), :] = upper
        fzl[pl.ds(128 * q, 128), :] = lower
    own_y = iota((128, 1024), 0) // 8 == iota((128, 1024), 1) % 128 // 8
    for q in range(NY):
        part = jnp.concatenate([izc_ref[pl.ds(8 * q, 8), :]] * 16, axis=0)
        iz[pl.ds(128 * q, 128), :] = jnp.where(own_y, part, 0.0).astype(BF16)
    part = jnp.concatenate(
        [jnp.broadcast_to(fxc_ref[pl.ds(n, 1), :], (8, 128)) for n in range(16)], axis=0
    )
    row, lane = iota((128, 128), 0), iota((128, 128), 1)
    fxh[...], fxl[...] = split_two(jnp.where(row % 8 == lane % 8, part, 0.0))
    part = jnp.concatenate(
        [jnp.broadcast_to(ixc_ref[pl.ds(n, 1), :], (8, 256)) for n in range(8)], axis=0
    )
    ixh[...], ixl[...] = split_two(jnp.where(iota((64, 256), 0) % 8 == iota((64, 256), 1) % 8, part, 0.0))
    arrived(7, around, 26)
    for b in range(27):
        for t in range(4):
            block = around[b, pl.ds(t, 6, stride=4), :]
            place = block[0:3]
            upper = place.astype(BF16).astype(F32)
            table_rows[pl.ds(9 * b, 9), pl.ds(128 * t, 128)] = jnp.concatenate(
                [upper, place - upper, block[3:6]], axis=0
            )
    tab[...] = table_rows[...].astype(BF16)
    one = jnp.ones((PTS, 128), BF16)
    none = jnp.zeros((PTS, 128), BF16)

    def step(t, masked_out, masked_in, hid_out, hid_in):
        early = jnp.minimum(t, CHUNKS - 1)
        middle = jnp.clip(t - 1, 0, CHUNKS - 1)
        late = jnp.maximum(t - 2, 0)
        slots, blocks = slot_ids[early], block_ids[early]
        base = jnp.concatenate([pre[middle // 4]] * 2, axis=1)
        valid = jnp.where(t >= 2, valid_slots[late // 4], 0.0)[0:1]
        first = (late % 4 * 8).astype(F32)
        total = jnp.zeros((KH, 128), F32)
        for part in range(4):
            span = pl.ds(part * PART, PART)
            hot = []
            for s in (2 * part, 2 * part + 1):
                chosen = jnp.broadcast_to(slots[s : s + 1], (PTS, 128)).astype(BF16)
                hot.append(jnp.where(ids[...] == chosen, one, none))
            found = dot(tab[...], jnp.concatenate(hot, axis=1))
            ahead = dot(win[...], masked_in[:, span])
            last = dot(wmid[...], hid_in[:, span])
            hid_out[:, span] = twice_gelu(ahead + base).astype(BF16)
            last = twice_gelu(last).astype(BF16).astype(F32)
            for n in range(2):
                used = valid > first + (2 * part + n)
                total = total + jnp.where(used, last[:, n * 128 : (n + 1) * 128], 0.0)
            found = found.astype(BF16)
            for n in range(2):
                s = 2 * part + n
                chosen = jnp.broadcast_to(blocks[s : s + 1], (256, 128)).astype(BF16)
                masked_out[:, pl.ds(s * 128, 128)] = jnp.where(
                    rowblk[...] == chosen, found[:, n * 128 : (n + 1) * 128], none[0:256]
                )
        acc[late // 4] += total

    for unset in (masked_a, masked_b):
        unset[...] = jnp.zeros((256, 1024), BF16)
    for unset in (hid_a, hid_b):
        unset[...] = jnp.zeros((KH, 1024), BF16)

    def two_steps(tt, carry):
        step(2 * tt, masked_a, masked_b, hid_a, hid_b)
        step(2 * tt + 1, masked_b, masked_a, hid_b, hid_a)
        return carry

    lax.fori_loop(0, CHUNKS // 2 + 1, two_steps, 0)
    for x in range(8):
        upper, lower = split_two(0.5 * acc[x])
        values = dot(kout_ref[...], upper) + dot(kout_ref[...], lower)
        latent = (values / valid_slots[x, 0:1]).astype(BF16)
        skip_ref[x] = dot_first(wskip_ref[...], latent)
        lat_ref[x] = latent.astype(F32)
    for q in range(NZ):
        s1[q] = lat_ref[:, pl.ds(8 * q, 8), :].reshape(64, 128).astype(BF16)
    for d in range(1, NZ):
        peer = along_z(d)
        send(0, s1.at[peer[2]], r1.at[gz], peer)
    r1[gz] = s1[gz]
    row, lane = iota((128, 128), 0), iota((128, 128), 1)
    row_i, lane_i = row // 8 % 8 * 2 + row // 64, lane // 8 % 8 * 2 + lane // 64
    mirror = (row % 8 == lane % 8) & (row_i != 8) & (lane_i == (16 - row_i) % 16)
    mirror = jnp.where(mirror, 1.0, 0.0).astype(BF16)
    row_j, lane_j = row // 16 * 2 + row // 4 % 2, lane // 16 * 2 + lane // 4 % 2
    flip = (row % 4 == 0) & (lane % 4 == 0) & (row // 8 % 2 == lane // 8 % 2)
    flip = flip & (lane_j != 8) & (row_j == (16 - lane_j) % 16)
    flip = jnp.where(flip, jnp.where(lane // 8 % 2 == 0, 1.0, -1.0), 0.0).astype(BF16)
    pick = jnp.where(iota((16, 128), 1) % 16 == iota((16, 128), 0), 1.0, 0.0).astype(BF16)
    own_channel = iota((64, 128), 0) % 8 == iota((64, 128), 1) // 16
    own_mode = iota((32, 1024), 1) // CH == iota((32, 1024), 0) % MODES
    for n in range(5, 10):
        fetch(n).wait()
    arrived(0, r1, NZ - 1)
    line = jnp.concatenate([r1[q] for q in range(NZ)], axis=1)
    deep = dot(line, fzh[...]) + dot(line, fzl[...])
    for q in range(NY):
        s2[q] = deep[:, q * 128 : (q + 1) * 128]
    for d in range(1, NY):
        peer = along_y(d)
        send(1, s2.at[peer[1]], r2.at[gy], peer)
    r2[gy] = s2[gy]
    arrived(1, r2, NY - 1)
    upper, lower = split_two(jnp.concatenate([r2[q] for q in range(NY)], axis=1))
    flat = dot(upper, fyh_ref[...]) + dot(upper, fyl_ref[...]) + dot(lower, fyh_ref[...])
    real = iota((64, 128), 1) // 8 % 2 == 0
    turned = jnp.where(real, pltpu.roll(flat, 120, axis=1), -pltpu.roll(flat, 8, axis=1))
    upper, lower = split_two(jnp.concatenate([flat, turned], axis=0))
    share = block_swap(dot(fxh[...], upper) + dot(fxl[...], upper) + dot(fxh[...], lower))
    for i in range(2):
        s4[:, i, :] = share[64 * i : 64 * i + 64]
    for peer in plane:
        send(2, s4.at[peer[2] * NX + peer[0]], r4.at[me], peer)
    r4[me] = s4[me]
    arrived(2, r4, 63)
    for q in range(NZ):
        pair = r4[q * NX]
        for n in range(1, NX):
            pair = pair + r4[q * NX + n]
        grid[pl.ds(2 * q, 2), :] = pair
    found = []
    for i in range(2):
        values = jnp.concatenate(
            [jnp.broadcast_to(grid[pl.ds(2 * q + i, 1), :], (8, 128)) for q in range(NZ)], axis=0
        )
        values = jnp.where(own_channel, values, 0.0).astype(BF16)
        found.append(
            lax.dot_general(
                pick,
                jnp.concatenate([values, values], axis=0),
                (((1,), (1,)), ((), ())),
                preferred_element_type=F32,
            )
        )
    rows = jnp.concatenate(
        [found[0][0:8], found[1][0:8], found[0][8:16], found[1][8:16]], axis=0
    )
    spread = jnp.where(own_mode, jnp.concatenate([rows] * 8, axis=1), 0.0).astype(BF16)
    by_real, by_imag = dot(spread, w_ref[0:1024]), dot(spread, w_ref[1024:2048])
    mixed_real = by_real[0:16] - by_imag[16:32]
    mixed_imag = by_imag[0:16] + by_real[16:32]
    for i in range(2):
        mine = jnp.concatenate(
            [mixed_real[8 * i : 8 * i + 8], mixed_imag[8 * i : 8 * i + 8]], axis=0
        ).astype(BF16)
        placed = jnp.where(own_channel, dot_first(mine, pick), 0.0).astype(BF16)
        s5[:, i, :] = dot(gather, placed)
    for peer in plane:
        send(3, s5.at[peer[2]], r5.at[me], peer)
    r5[me] = s5[gz]
    arrived(3, r5, 63)
    values = block_swap(jnp.concatenate([r5[:, i, :] for i in range(2)], axis=0))
    is_mean = (row < 8) & ((lane == 0) | (lane == 8)) & (gy == 0)
    values = jnp.where(is_mean, 0.0, values)
    exact = values.astype(BF16)
    real = lane // 8 % 2 == 0
    turned = jnp.where(real, -pltpu.roll(values, 120, axis=1), pltpu.roll(values, 8, axis=1))
    stacked = jnp.concatenate([exact, turned.astype(BF16)], axis=0)
    plain = (dot(ixh[...], stacked) + dot(ixl[...], stacked)).astype(BF16)
    flat = dot(plain, iyh_ref[...]) + dot(plain, iyl_ref[...])
    for q in range(NY):
        s7[q] = flat[:, q * 128 : (q + 1) * 128].astype(BF16)
    for d in range(1, NY):
        peer = along_y(d)
        send(4, s7.at[peer[1]], r7.at[gy], peer)
    r7[gy] = s7[gy]
    weight = jnp.where((lane % 4 == 0) & (gy == 0), 0.5, 2.0)
    pairs = dot(dot(mirror, exact).astype(BF16), flip)
    pairs = jnp.where(gy == 0, 0.5 * pairs, 0.0)
    power = jnp.sum(values * (weight * values + pairs), axis=1, keepdims=True)
    power = jnp.sum(power.reshape(16, 8, 1), axis=0)
    sv[...] = jnp.broadcast_to(power, (8, 128))
    for d in range(1, NY):
        send(5, sv, rv.at[gy], along_y(d))
    rv[gy] = sv[...]
    arrived(4, r7, NY - 1)
    line = jnp.concatenate([r7[q] for q in range(NY)], axis=1)
    depth = dot(line, iz[...])
    arrived(5, rv, NY - 1)
    power = (rv[0] + rv[1]) + (rv[2] + rv[3])
    scale = 1.0 / jnp.sqrt(power * (1.0 / float(GRID) ** 6) + 1.0)
    scale = jnp.concatenate([scale] * 8, axis=0)
    for q in range(NZ):
        s8[q] = (depth[:, q * 128 : (q + 1) * 128] * scale).astype(BF16)
    for d in range(1, NZ):
        peer = along_z(d)
        send(6, s8.at[peer[2]], r8.at[gz], peer)
    r8[gz] = s8[gz]
    arrived(6, r8, NZ - 1)
    wide[...] = r8[...].astype(F32)
    for x in range(8):
        out_ref[x] = gelu(wide[:, pl.ds(8 * x, 8), :].reshape(CH, 128) + skip_ref[x]).T
    left(0, r1, NZ - 1)
    left(1, r2, NY - 1)
    left(2, r4, 63)
    left(3, r5, 63)
    left(4, r7, NY - 1)
    left(5, rv, NY - 1)
    left(6, r8, NZ - 1)
    left(7, around, 26)


def whole(points, counts, kin, kmid, kout, wskip, near, weights):
    fz, fy, fx, ix, iy, iz = transform_tables()
    tables = [wide_table(fz), *two_tables(fy), wide_table(fx), wide_table(ix)]
    tables += [*two_tables(iy), wide_table(iz)]
    vmem, anywhere = (pl.BlockSpec(memory_space=m) for m in (pltpu.VMEM, pl.ANY))
    v = pltpu.VMEM
    return pl.pallas_call(
        whole_kernel,
        out_shape=jax.ShapeDtypeStruct((8, 128, CH), F32),
        in_specs=[vmem] * 6 + [anywhere] * (2 + len(tables)),
        out_specs=vmem,
        scratch_shapes=[
            v((8, 128, NB), jnp.int32), v((2048, CH), BF16),
            v((GRID, 512), F32), v((512, 128), BF16), v((512, 128), BF16),
            v((16, 128), F32), v((8, 256), F32), v((128, 512), BF16), v((128, 512), BF16),
            v((32, 1024), F32),
            v((27, 24, 128), F32), v((256, PTS), F32), v((256, PTS), BF16),
            v((CHUNKS, 8, 128), F32), v((CHUNKS, 8, 128), F32), v((8, 8, 128), F32),
            v((8, KH, 128), F32), v((PTS, 128), BF16), v((256, 128), BF16),
            v((KH, 256), BF16), v((KH, KH), BF16),
            v((256, 1024), BF16), v((256, 1024), BF16), v((KH, 1024), BF16), v((KH, 1024), BF16),
            v((8, KH, 128), F32), v((8, CH, 128), F32), v((8, CH, 128), F32),
            v((128, 128), BF16), v((128, 128), BF16), v((64, 256), BF16), v((64, 256), BF16),
            v((NZ, 64, 128), BF16), v((NZ, 64, 128), BF16),
            v((NY, 64, 128), F32), v((NY, 64, 128), F32),
            v((CH, 2, 128), F32), v((CH, 2, 128), F32),
            v((NZ, 2, 128), F32), v((CH, 2, 128), F32),
            v((NY, 64, 128), BF16), v((NY, 64, 128), BF16),
            v((8, 128), F32), v((NY, 8, 128), F32),
            v((NZ, 64, 128), BF16), v((NZ, 64, 128), BF16),
            v((1024, 512), BF16), v((1024, 512), BF16), v((512, 1024), BF16),
            v((MODES, 128), F32), v((NZ, 64, 128), F32),
            pltpu.SemaphoreType.DMA((8,)), pltpu.SemaphoreType.DMA((8,)),
            pltpu.SemaphoreType.DMA((10,)),
        ],
        compiler_params=pltpu.CompilerParams(collective_id=0, has_side_effects=True),
        name="whole",
    )(points, counts, kin, kmid, kout, wskip, near, weights, *tables)


def body(point_data, neighbours, counts, kernel_in, kernel_mid, kernel_out, spectral, skip_weight):
    out = whole(
        point_data.reshape(24, 128),
        jnp.swapaxes(counts[0], 1, 2).reshape(64, 16),
        kernel_in,
        kernel_mid,
        kernel_out.T,
        skip_weight,
        neighbours.reshape(8, 128, NB),
        spectral.reshape(2048, CH),
    )
    return out.reshape(1, 8, 16, 8, CH)


def solution(mesh):
    cells = P(None, "gx", "gy", "gz", None)
    return jax.shard_map(
        body,
        mesh=mesh,
        in_specs=(
            P(None, None, ("gx", "gy", "gz")),
            cells,
            P(None, "gx", "gy", "gz"),
            P(),
            P(),
            P(),
            P(None, "gz", "gx", "gy", None, None),
            P(),
        ),
        out_specs=cells,
        check_vma=False,
    )
```

time: 87.7 us -> 74.8 us (0.85)
  Pallas kernels: 80.4 us -> 72.7 us
  local copies, waits for them, and re-layouts: 5.87 us -> 1.87 us
  other arithmetic: 1.08 us -> 0 us
    pallas_call x3 -> x1, Pallas kernels: 80.4 us -> 72.7 us  [whole(): pl.pallas_call(whole_kernel, out_shape=jax.ShapeDtypeStruct((8, 128, CH),...]
    unnamed x9 -> x1, local copies, waits for them, and re-layouts: 3.9 us -> 1.87 us
    reshape x1 -> x0, local copies, waits for them, and re-layouts: 1.21 us -> none  [body(): near = jnp.swapaxes(neighbours.reshape(8, 128, NB), 1, 2)]
    convert_element_type x2 -> x0, other arithmetic: 1.08 us -> none  [the longest x1 1.07 us: body(): slot = (near % PTS - 256).astype(F32).reshape(CHUNKS, 8, 128)]
where the time goes in v4:
time: 74.8 us; the launch traced here: 74.6 us
  Pallas kernels  72.7 us (97%)
  local copies, waits for them, and re-layouts  1.87 us (2%)
    pallas_call x1, Pallas kernels, whole(): pl.pallas_call(whole_kernel, out_shape=jax.ShapeDtypeStruct((8, 128, CH),...  72.7 us
    unnamed x1, local copies, waits for them, and re-layouts  1.87 us

profile of v4, /device:TPU:1, one launch (start us, length us, event | category | flops | bytes accessed | tf_op | source)
XLA Modules:
  0.0 74.6 jit_solution(190310925403190256)
XLA Ops:
  0.0 72.7 %whole.1 = f32[8,128,64]{2,1,0:T(8,128)} custom-call(f32[24,128]{1,0:T(8,128)} %bitcast.15, s32[64,16]{1,0:T(8,128)} %bitcast.13, bf16[6,80]{1,0:T(8,128)(2,1)} %kin_ref.1, bf16[80,80]{1,0:T(8,128)(2,1)} %kmid_ref.1, bf16[64,80]{1,0:T(8,128)(2,1)} %bitcast.14, bf16[64,64]{1,0:T(8,128)(2,1)} %wskip_ref.1, s32[8,128,32]{2,1,0:T(8,128)} %bitcast.11, ...), custom_call_target="tpu_custom_call" | custom-call | tf_op jit(solution)/shard_map/whole/pallas_call | solution.py:439
  72.7 1.9 %copy.18 = f32[1,8,16,8,64]{4,3,2,1,0:T(8,128)} copy(f32[1,8,16,8,64]{4,3,2,1,0:T(8,128)} %bitcast.10) | data formatting | bytes 524288

commit v5 on v4

--- a/solution.py
+++ b/solution.py
@@ -41,11 +41,35 @@
 
 
 def twice_gelu(v):
-    inner = v * (0.7978845608028654 + 0.035677408136300125 * (v * v))
+    v = v.astype(BF16)
+    inner = v * (BF16(0.7978845608028654) + BF16(0.035677408136300125) * (v * v))
     return v + v * jnp.tanh(inner)
 
 
+def looked_up(lookup, chosen, block):
+    low = chosen & 127
+    odd, upper = (chosen & 128) != 0, (chosen & 256) != 0
+    bits = [(block & (1 << n)) != 0 for n in range(5)]
+
+    def tile(n):
+        return jnp.take_along_axis(lookup[n], low, axis=1, mode="promise_in_bounds")
+
+    def tree(first, level):
+        if level < 0:
+            near, far = (
+                jnp.where(odd, tile(4 * first + n + 1), tile(4 * first + n)) for n in (0, 2)
+            )
+            return jnp.where(upper, far, near)
+        left = tree(first, level - 1)
+        if first + (1 << level) >= 27:
+            return left
+        return jnp.where(bits[level], tree(first + (1 << level), level - 1), left)
+
+    return tree(0, 4)
+
+
 CHUNKS = 32
+BY_LANES = (6, 7)
 PART = 256
 
 
@@ -114,7 +138,8 @@
     near_hbm, w_hbm, fzc_hbm, fyh_hbm, fyl_hbm, fxc_hbm, ixc_hbm, iyh_hbm, iyl_hbm, izc_hbm,
     out_ref,
     near, w_ref, fzc_ref, fyh_ref, fyl_ref, fxc_ref, ixc_ref, iyh_ref, iyl_ref, izc_ref,
-    around, table_rows, tab, slot_ids, block_ids, valid_slots, pre, ids, rowblk, win, wmid,
+    around, table_rows, tab, slot_ids, block_ids, valid_slots,
+    lookup, centres, win_few, pair_a, pair_b, pre, rowblk, win, wmid,
     masked_a, masked_b, hid_a, hid_b, acc, lat_ref, skip_ref, fxh, fxl, ixh, ixl,
     s1, r1, s2, r2, s4, r4, s5, r5, s7, r7, sv, rv, s8, r8, fzh, fzl, iz, grid, wide,
     send_sem, recv_sem, in_sem,
@@ -161,7 +186,6 @@
     for peer in peers:
         pl.semaphore_signal(barrier, inc=1, device_id=peer, device_id_type=MESH_ID)
 
-    ids[...] = (iota((PTS, 128), 0) - 256).astype(F32).astype(BF16)
     rowblk[...] = (iota((256, 128), 0) // 9).astype(F32).astype(BF16)
     col = iota((6, 256), 1)
     nine = col % 9
@@ -170,12 +194,15 @@
     win[...] = dot_first(kin_ref[...], chosen).astype(BF16)
     eye = jnp.where(iota((KH, KH), 0) == iota((KH, KH), 1), 0.5, 0.0).astype(BF16)
     wmid[...] = dot_first(kmid_ref[...], eye).astype(BF16)
-    row, lane = iota((6, 128), 0), iota((6, 128), 1)
+    few = jnp.where(iota((6, 8), 0) == iota((6, 8), 1), 1.0, 0.0).astype(BF16)
+    win_few[...] = dot_first(kin_ref[...], few).astype(BF16)
+    row, lane = iota((8, 128), 0), iota((8, 128), 1)
     index_y, index_z = gy * 16 + lane // 8, gz * 8 + lane % 8
     for x in range(8):
         index = jnp.where(row == 0, gx * 8 + x, jnp.where(row == 1, index_y, index_z))
-        centre = jnp.where(row < 3, -(index.astype(F32) + 0.5) / GRID, 0.0).astype(BF16)
-        pre[x] = dot_first(kin_ref[...], centre)
+        centre = jnp.where(row < 3, -(index.astype(F32) + 0.5) / GRID, 0.0)
+        centres[x] = centre
+        pre[x] = dot_first(kin_ref[...], centre[0:6].astype(BF16))
     by_row = jnp.where(iota((16, 128), 1) // 8 == iota((16, 128), 0), 1.0, 0.0).astype(BF16)
     spread = dot(cnt_ref[...].astype(F32).astype(BF16), by_row)
     spread = jnp.where(iota((64, 128), 0) % 8 == iota((64, 128), 1) % 8, spread, 0.0)
@@ -185,6 +212,7 @@
         valid_slots[x] = jnp.broadcast_to(spread[x : x + 1], (8, 128))
     acc[...] = jnp.zeros((8, KH, 128), F32)
     table_rows[pl.ds(240, 16), :] = jnp.zeros((16, PTS), F32)
+    lookup[:, 6:8, :] = jnp.zeros((108, 2, 128), F32)
     fetch(0).wait()
     for x in range(8):
         point = near[x].T
@@ -192,9 +220,9 @@
         offset_z = (owner & 7) - gz + 1
         offset_y = ((owner >> 3) & 3) - gy + 1
         offset_x = (owner >> 5) - gx + 1
-        block = ((offset_x * 3 + offset_y) * 3 + offset_z).astype(F32)
+        block = (offset_x * 3 + offset_y) * 3 + offset_z
         block_ids[pl.ds(4 * x, 4)] = block.reshape(4, 8, 128)
-        slot_ids[pl.ds(4 * x, 4)] = ((point & 511) - 256).astype(F32).reshape(4, 8, 128)
+        slot_ids[pl.ds(4 * x, 4)] = (point & 511).reshape(4, 8, 128)
     pl.semaphore_wait(barrier, len(peers))
 
     def send(n, source, target, peer):
@@ -244,55 +272,79 @@
     for b in range(27):
         for t in range(4):
             block = around[b, pl.ds(t, 6, stride=4), :]
+            lookup[4 * b + t, 0:6, :] = block
             place = block[0:3]
             upper = place.astype(BF16).astype(F32)
             table_rows[pl.ds(9 * b, 9), pl.ds(128 * t, 128)] = jnp.concatenate(
                 [upper, place - upper, block[3:6]], axis=0
             )
     tab[...] = table_rows[...].astype(BF16)
-    one = jnp.ones((PTS, 128), BF16)
-    none = jnp.zeros((PTS, 128), BF16)
-
-    def step(t, masked_out, masked_in, hid_out, hid_in):
+    none = jnp.zeros((256, 128), BF16)
+    low_ids = iota((64, 128), 0)
+
+    def step(t, masked_out, masked_in, pair_out, pair_in, hid_out, hid_in):
         early = jnp.minimum(t, CHUNKS - 1)
         middle = jnp.clip(t - 1, 0, CHUNKS - 1)
         late = jnp.maximum(t - 2, 0)
-        slots, blocks = slot_ids[early], block_ids[early]
+        slots, owners = slot_ids[early], block_ids[early]
+        blocks = owners.astype(F32)
+        centre = centres[early // 4]
         base = jnp.concatenate([pre[middle // 4]] * 2, axis=1)
         valid = jnp.where(t >= 2, valid_slots[late // 4], 0.0)[0:1]
         first = (late % 4 * 8).astype(F32)
         total = jnp.zeros((KH, 128), F32)
         for part in range(4):
             span = pl.ds(part * PART, PART)
-            hot = []
-            for s in (2 * part, 2 * part + 1):
-                chosen = jnp.broadcast_to(slots[s : s + 1], (PTS, 128)).astype(BF16)
-                hot.append(jnp.where(ids[...] == chosen, one, none))
-            found = dot(tab[...], jnp.concatenate(hot, axis=1))
-            ahead = dot(win[...], masked_in[:, span])
+            by_lanes = 2 * part in BY_LANES
+            if by_lanes:
+                ahead = dot(win_few[...], pair_in[...])
+            else:
+                hot = []
+                for s in (2 * part, 2 * part + 1):
+                    chosen = jnp.broadcast_to(slots[s : s + 1], (8, 128))
+                    low = jnp.broadcast_to((chosen & 63)[0:1], (64, 128))
+                    low = jnp.where(low == low_ids, 1.0, 0.0).astype(BF16)
+                    high = chosen >> 6
+                    for n in range(8):
+                        here = jnp.where(high == n, 1.0, 0.0)
+                        here = jnp.concatenate([here] * 8, axis=0).astype(BF16)
+                        hot.append(low * here)
+                hot = [jnp.concatenate(hot[:8], axis=0), jnp.concatenate(hot[8:], axis=0)]
+                found = dot(tab[...], jnp.concatenate(hot, axis=1))
+                ahead = dot(win[...], masked_in[:, span]) + base
             last = dot(wmid[...], hid_in[:, span])
-            hid_out[:, span] = twice_gelu(ahead + base).astype(BF16)
-            last = twice_gelu(last).astype(BF16).astype(F32)
+            hid_out[:, span] = twice_gelu(ahead)
+            last = twice_gelu(last).astype(F32)
             for n in range(2):
                 used = valid > first + (2 * part + n)
                 total = total + jnp.where(used, last[:, n * 128 : (n + 1) * 128], 0.0)
-            found = found.astype(BF16)
-            for n in range(2):
-                s = 2 * part + n
-                chosen = jnp.broadcast_to(blocks[s : s + 1], (256, 128)).astype(BF16)
-                masked_out[:, pl.ds(s * 128, 128)] = jnp.where(
-                    rowblk[...] == chosen, found[:, n * 128 : (n + 1) * 128], none[0:256]
-                )
+            if by_lanes:
+                for n in range(2):
+                    s = 2 * part + n
+                    chosen = jnp.broadcast_to(slots[s : s + 1], (8, 128))
+                    block = jnp.broadcast_to(owners[s : s + 1], (8, 128))
+                    pair = looked_up(lookup, chosen, block) + centre
+                    pair_out[:, pl.ds(n * 128, 128)] = pair.astype(BF16)
+            else:
+                found = found.astype(BF16)
+                for n in range(2):
+                    s = 2 * part + n
+                    chosen = jnp.broadcast_to(blocks[s : s + 1], (256, 128)).astype(BF16)
+                    masked_out[:, pl.ds(s * 128, 128)] = jnp.where(
+                        rowblk[...] == chosen, found[:, n * 128 : (n + 1) * 128], none
+                    )
         acc[late // 4] += total
 
     for unset in (masked_a, masked_b):
         unset[...] = jnp.zeros((256, 1024), BF16)
+    for unset in (pair_a, pair_b):
+        unset[...] = jnp.zeros((8, 256), BF16)
     for unset in (hid_a, hid_b):
         unset[...] = jnp.zeros((KH, 1024), BF16)
 
     def two_steps(tt, carry):
-        step(2 * tt, masked_a, masked_b, hid_a, hid_b)
-        step(2 * tt + 1, masked_b, masked_a, hid_b, hid_a)
+        step(2 * tt, masked_a, masked_b, pair_a, pair_b, hid_a, hid_b)
+        step(2 * tt + 1, masked_b, masked_a, pair_b, pair_a, hid_b, hid_a)
         return carry
 
     lax.fori_loop(0, CHUNKS // 2 + 1, two_steps, 0)
@@ -447,8 +499,10 @@
             v((16, 128), F32), v((8, 256), F32), v((128, 512), BF16), v((128, 512), BF16),
             v((32, 1024), F32),
             v((27, 24, 128), F32), v((256, PTS), F32), v((256, PTS), BF16),
-            v((CHUNKS, 8, 128), F32), v((CHUNKS, 8, 128), F32), v((8, 8, 128), F32),
-            v((8, KH, 128), F32), v((PTS, 128), BF16), v((256, 128), BF16),
+            v((CHUNKS, 8, 128), jnp.int32), v((CHUNKS, 8, 128), jnp.int32), v((8, 8, 128), F32),
+            v((108, 8, 128), F32), v((8, 8, 128), F32), v((KH, 8), BF16),
+            v((8, 256), BF16), v((8, 256), BF16),
+            v((8, KH, 128), F32), v((256, 128), BF16),
             v((KH, 256), BF16), v((KH, KH), BF16),
             v((256, 1024), BF16), v((256, 1024), BF16), v((KH, 1024), BF16), v((KH, 1024), BF16),
             v((8, KH, 128), F32), v((8, CH, 128), F32), v((8, CH, 128), F32),

time: 74.8 us -> 69.3 us (0.926)
  Pallas kernels: 72.7 us -> 67.3 us
    pallas_call x1, Pallas kernels: 72.7 us -> 67.3 us  [whole(): pl.pallas_call(whole_kernel, out_shape=jax.ShapeDtypeStruct((8, 128, CH),...]
where the time goes in v5:
time: 69.3 us; the launch traced here: 69.1 us
  Pallas kernels  67.3 us (97%)
  local copies, waits for them, and re-layouts  1.87 us (3%)
    pallas_call x1, Pallas kernels, whole(): pl.pallas_call(whole_kernel, out_shape=jax.ShapeDtypeStruct((8, 128, CH),...  67.3 us
    unnamed x1, local copies, waits for them, and re-layouts  1.87 us

profile of v5, /device:TPU:1, one launch (start us, length us, event | category | flops | bytes accessed | tf_op | source)
XLA Modules:
  0.0 69.1 jit_solution(18173180962399908868)
XLA Ops:
  0.0 67.3 %whole.1 = f32[8,128,64]{2,1,0:T(8,128)} custom-call(f32[24,128]{1,0:T(8,128)} %bitcast.15, s32[64,16]{1,0:T(8,128)} %bitcast.13, bf16[6,80]{1,0:T(8,128)(2,1)} %kin_ref.1, bf16[80,80]{1,0:T(8,128)(2,1)} %kmid_ref.1, bf16[64,80]{1,0:T(8,128)(2,1)} %bitcast.14, bf16[64,64]{1,0:T(8,128)(2,1)} %wskip_ref.1, s32[8,128,32]{2,1,0:T(8,128)} %bitcast.11, ...), custom_call_target="tpu_custom_call" | custom-call | tf_op jit(solution)/shard_map/whole/pallas_call | solution.py:491
  67.3 1.9 %copy.18 = f32[1,8,16,8,64]{4,3,2,1,0:T(8,128)} copy(f32[1,8,16,8,64]{4,3,2,1,0:T(8,128)} %bitcast.10) | data formatting | bytes 524288

commit v6 on v5

--- a/solution.py
+++ b/solution.py
@@ -134,10 +134,9 @@
 
 
 def whole_kernel(
-    pts_ref, cnt_ref, kin_ref, kmid_ref, kout_ref, wskip_ref,
-    near_hbm, w_hbm, fzc_hbm, fyh_hbm, fyl_hbm, fxc_hbm, ixc_hbm, iyh_hbm, iyl_hbm, izc_hbm,
+    pts_hbm, cnt_hbm, kin_hbm, kmid_hbm, kout_hbm, wskip_hbm, near_hbm, w_hbm, fzc_hbm, fyh_hbm, fyl_hbm, fxc_hbm, ixc_hbm, iyh_hbm, iyl_hbm, izc_hbm,
     out_ref,
-    near, w_ref, fzc_ref, fyh_ref, fyl_ref, fxc_ref, ixc_ref, iyh_ref, iyl_ref, izc_ref,
+    pts_ref, cnt_ref, kin_ref, kmid_ref, kout_ref, wskip_ref, near, w_ref, fzc_ref, fyh_ref, fyl_ref, fxc_ref, ixc_ref, iyh_ref, iyl_ref, izc_ref,
     around, table_rows, tab, slot_ids, block_ids, valid_slots,
     lookup, centres, win_few, pair_a, pair_b, pre, rowblk, win, wmid,
     masked_a, masked_b, hid_a, hid_b, acc, lat_ref, skip_ref, fxh, fxl, ixh, ixl,
@@ -150,13 +149,14 @@
     fetched = [
         (near_hbm, near), (fzc_hbm, fzc_ref), (fxc_hbm.at[gx], fxc_ref), (ixc_hbm.at[gx], ixc_ref),
         (izc_hbm, izc_ref), (fyh_hbm, fyh_ref), (fyl_hbm, fyl_ref), (iyh_hbm, iyh_ref),
-        (iyl_hbm, iyl_ref), (w_hbm, w_ref),
+        (iyl_hbm, iyl_ref), (w_hbm, w_ref), (kin_hbm, kin_ref), (kmid_hbm, kmid_ref),
+        (cnt_hbm, cnt_ref), (pts_hbm, pts_ref), (kout_hbm, kout_ref), (wskip_hbm, wskip_ref),
     ]
 
     def fetch(n):
         return pltpu.make_async_copy(fetched[n][0], fetched[n][1], in_sem.at[n])
 
-    for n in range(len(fetched)):
+    for n in (13, 10, 11, 12, 0, 14, 15, *range(1, 10)):
         fetch(n).start()
 
     def along_y(d):
@@ -165,14 +165,17 @@
     def along_z(d):
         return (gx, gy, lax.rem(gz + d, NZ))
 
+    far_z = (4, 3, 5, 2, 6, 1, 7)
+
     def beside(step):
         return tuple(lax.rem(p + d + n, n) for p, d, n in zip((gx, gy, gz), step, (NX, NY, NZ)))
 
     plane = [
         (lax.rem(gx + dx, NX), gy, lax.rem(gz + dz, NZ))
-        for dx in range(NX)
-        for dz in range(NZ)
-        if (dx, dz) != (0, 0)
+        for dx, dz in sorted(
+            ((dx, dz) for dx in range(NX) for dz in range(NZ) if (dx, dz) != (0, 0)),
+            key=lambda d: -2 * min(d[0], NX - d[0]) - min(d[1], NZ - d[1]),
+        )
     ]
     steps = [
         (dx, dy, dz)
@@ -186,7 +189,9 @@
     for peer in peers:
         pl.semaphore_signal(barrier, inc=1, device_id=peer, device_id_type=MESH_ID)
 
-    rowblk[...] = (iota((256, 128), 0) // 9).astype(F32).astype(BF16)
+    for n in range(10, 16):
+        fetch(n).wait()
+    rowblk[...] = iota((256, 128), 0) // 9
     col = iota((6, 256), 1)
     nine = col % 9
     source = jnp.where(nine < 3, nine, nine - 3)
@@ -279,7 +284,6 @@
                 [upper, place - upper, block[3:6]], axis=0
             )
     tab[...] = table_rows[...].astype(BF16)
-    none = jnp.zeros((256, 128), BF16)
     low_ids = iota((64, 128), 0)
 
     def step(t, masked_out, masked_in, pair_out, pair_in, hid_out, hid_in):
@@ -287,7 +291,6 @@
         middle = jnp.clip(t - 1, 0, CHUNKS - 1)
         late = jnp.maximum(t - 2, 0)
         slots, owners = slot_ids[early], block_ids[early]
-        blocks = owners.astype(F32)
         centre = centres[early // 4]
         base = jnp.concatenate([pre[middle // 4]] * 2, axis=1)
         valid = jnp.where(t >= 2, valid_slots[late // 4], 0.0)[0:1]
@@ -326,13 +329,11 @@
                     pair = looked_up(lookup, chosen, block) + centre
                     pair_out[:, pl.ds(n * 128, 128)] = pair.astype(BF16)
             else:
-                found = found.astype(BF16)
                 for n in range(2):
                     s = 2 * part + n
-                    chosen = jnp.broadcast_to(blocks[s : s + 1], (256, 128)).astype(BF16)
-                    masked_out[:, pl.ds(s * 128, 128)] = jnp.where(
-                        rowblk[...] == chosen, found[:, n * 128 : (n + 1) * 128], none
-                    )
+                    chosen = jnp.broadcast_to(owners[s : s + 1], (256, 128))
+                    kept = jnp.where(rowblk[...] == chosen, found[:, n * 128 : (n + 1) * 128], 0.0)
+                    masked_out[:, pl.ds(s * 128, 128)] = kept.astype(BF16)
         acc[late // 4] += total
 
     for unset in (masked_a, masked_b):
@@ -347,19 +348,30 @@
         step(2 * tt + 1, masked_b, masked_a, pair_b, pair_a, hid_b, hid_a)
         return carry
 
-    lax.fori_loop(0, CHUNKS // 2 + 1, two_steps, 0)
-    for x in range(8):
-        upper, lower = split_two(0.5 * acc[x])
-        values = dot(kout_ref[...], upper) + dot(kout_ref[...], lower)
-        latent = (values / valid_slots[x, 0:1]).astype(BF16)
-        skip_ref[x] = dot_first(wskip_ref[...], latent)
-        lat_ref[x] = latent.astype(F32)
-    for q in range(NZ):
-        s1[q] = lat_ref[:, pl.ds(8 * q, 8), :].reshape(64, 128).astype(BF16)
-    for d in range(1, NZ):
+    def finish(slabs):
+        for x in slabs:
+            upper, lower = split_two(0.5 * acc[x])
+            values = dot(kout_ref[...], upper) + dot(kout_ref[...], lower)
+            latent = (values / valid_slots[x, 0:1]).astype(BF16)
+            skip_ref[x] = dot_first(wskip_ref[...], latent)
+            lat_ref[x] = latent.astype(F32)
+        span = pl.ds(8 * slabs[0], 8 * len(slabs))
+        for q in range(NZ):
+            ready = lat_ref[slabs[0] : slabs[-1] + 1, pl.ds(8 * q, 8), :]
+            s1[q, span, :] = ready.reshape(8 * len(slabs), 128).astype(BF16)
+        r1[gz, span, :] = s1[gz, span, :]
+        return span
+
+    lax.fori_loop(0, 13, two_steps, 0)
+    span = finish(range(6))
+    for d in far_z:
         peer = along_z(d)
-        send(0, s1.at[peer[2]], r1.at[gz], peer)
-    r1[gz] = s1[gz]
+        send(0, s1.at[peer[2], span], r1.at[gz, span], peer)
+    lax.fori_loop(13, CHUNKS // 2 + 1, two_steps, 0)
+    span = finish(range(6, 8))
+    for d in far_z:
+        peer = along_z(d)
+        send(8, s1.at[peer[2], span], r1.at[gz, span], peer)
     row, lane = iota((128, 128), 0), iota((128, 128), 1)
     row_i, lane_i = row // 8 % 8 * 2 + row // 64, lane // 8 % 8 * 2 + lane // 64
     mirror = (row % 8 == lane % 8) & (row_i != 8) & (lane_i == (16 - row_i) % 16)
@@ -373,7 +385,9 @@
     own_mode = iota((32, 1024), 1) // CH == iota((32, 1024), 0) % MODES
     for n in range(5, 10):
         fetch(n).wait()
-    arrived(0, r1, NZ - 1)
+    for n, span in ((0, pl.ds(0, 48)), (8, pl.ds(48, 16))):
+        part = r1.at[pl.ds(0, NZ - 1), span]
+        pltpu.make_async_copy(part, part, recv_sem.at[n]).wait()
     line = jnp.concatenate([r1[q] for q in range(NZ)], axis=1)
     deep = dot(line, fzh[...]) + dot(line, fzl[...])
     for q in range(NY):
@@ -464,7 +478,7 @@
     scale = jnp.concatenate([scale] * 8, axis=0)
     for q in range(NZ):
         s8[q] = (depth[:, q * 128 : (q + 1) * 128] * scale).astype(BF16)
-    for d in range(1, NZ):
+    for d in far_z:
         peer = along_z(d)
         send(6, s8.at[peer[2]], r8.at[gz], peer)
     r8[gz] = s8[gz]
@@ -472,7 +486,9 @@
     wide[...] = r8[...].astype(F32)
     for x in range(8):
         out_ref[x] = gelu(wide[:, pl.ds(8 * x, 8), :].reshape(CH, 128) + skip_ref[x]).T
-    left(0, r1, NZ - 1)
+    for n, span in ((0, pl.ds(0, 48)), (8, pl.ds(48, 16))):
+        part = r1.at[pl.ds(0, NZ - 1), span]
+        pltpu.make_async_copy(part, part, send_sem.at[n]).wait()
     left(1, r2, NY - 1)
     left(2, r4, 63)
     left(3, r5, 63)
@@ -491,9 +507,11 @@
     return pl.pallas_call(
         whole_kernel,
         out_shape=jax.ShapeDtypeStruct((8, 128, CH), F32),
-        in_specs=[vmem] * 6 + [anywhere] * (2 + len(tables)),
+        in_specs=[anywhere] * (8 + len(tables)),
         out_specs=vmem,
         scratch_shapes=[
+            v((24, 128), F32), v((64, 16), jnp.int32), v((6, KH), BF16), v((KH, KH), BF16),
+            v((CH, KH), BF16), v((CH, CH), BF16),
             v((8, 128, NB), jnp.int32), v((2048, CH), BF16),
             v((GRID, 512), F32), v((512, 128), BF16), v((512, 128), BF16),
             v((16, 128), F32), v((8, 256), F32), v((128, 512), BF16), v((128, 512), BF16),
@@ -502,7 +520,7 @@
             v((CHUNKS, 8, 128), jnp.int32), v((CHUNKS, 8, 128), jnp.int32), v((8, 8, 128), F32),
             v((108, 8, 128), F32), v((8, 8, 128), F32), v((KH, 8), BF16),
             v((8, 256), BF16), v((8, 256), BF16),
-            v((8, KH, 128), F32), v((256, 128), BF16),
+            v((8, KH, 128), F32), v((256, 128), jnp.int32),
             v((KH, 256), BF16), v((KH, KH), BF16),
             v((256, 1024), BF16), v((256, 1024), BF16), v((KH, 1024), BF16), v((KH, 1024), BF16),
             v((8, KH, 128), F32), v((8, CH, 128), F32), v((8, CH, 128), F32),
@@ -516,8 +534,8 @@
             v((NZ, 64, 128), BF16), v((NZ, 64, 128), BF16),
             v((1024, 512), BF16), v((1024, 512), BF16), v((512, 1024), BF16),
             v((MODES, 128), F32), v((NZ, 64, 128), F32),
-            pltpu.SemaphoreType.DMA((8,)), pltpu.SemaphoreType.DMA((8,)),
-            pltpu.SemaphoreType.DMA((10,)),
+            pltpu.SemaphoreType.DMA((9,)), pltpu.SemaphoreType.DMA((9,)),
+            pltpu.SemaphoreType.DMA((16,)),
         ],
         compiler_params=pltpu.CompilerParams(collective_id=0, has_side_effects=True),
         name="whole",

time: 69.3 us -> 67.3 us (0.971)
  Pallas kernels: 67.3 us -> 65.3 us
    pallas_call x1, Pallas kernels: 67.3 us -> 65.3 us  [whole(): pl.pallas_call(whole_kernel, out_shape=jax.ShapeDtypeStruct((8, 128, CH),...]
where the time goes in v6:
time: 67.3 us; the launch traced here: 67.2 us
  Pallas kernels  65.3 us (97%)
  local copies, waits for them, and re-layouts  1.87 us (3%)
    pallas_call x1, Pallas kernels, whole(): pl.pallas_call(whole_kernel, out_shape=jax.ShapeDtypeStruct((8, 128, CH),...  65.3 us
    unnamed x1, local copies, waits for them, and re-layouts  1.87 us

profile of v6, /device:TPU:1, one launch (start us, length us, event | category | flops | bytes accessed | tf_op | source)
XLA Modules:
  0.0 67.2 jit_solution(14473449665344140025)
XLA Ops:
  0.0 65.3 %whole.1 = f32[8,128,64]{2,1,0:T(8,128)} custom-call(f32[24,128]{1,0:T(8,128)} %bitcast.15, s32[64,16]{1,0:T(8,128)} %bitcast.13, bf16[6,80]{1,0:T(8,128)(2,1)} %kin_hbm.1, bf16[80,80]{1,0:T(8,128)(2,1)} %kmid_hbm.1, bf16[64,80]{1,0:T(8,128)(2,1)} %bitcast.14, bf16[64,64]{1,0:T(8,128)(2,1)} %wskip_hbm.1, s32[8,128,32]{2,1,0:T(8,128)} %bitcast.11, ...), custom_call_target="tpu_custom_call" | custom-call | tf_op jit(solution)/shard_map/whole/pallas_call | solution.py:507
  65.3 1.9 %copy.18 = f32[1,8,16,8,64]{4,3,2,1,0:T(8,128)} copy(f32[1,8,16,8,64]{4,3,2,1,0:T(8,128)} %bitcast.10) | data formatting | bytes 524288

commit v7 on v6

--- a/solution.py
+++ b/solution.py
@@ -141,7 +141,7 @@
     lookup, centres, win_few, pair_a, pair_b, pre, rowblk, win, wmid,
     masked_a, masked_b, hid_a, hid_b, acc, lat_ref, skip_ref, fxh, fxl, ixh, ixl,
     s1, r1, s2, r2, s4, r4, s5, r5, s7, r7, sv, rv, s8, r8, fzh, fzl, iz, grid, wide,
-    send_sem, recv_sem, in_sem,
+    send_sem, recv_sem, in_sem, heard,
 ):
     gx, gy, gz = lax.axis_index("gx"), lax.axis_index("gy"), lax.axis_index("gz")
     me = gz * NX + gx
@@ -184,10 +184,17 @@
         for dz in (-1, 0, 1)
         if (dx, dy, dz) != (0, 0, 0)
     ]
-    apart = [beside(s) for s in steps if s[1] != 0 and (s[0], s[2]) != (0, 0)]
-    peers = plane + [along_y(d) for d in range(1, NY)] + apart
-    for peer in peers:
-        pl.semaphore_signal(barrier, inc=1, device_id=peer, device_id_type=MESH_ID)
+    flat_steps = [s for s in steps if s[1] == 0]
+    near_steps = flat_steps + [(0, -1, 0), (0, 1, 0)]
+
+    def tell(n, whom):
+        for s in whom:
+            pl.semaphore_signal(
+                heard.at[n], inc=1, device_id=beside(s), device_id_type=MESH_ID
+            )
+
+    for s in steps:
+        pl.semaphore_signal(barrier, inc=1, device_id=beside(s), device_id_type=MESH_ID)
 
     for n in range(10, 16):
         fetch(n).wait()
@@ -218,6 +225,31 @@
     acc[...] = jnp.zeros((8, KH, 128), F32)
     table_rows[pl.ds(240, 16), :] = jnp.zeros((16, PTS), F32)
     lookup[:, 6:8, :] = jnp.zeros((108, 2, 128), F32)
+    pl.semaphore_wait(barrier, len(steps))
+    tell(0, near_steps)
+
+    def send(n, source, target, peer):
+        pltpu.make_async_remote_copy(
+            src_ref=source,
+            dst_ref=target,
+            send_sem=send_sem.at[n],
+            recv_sem=recv_sem.at[n],
+            device_id=peer,
+            device_id_type=MESH_ID,
+        ).start()
+
+    def arrived(n, buffer, count):
+        part = buffer.at[pl.ds(0, count)]
+        pltpu.make_async_copy(part, part, recv_sem.at[n]).wait()
+
+    def left(n, buffer, count):
+        part = buffer.at[pl.ds(0, count)]
+        pltpu.make_async_copy(part, part, send_sem.at[n]).wait()
+
+    for step in steps:
+        block = ((1 - step[0]) * 3 + (1 - step[1])) * 3 + (1 - step[2])
+        send(7, pts_ref, around.at[block], beside(step))
+    around[13] = pts_ref[...]
     fetch(0).wait()
     for x in range(8):
         point = near[x].T
@@ -228,30 +260,8 @@
         block = (offset_x * 3 + offset_y) * 3 + offset_z
         block_ids[pl.ds(4 * x, 4)] = block.reshape(4, 8, 128)
         slot_ids[pl.ds(4 * x, 4)] = (point & 511).reshape(4, 8, 128)
-    pl.semaphore_wait(barrier, len(peers))
-
-    def send(n, source, target, peer):
-        pltpu.make_async_remote_copy(
-            src_ref=source,
-            dst_ref=target,
-            send_sem=send_sem.at[n],
-            recv_sem=recv_sem.at[n],
-            device_id=peer,
-            device_id_type=MESH_ID,
-        ).start()
-
-    def arrived(n, buffer, count):
-        part = buffer.at[pl.ds(0, count)]
-        pltpu.make_async_copy(part, part, recv_sem.at[n]).wait()
-
-    def left(n, buffer, count):
-        part = buffer.at[pl.ds(0, count)]
-        pltpu.make_async_copy(part, part, send_sem.at[n]).wait()
-
-    for step in steps:
-        block = ((1 - step[0]) * 3 + (1 - step[1])) * 3 + (1 - step[2])
-        send(7, pts_ref, around.at[block], beside(step))
-    around[13] = pts_ref[...]
+    pl.semaphore_wait(heard.at[0], len(near_steps))
+    tell(1, flat_steps)
     for n in range(1, 5):
         fetch(n).wait()
     own_y = iota((128, 512), 0) // 8 == iota((128, 512), 1) % 128 // 8
@@ -273,6 +283,8 @@
         [jnp.broadcast_to(ixc_ref[pl.ds(n, 1), :], (8, 256)) for n in range(8)], axis=0
     )
     ixh[...], ixl[...] = split_two(jnp.where(iota((64, 256), 0) % 8 == iota((64, 256), 1) % 8, part, 0.0))
+    pl.semaphore_wait(heard.at[1], len(flat_steps))
+    tell(2, flat_steps)
     arrived(7, around, 26)
     for b in range(27):
         for t in range(4):
@@ -364,6 +376,7 @@
 
     lax.fori_loop(0, 13, two_steps, 0)
     span = finish(range(6))
+    pl.semaphore_wait(heard.at[2], len(flat_steps))
     for d in far_z:
         peer = along_z(d)
         send(0, s1.at[peer[2], span], r1.at[gz, span], peer)
@@ -535,7 +548,7 @@
             v((1024, 512), BF16), v((1024, 512), BF16), v((512, 1024), BF16),
             v((MODES, 128), F32), v((NZ, 64, 128), F32),
             pltpu.SemaphoreType.DMA((9,)), pltpu.SemaphoreType.DMA((9,)),
-            pltpu.SemaphoreType.DMA((16,)),
+            pltpu.SemaphoreType.DMA((16,)), pltpu.SemaphoreType.REGULAR((3,)),
         ],
         compiler_params=pltpu.CompilerParams(collective_id=0, has_side_effects=True),
         name="whole",

time: 67.3 us -> 65.7 us (0.976)
  Pallas kernels: 65.3 us -> 63.7 us
    pallas_call x1, Pallas kernels: 65.3 us -> 63.7 us  [whole(): pl.pallas_call(whole_kernel, out_shape=jax.ShapeDtypeStruct((8, 128, CH),...]
where the time goes in v7:
time: 65.7 us; the launch traced here: 65.6 us
  Pallas kernels  63.7 us (97%)
  local copies, waits for them, and re-layouts  1.87 us (3%)
    pallas_call x1, Pallas kernels, whole(): pl.pallas_call(whole_kernel, out_shape=jax.ShapeDtypeStruct((8, 128, CH),...  63.7 us
    unnamed x1, local copies, waits for them, and re-layouts  1.87 us

profile of v7, /device:TPU:1, one launch (start us, length us, event | category | flops | bytes accessed | tf_op | source)
XLA Modules:
  0.0 65.6 jit_solution(7438746046809966690)
XLA Ops:
  0.0 63.7 %whole.1 = f32[8,128,64]{2,1,0:T(8,128)} custom-call(f32[24,128]{1,0:T(8,128)} %bitcast.15, s32[64,16]{1,0:T(8,128)} %bitcast.13, bf16[6,80]{1,0:T(8,128)(2,1)} %kin_hbm.1, bf16[80,80]{1,0:T(8,128)(2,1)} %kmid_hbm.1, bf16[64,80]{1,0:T(8,128)(2,1)} %bitcast.14, bf16[64,64]{1,0:T(8,128)(2,1)} %wskip_hbm.1, s32[8,128,32]{2,1,0:T(8,128)} %bitcast.11, ...), custom_call_target="tpu_custom_call" | custom-call | tf_op jit(solution)/shard_map/whole/pallas_call | solution.py:520
  63.7 1.9 %copy.18 = f32[1,8,16,8,64]{4,3,2,1,0:T(8,128)} copy(f32[1,8,16,8,64]{4,3,2,1,0:T(8,128)} %bitcast.10) | data formatting | bytes 524288

commit v8 on v7

--- a/solution.py
+++ b/solution.py
@@ -71,6 +71,7 @@
 CHUNKS = 32
 BY_LANES = (6, 7)
 PART = 256
+ROWS = 176
 
 
 @functools.cache
@@ -141,7 +142,7 @@
     lookup, centres, win_few, pair_a, pair_b, pre, rowblk, win, wmid,
     masked_a, masked_b, hid_a, hid_b, acc, lat_ref, skip_ref, fxh, fxl, ixh, ixl,
     s1, r1, s2, r2, s4, r4, s5, r5, s7, r7, sv, rv, s8, r8, fzh, fzl, iz, grid, wide,
-    send_sem, recv_sem, in_sem, heard,
+    result, send_sem, recv_sem, in_sem, heard, out_sem,
 ):
     gx, gy, gz = lax.axis_index("gx"), lax.axis_index("gy"), lax.axis_index("gz")
     me = gz * NX + gx
@@ -198,20 +199,19 @@
 
     for n in range(10, 16):
         fetch(n).wait()
-    rowblk[...] = iota((256, 128), 0) // 9
-    col = iota((6, 256), 1)
-    nine = col % 9
-    source = jnp.where(nine < 3, nine, nine - 3)
-    chosen = jnp.where((source == iota((6, 256), 0)) & (col < 243), 1.0, 0.0).astype(BF16)
+    rowblk[...] = iota((ROWS, 128), 0) // 6
+    col = iota((6, ROWS), 1)
+    chosen = (col % 6 == iota((6, ROWS), 0)) & (col < 162)
+    chosen = jnp.where(chosen, 1.0, 0.0).astype(BF16)
     win[...] = dot_first(kin_ref[...], chosen).astype(BF16)
     eye = jnp.where(iota((KH, KH), 0) == iota((KH, KH), 1), 0.5, 0.0).astype(BF16)
     wmid[...] = dot_first(kmid_ref[...], eye).astype(BF16)
     few = jnp.where(iota((6, 8), 0) == iota((6, 8), 1), 1.0, 0.0).astype(BF16)
     win_few[...] = dot_first(kin_ref[...], few).astype(BF16)
     row, lane = iota((8, 128), 0), iota((8, 128), 1)
-    index_y, index_z = gy * 16 + lane // 8, gz * 8 + lane % 8
+    index_y, index_z = lane // 8 - 8, lane % 8 - 4
     for x in range(8):
-        index = jnp.where(row == 0, gx * 8 + x, jnp.where(row == 1, index_y, index_z))
+        index = jnp.where(row == 0, x - 4, jnp.where(row == 1, index_y, index_z))
         centre = jnp.where(row < 3, -(index.astype(F32) + 0.5) / GRID, 0.0)
         centres[x] = centre
         pre[x] = dot_first(kin_ref[...], centre[0:6].astype(BF16))
@@ -223,7 +223,10 @@
     for x in range(8):
         valid_slots[x] = jnp.broadcast_to(spread[x : x + 1], (8, 128))
     acc[...] = jnp.zeros((8, KH, 128), F32)
-    table_rows[pl.ds(240, 16), :] = jnp.zeros((16, PTS), F32)
+    table_rows[pl.ds(ROWS - 16, 16), :] = jnp.zeros((16, PTS), F32)
+    row = iota((6, 128), 0)
+    middle = jnp.where(row == 0, gx * 8 + 4, jnp.where(row == 1, gy * 16 + 8, gz * 8 + 4))
+    middle = jnp.where(row < 3, middle.astype(F32) / GRID, 0.0)
     lookup[:, 6:8, :] = jnp.zeros((108, 2, 128), F32)
     pl.semaphore_wait(barrier, len(steps))
     tell(0, near_steps)
@@ -288,13 +291,9 @@
     arrived(7, around, 26)
     for b in range(27):
         for t in range(4):
-            block = around[b, pl.ds(t, 6, stride=4), :]
+            block = around[b, pl.ds(t, 6, stride=4), :] - middle
             lookup[4 * b + t, 0:6, :] = block
-            place = block[0:3]
-            upper = place.astype(BF16).astype(F32)
-            table_rows[pl.ds(9 * b, 9), pl.ds(128 * t, 128)] = jnp.concatenate(
-                [upper, place - upper, block[3:6]], axis=0
-            )
+            table_rows[pl.ds(6 * b, 6), pl.ds(128 * t, 128)] = block
     tab[...] = table_rows[...].astype(BF16)
     low_ids = iota((64, 128), 0)
 
@@ -343,13 +342,13 @@
             else:
                 for n in range(2):
                     s = 2 * part + n
-                    chosen = jnp.broadcast_to(owners[s : s + 1], (256, 128))
+                    chosen = jnp.broadcast_to(owners[s : s + 1], (ROWS, 128))
                     kept = jnp.where(rowblk[...] == chosen, found[:, n * 128 : (n + 1) * 128], 0.0)
                     masked_out[:, pl.ds(s * 128, 128)] = kept.astype(BF16)
         acc[late // 4] += total
 
     for unset in (masked_a, masked_b):
-        unset[...] = jnp.zeros((256, 1024), BF16)
+        unset[...] = jnp.zeros((ROWS, 1024), BF16)
     for unset in (pair_a, pair_b):
         unset[...] = jnp.zeros((8, 256), BF16)
     for unset in (hid_a, hid_b):
@@ -469,9 +468,11 @@
     flat = dot(plain, iyh_ref[...]) + dot(plain, iyl_ref[...])
     for q in range(NY):
         s7[q] = flat[:, q * 128 : (q + 1) * 128].astype(BF16)
-    for d in range(1, NY):
-        peer = along_y(d)
-        send(4, s7.at[peer[1]], r7.at[gy], peer)
+    halves = [pl.ds(32 * h, 32) for h in range(2)]
+    for h, span in enumerate(halves):
+        for d in (2, 1, 3):
+            peer = along_y(d)
+            send((4, 9)[h], s7.at[peer[1], span], r7.at[gy, span], peer)
     r7[gy] = s7[gy]
     weight = jnp.where((lane % 4 == 0) & (gy == 0), 0.5, 2.0)
     pairs = dot(dot(mirror, exact).astype(BF16), flip)
@@ -482,32 +483,47 @@
     for d in range(1, NY):
         send(5, sv, rv.at[gy], along_y(d))
     rv[gy] = sv[...]
-    arrived(4, r7, NY - 1)
-    line = jnp.concatenate([r7[q] for q in range(NY)], axis=1)
-    depth = dot(line, iz[...])
-    arrived(5, rv, NY - 1)
-    power = (rv[0] + rv[1]) + (rv[2] + rv[3])
-    scale = 1.0 / jnp.sqrt(power * (1.0 / float(GRID) ** 6) + 1.0)
-    scale = jnp.concatenate([scale] * 8, axis=0)
-    for q in range(NZ):
-        s8[q] = (depth[:, q * 128 : (q + 1) * 128] * scale).astype(BF16)
-    for d in far_z:
-        peer = along_z(d)
-        send(6, s8.at[peer[2]], r8.at[gz], peer)
-    r8[gz] = s8[gz]
-    arrived(6, r8, NZ - 1)
-    wide[...] = r8[...].astype(F32)
-    for x in range(8):
-        out_ref[x] = gelu(wide[:, pl.ds(8 * x, 8), :].reshape(CH, 128) + skip_ref[x]).T
+    def both_waits(sems, n, buffer, count, span):
+        part = buffer.at[pl.ds(0, count), span]
+        pltpu.make_async_copy(part, part, sems.at[n]).wait()
+
+    for h, span in enumerate(halves):
+        both_waits(recv_sem, (4, 9)[h], r7, NY - 1, span)
+        line = jnp.concatenate([r7[q, span, :] for q in range(NY)], axis=1)
+        depth = dot(line, iz[...])
+        if h == 0:
+            arrived(5, rv, NY - 1)
+            power = (rv[0] + rv[1]) + (rv[2] + rv[3])
+            scale = 1.0 / jnp.sqrt(power * (1.0 / float(GRID) ** 6) + 1.0)
+            scale = jnp.concatenate([scale] * 4, axis=0)
+        for q in range(NZ):
+            s8[q, span, :] = (depth[:, q * 128 : (q + 1) * 128] * scale).astype(BF16)
+        for d in far_z:
+            peer = along_z(d)
+            send((6, 10)[h], s8.at[peer[2], span], r8.at[gz, span], peer)
+        r8[gz, span, :] = s8[gz, span, :]
+
+    def put(x):
+        return pltpu.make_async_copy(result.at[x], out_ref.at[x], out_sem.at[x])
+
+    for h, span in enumerate(halves):
+        both_waits(recv_sem, (6, 10)[h], r8, NZ - 1, span)
+        wide[:, span, :] = r8[:, span, :].astype(F32)
+        for x in range(4 * h, 4 * h + 4):
+            result[x] = gelu(wide[:, pl.ds(8 * x, 8), :].reshape(CH, 128) + skip_ref[x]).T
+            put(x).start()
     for n, span in ((0, pl.ds(0, 48)), (8, pl.ds(48, 16))):
         part = r1.at[pl.ds(0, NZ - 1), span]
         pltpu.make_async_copy(part, part, send_sem.at[n]).wait()
     left(1, r2, NY - 1)
     left(2, r4, 63)
     left(3, r5, 63)
-    left(4, r7, NY - 1)
+    for h, span in enumerate(halves):
+        both_waits(send_sem, (4, 9)[h], r7, NY - 1, span)
+        both_waits(send_sem, (6, 10)[h], r8, NZ - 1, span)
+    for x in range(8):
+        put(x).wait()
     left(5, rv, NY - 1)
-    left(6, r8, NZ - 1)
     left(7, around, 26)
 
 
@@ -515,13 +531,13 @@
     fz, fy, fx, ix, iy, iz = transform_tables()
     tables = [wide_table(fz), *two_tables(fy), wide_table(fx), wide_table(ix)]
     tables += [*two_tables(iy), wide_table(iz)]
-    vmem, anywhere = (pl.BlockSpec(memory_space=m) for m in (pltpu.VMEM, pl.ANY))
+    anywhere = pl.BlockSpec(memory_space=pl.ANY)
     v = pltpu.VMEM
     return pl.pallas_call(
         whole_kernel,
         out_shape=jax.ShapeDtypeStruct((8, 128, CH), F32),
         in_specs=[anywhere] * (8 + len(tables)),
-        out_specs=vmem,
+        out_specs=anywhere,
         scratch_shapes=[
             v((24, 128), F32), v((64, 16), jnp.int32), v((6, KH), BF16), v((KH, KH), BF16),
             v((CH, KH), BF16), v((CH, CH), BF16),
@@ -529,13 +545,13 @@
             v((GRID, 512), F32), v((512, 128), BF16), v((512, 128), BF16),
             v((16, 128), F32), v((8, 256), F32), v((128, 512), BF16), v((128, 512), BF16),
             v((32, 1024), F32),
-            v((27, 24, 128), F32), v((256, PTS), F32), v((256, PTS), BF16),
+            v((27, 24, 128), F32), v((ROWS, PTS), F32), v((ROWS, PTS), BF16),
             v((CHUNKS, 8, 128), jnp.int32), v((CHUNKS, 8, 128), jnp.int32), v((8, 8, 128), F32),
             v((108, 8, 128), F32), v((8, 8, 128), F32), v((KH, 8), BF16),
             v((8, 256), BF16), v((8, 256), BF16),
-            v((8, KH, 128), F32), v((256, 128), jnp.int32),
-            v((KH, 256), BF16), v((KH, KH), BF16),
-            v((256, 1024), BF16), v((256, 1024), BF16), v((KH, 1024), BF16), v((KH, 1024), BF16),
+            v((8, KH, 128), F32), v((ROWS, 128), jnp.int32),
+            v((KH, ROWS), BF16), v((KH, KH), BF16),
+            v((ROWS, 1024), BF16), v((ROWS, 1024), BF16), v((KH, 1024), BF16), v((KH, 1024), BF16),
             v((8, KH, 128), F32), v((8, CH, 128), F32), v((8, CH, 128), F32),
             v((128, 128), BF16), v((128, 128), BF16), v((64, 256), BF16), v((64, 256), BF16),
             v((NZ, 64, 128), BF16), v((NZ, 64, 128), BF16),
@@ -547,8 +563,9 @@
             v((NZ, 64, 128), BF16), v((NZ, 64, 128), BF16),
             v((1024, 512), BF16), v((1024, 512), BF16), v((512, 1024), BF16),
             v((MODES, 128), F32), v((NZ, 64, 128), F32),
-            pltpu.SemaphoreType.DMA((9,)), pltpu.SemaphoreType.DMA((9,)),
+            v((8, 128, CH), F32), pltpu.SemaphoreType.DMA((11,)), pltpu.SemaphoreType.DMA((11,)),
             pltpu.SemaphoreType.DMA((16,)), pltpu.SemaphoreType.REGULAR((3,)),
+            pltpu.SemaphoreType.DMA((8,)),
         ],
         compiler_params=pltpu.CompilerParams(collective_id=0, has_side_effects=True),
         name="whole",

time: 65.7 us -> 63.4 us (0.965)
  Pallas kernels: 63.7 us -> 61.4 us
    pallas_call x1, Pallas kernels: 63.7 us -> 61.4 us  [whole(): pl.pallas_call(whole_kernel, out_shape=jax.ShapeDtypeStruct((8, 128, CH),...]
where the time goes in v8:
time: 63.4 us; the launch traced here: 63.3 us
  Pallas kernels  61.4 us (97%)
  local copies, waits for them, and re-layouts  1.87 us (3%)
    pallas_call x1, Pallas kernels, whole(): pl.pallas_call(whole_kernel, out_shape=jax.ShapeDtypeStruct((8, 128, CH),...  61.4 us
    unnamed x1, local copies, waits for them, and re-layouts  1.87 us

profile of v8, /device:TPU:1, one launch (start us, length us, event | category | flops | bytes accessed | tf_op | source)
XLA Modules:
  0.0 63.3 jit_solution(6272148955869393901)
XLA Ops:
  0.0 61.4 %whole.1 = f32[8,128,64]{2,1,0:T(8,128)} custom-call(f32[24,128]{1,0:T(8,128)} %bitcast.15, s32[64,16]{1,0:T(8,128)} %bitcast.13, bf16[6,80]{1,0:T(8,128)(2,1)} %kin_hbm.1, bf16[80,80]{1,0:T(8,128)(2,1)} %kmid_hbm.1, bf16[64,80]{1,0:T(8,128)(2,1)} %bitcast.14, bf16[64,64]{1,0:T(8,128)(2,1)} %wskip_hbm.1, s32[8,128,32]{2,1,0:T(8,128)} %bitcast.11, ...), custom_call_target="tpu_custom_call" | custom-call | tf_op jit(solution)/shard_map/whole/pallas_call | solution.py:536
  61.4 1.9 %copy.18 = f32[1,8,16,8,64]{4,3,2,1,0:T(8,128)} copy(f32[1,8,16,8,64]{4,3,2,1,0:T(8,128)} %bitcast.10) | data formatting | bytes 524288

commit v9 on v8

--- a/solution.py
+++ b/solution.py
@@ -297,22 +297,21 @@
     tab[...] = table_rows[...].astype(BF16)
     low_ids = iota((64, 128), 0)
 
-    def step(t, masked_out, masked_in, pair_out, pair_in, hid_out, hid_in):
-        early = jnp.minimum(t, CHUNKS - 1)
-        middle = jnp.clip(t - 1, 0, CHUNKS - 1)
-        late = jnp.maximum(t - 2, 0)
-        slots, owners = slot_ids[early], block_ids[early]
-        centre = centres[early // 4]
-        base = jnp.concatenate([pre[middle // 4]] * 2, axis=1)
-        valid = jnp.where(t >= 2, valid_slots[late // 4], 0.0)[0:1]
-        first = (late % 4 * 8).astype(F32)
-        total = jnp.zeros((KH, 128), F32)
+    def step(t, masked_out, masked_in, pair_out, pair_in, hid_out, hid_in, stages="ghs"):
+        if "g" in stages:
+            slots, owners = slot_ids[t], block_ids[t]
+            centre = centres[t // 4]
+        if "h" in stages:
+            base = jnp.concatenate([pre[(t - 1) // 4]] * 2, axis=1)
+        if "s" in stages:
+            slab = (t - 2) // 4
+            valid = valid_slots[slab][0:1]
+            first = lax.convert_element_type((t - 2) % 4 * 8, F32)
+            total = jnp.zeros((KH, 128), F32)
         for part in range(4):
             span = pl.ds(part * PART, PART)
             by_lanes = 2 * part in BY_LANES
-            if by_lanes:
-                ahead = dot(win_few[...], pair_in[...])
-            else:
+            if "g" in stages and not by_lanes:
                 hot = []
                 for s in (2 * part, 2 * part + 1):
                     chosen = jnp.broadcast_to(slots[s : s + 1], (8, 128))
@@ -325,38 +324,42 @@
                         hot.append(low * here)
                 hot = [jnp.concatenate(hot[:8], axis=0), jnp.concatenate(hot[8:], axis=0)]
                 found = dot(tab[...], jnp.concatenate(hot, axis=1))
-                ahead = dot(win[...], masked_in[:, span]) + base
-            last = dot(wmid[...], hid_in[:, span])
-            hid_out[:, span] = twice_gelu(ahead)
-            last = twice_gelu(last).astype(F32)
+            if "h" in stages:
+                if by_lanes:
+                    ahead = dot(win_few[...], pair_in[...])
+                else:
+                    ahead = dot(win[...], masked_in[:, span]) + base
+            if "s" in stages:
+                last = dot(wmid[...], hid_in[:, span])
+            if "h" in stages:
+                hid_out[:, span] = twice_gelu(ahead)
+            if "s" in stages:
+                last = twice_gelu(last).astype(F32)
+                for n in range(2):
+                    used = valid > first + (2 * part + n)
+                    total = total + jnp.where(used, last[:, n * 128 : (n + 1) * 128], 0.0)
+            if "g" not in stages:
+                continue
             for n in range(2):
-                used = valid > first + (2 * part + n)
-                total = total + jnp.where(used, last[:, n * 128 : (n + 1) * 128], 0.0)
-            if by_lanes:
-                for n in range(2):
-                    s = 2 * part + n
+                s = 2 * part + n
+                if by_lanes:
                     chosen = jnp.broadcast_to(slots[s : s + 1], (8, 128))
                     block = jnp.broadcast_to(owners[s : s + 1], (8, 128))
                     pair = looked_up(lookup, chosen, block) + centre
                     pair_out[:, pl.ds(n * 128, 128)] = pair.astype(BF16)
-            else:
-                for n in range(2):
-                    s = 2 * part + n
+                else:
                     chosen = jnp.broadcast_to(owners[s : s + 1], (ROWS, 128))
                     kept = jnp.where(rowblk[...] == chosen, found[:, n * 128 : (n + 1) * 128], 0.0)
                     masked_out[:, pl.ds(s * 128, 128)] = kept.astype(BF16)
-        acc[late // 4] += total
-
-    for unset in (masked_a, masked_b):
-        unset[...] = jnp.zeros((ROWS, 1024), BF16)
-    for unset in (pair_a, pair_b):
-        unset[...] = jnp.zeros((8, 256), BF16)
-    for unset in (hid_a, hid_b):
-        unset[...] = jnp.zeros((KH, 1024), BF16)
+        if "s" in stages:
+            acc[slab] += total
+
+    even = (masked_a, masked_b, pair_a, pair_b, hid_a, hid_b)
+    odd = (masked_b, masked_a, pair_b, pair_a, hid_b, hid_a)
 
     def two_steps(tt, carry):
-        step(2 * tt, masked_a, masked_b, pair_a, pair_b, hid_a, hid_b)
-        step(2 * tt + 1, masked_b, masked_a, pair_b, pair_a, hid_b, hid_a)
+        step(2 * tt, *even)
+        step(2 * tt + 1, *odd)
         return carry
 
     def finish(slabs):
@@ -373,13 +376,17 @@
         r1[gz, span, :] = s1[gz, span, :]
         return span
 
-    lax.fori_loop(0, 13, two_steps, 0)
+    step(0, *even, "g")
+    step(1, *odd, "gh")
+    lax.fori_loop(1, 13, two_steps, 0)
     span = finish(range(6))
     pl.semaphore_wait(heard.at[2], len(flat_steps))
     for d in far_z:
         peer = along_z(d)
         send(0, s1.at[peer[2], span], r1.at[gz, span], peer)
-    lax.fori_loop(13, CHUNKS // 2 + 1, two_steps, 0)
+    lax.fori_loop(13, CHUNKS // 2, two_steps, 0)
+    step(CHUNKS, *even, "hs")
+    step(CHUNKS + 1, *odd, "s")
     span = finish(range(6, 8))
     for d in far_z:
         peer = along_z(d)

time: 63.4 us -> 62.8 us (level)
    pallas_call x1, Pallas kernels: 61.4 us -> 60.8 us  [whole(): pl.pallas_call(whole_kernel, out_shape=jax.ShapeDtypeStruct((8, 128, CH),...]
where the time goes in v9:
time: 62.8 us; the launch traced here: 62.7 us
  Pallas kernels  60.8 us (97%)
  local copies, waits for them, and re-layouts  1.87 us (3%)
    pallas_call x1, Pallas kernels, whole(): pl.pallas_call(whole_kernel, out_shape=jax.ShapeDtypeStruct((8, 128, CH),...  60.8 us
    unnamed x1, local copies, waits for them, and re-layouts  1.87 us

profile of v9, /device:TPU:1, one launch (start us, length us, event | category | flops | bytes accessed | tf_op | source)
XLA Modules:
  0.0 62.7 jit_solution(2697884437748964929)
XLA Ops:
  0.0 60.8 %whole.1 = f32[8,128,64]{2,1,0:T(8,128)} custom-call(f32[24,128]{1,0:T(8,128)} %bitcast.15, s32[64,16]{1,0:T(8,128)} %bitcast.13, bf16[6,80]{1,0:T(8,128)(2,1)} %kin_hbm.1, bf16[80,80]{1,0:T(8,128)(2,1)} %kmid_hbm.1, bf16[64,80]{1,0:T(8,128)(2,1)} %bitcast.14, bf16[64,64]{1,0:T(8,128)(2,1)} %wskip_hbm.1, s32[8,128,32]{2,1,0:T(8,128)} %bitcast.11, ...), custom_call_target="tpu_custom_call" | custom-call | tf_op jit(solution)/shard_map/whole/pallas_call | solution.py:543
  60.8 1.9 %copy.18 = f32[1,8,16,8,64]{4,3,2,1,0:T(8,128)} copy(f32[1,8,16,8,64]{4,3,2,1,0:T(8,128)} %bitcast.10) | data formatting | bytes 524288

commit v10 on v9

--- a/solution.py
+++ b/solution.py
@@ -249,7 +249,7 @@
         part = buffer.at[pl.ds(0, count)]
         pltpu.make_async_copy(part, part, send_sem.at[n]).wait()
 
-    for step in steps:
+    for step in sorted(steps, key=lambda d: -sum(map(abs, d))):
         block = ((1 - step[0]) * 3 + (1 - step[1])) * 3 + (1 - step[2])
         send(7, pts_ref, around.at[block], beside(step))
     around[13] = pts_ref[...]
@@ -411,7 +411,7 @@
     deep = dot(line, fzh[...]) + dot(line, fzl[...])
     for q in range(NY):
         s2[q] = deep[:, q * 128 : (q + 1) * 128]
-    for d in range(1, NY):
+    for d in (2, 1, 3):
         peer = along_y(d)
         send(1, s2.at[peer[1]], r2.at[gy], peer)
     r2[gy] = s2[gy]

time: 62.8 us -> 62.4 us (level)
  no operation moved by 1% of the time
where the time goes in v10:
time: 62.4 us; the launch traced here: 62.3 us
  Pallas kernels  60.4 us (97%)
  local copies, waits for them, and re-layouts  1.87 us (3%)
    pallas_call x1, Pallas kernels, whole(): pl.pallas_call(whole_kernel, out_shape=jax.ShapeDtypeStruct((8, 128, CH),...  60.4 us
    unnamed x1, local copies, waits for them, and re-layouts  1.87 us

profile of v10, /device:TPU:1, one launch (start us, length us, event | category | flops | bytes accessed | tf_op | source)
XLA Modules:
  0.0 62.3 jit_solution(9666545675621678310)
XLA Ops:
  0.0 60.4 %whole.1 = f32[8,128,64]{2,1,0:T(8,128)} custom-call(f32[24,128]{1,0:T(8,128)} %bitcast.15, s32[64,16]{1,0:T(8,128)} %bitcast.13, bf16[6,80]{1,0:T(8,128)(2,1)} %kin_hbm.1, bf16[80,80]{1,0:T(8,128)(2,1)} %kmid_hbm.1, bf16[64,80]{1,0:T(8,128)(2,1)} %bitcast.14, bf16[64,64]{1,0:T(8,128)(2,1)} %wskip_hbm.1, s32[8,128,32]{2,1,0:T(8,128)} %bitcast.11, ...), custom_call_target="tpu_custom_call" | custom-call | tf_op jit(solution)/shard_map/whole/pallas_call | solution.py:543
  60.4 1.9 %copy.18 = f32[1,8,16,8,64]{4,3,2,1,0:T(8,128)} copy(f32[1,8,16,8,64]{4,3,2,1,0:T(8,128)} %bitcast.10) | data formatting | bytes 524288
